TPU v7x, 256 devices: a whole 4x4x8 slice. The times are simulated.
256 devices in a mesh: ctx: 128 (over z, y_hi, x, core), dp: 2 (over y_lo).
Axes of the slice: x: 4, y: 4 (y_hi: 2, y_lo: 2; y = y_hi * 2 + y_lo), z: 8, core: 2. Of those that a mesh axis runs over, the one named last changes fastest.
Arguments:
- queries: bfloat16 [32768, 1024], P(('dp', 'ctx')), parts along dimension 0, may hold values from -2.5 to 2.5
- keys: bfloat16 [32768, 128], P(('dp', 'ctx')), parts along dimension 0, may hold values from -2.5 to 2.5
- values: bfloat16 [32768, 128], P(('dp', 'ctx')), parts along dimension 0, may hold values from -6 to 6
- grad_out: bfloat16 [32768, 1024], P(('dp', 'ctx')), parts along dimension 0, may hold values from -6 to 6
- pair_order: int32 [256], P('dp'), parts along dimension 0, may hold values from 0 to 127, each once
- doc_lengths: int32 [32], P('dp'), parts along dimension 0, may hold values from 1 to 4096, 16384 in all
Outputs:
- attn_out: bfloat16 [32768, 1024], P(('dp', 'ctx')), parts along dimension 0
- query_grad: bfloat16 [32768, 1024], P(('dp', 'ctx')), parts along dimension 0
- key_grad: bfloat16 [32768, 128], P(('dp', 'ctx')), parts along dimension 0
- value_grad: bfloat16 [32768, 128], P(('dp', 'ctx')), parts along dimension 0
There are 2 independent parts, one for each index of `dp`. A program takes and returns all parts, laid end to end along the dimension named above; each array names one. Nothing has to cross between parts.
Inputs may be any that keep to these rules, and one draw needn't show every extreme that they name: A permutation; the device of index d along ctx holds the sequence blocks pair_order[d] and 255 - pair_order[d], of 64 tokens each, in this order. `doc_lengths`: the documents lie end to end in sequence order; the lengths sum to 16384 and the longest has exactly 4096 tokens.
All inputs are finite; a program needn't handle non-finite values.
Results may differ from a plain program's by a relative error of at most 0.01.
Values may be sent and summed in bfloat16 or wider, within the bound.
No kernel may reach another device: no remote copies, remote signals or barrier semaphores. Data moves between devices by JAX's collectives and lax.ppermute only.
A program may use at most 128 MiB of HBM per device.

v0:
```python
import functools

import jax
import jax.numpy as jnp
from jax import lax
from jax.experimental import pallas as pl
from jax.experimental.pallas import tpu as pltpu
from jax.sharding import Mesh
from jax.sharding import PartitionSpec as P

DIMS = (8, 2, 4, 2)
AXES = ("z", "y", "x", "core")
DP_CTX = ("dp",) + AXES
GROUP = 4
LOG2E = 1.4426950408889634
FAR = 1 << 20


class Sizes:
    def __init__(self, tokens, width, hdim, devices, docs):
        self.half = tokens // 2
        self.tokens = tokens
        self.width = width
        self.hdim = hdim
        self.heads = width // hdim
        self.rows = self.half * self.heads
        self.docs = docs
        self.local = 2 * devices // GROUP
        self.keys = self.local * self.half
        self.queries = 2 * GROUP
        self.per_tile = 4
        self.tile = self.per_tile * self.half
        self.scale = hdim ** (-0.5)
        self.at_key = 0
        self.at_value = self.local
        self.at_block = 2 * self.local
        self.at_ends = 3 * self.local
        self.at_own = self.at_ends + docs
        self.at_low = self.at_own + self.queries
        self.at_high = self.at_low + self.queries


def loaded(sizes, pieces, q_all, g_all, k_all, v_all, sems):
    moves = []
    tokens = sizes.tokens
    for i, piece in enumerate(pieces[:GROUP]):
        at = pl.ds(i * tokens, tokens)
        moves.append((piece.at[pl.ds(0, tokens), :], q_all.at[at, :]))
        moves.append((piece.at[pl.ds(tokens, tokens), :], g_all.at[at, :]))
    for part, whole in ((pieces[GROUP:-2], k_all), (pieces[-2:], v_all)):
        for i, piece in enumerate(part):
            count = piece.shape[0]
            moves.append((piece, whole.at[pl.ds(i * count, count), :]))
    copies = [pltpu.make_async_copy(*move, sems.at[i]) for i, move in enumerate(moves)]
    for copy in copies:
        copy.start()
    return copies


class Block:
    def __init__(self, sizes, table, b, q_all, g_all):
        self.sizes, self.table = sizes, table
        half, hdim = sizes.half, sizes.hdim
        self.own = pl.ds(pl.multiple_of(b * half, half), half)
        self.head = [slice(h * hdim, (h + 1) * hdim) for h in range(sizes.heads)]
        self.q_rows = jnp.concatenate([q_all[self.own, s] for s in self.head], axis=0)
        self.g_rows = jnp.concatenate([g_all[self.own, s] for s in self.head], axis=0)
        self.q_t = self.q_rows.T
        self.g_t = self.g_rows.T
        lane = lax.broadcasted_iota(jnp.int32, (1, sizes.rows), 1)
        self.position = table[sizes.at_own + b] * half + lax.rem(lane, half)
        start = jnp.zeros_like(self.position)
        for d in range(sizes.docs):
            end = table[sizes.at_ends + d]
            start = jnp.where(end <= self.position, jnp.maximum(start, end), start)
        self.start = start
        self.low = table[sizes.at_low + b]
        self.high = table[sizes.at_high + b]
        self.steps = lax.div(self.high - self.low + sizes.per_tile - 1, sizes.per_tile)

    def tile(self, i, k_all, v_all):
        sizes, half = self.sizes, self.sizes.half
        k_at, v_at, keys = [], [], []
        inside = lax.broadcasted_iota(jnp.int32, (half, 1), 0)
        for u in range(sizes.per_tile):
            rank = self.low + i * sizes.per_tile + u
            held = jnp.minimum(rank, self.high - 1)
            k_at.append(pl.ds(pl.multiple_of(self.table[sizes.at_key + held], half), half))
            v_at.append(pl.ds(pl.multiple_of(self.table[sizes.at_value + held], half), half))
            first = jnp.where(rank < self.high, self.table[sizes.at_block + held] * half, FAR)
            keys.append(first + inside)
        key = jnp.concatenate(keys, axis=0)
        k_tile = jnp.concatenate([k_all[p, :] for p in k_at], axis=0)
        v_tile = jnp.concatenate([v_all[p, :] for p in v_at], axis=0)
        s_t = jnp.dot(k_tile, self.q_t, preferred_element_type=jnp.float32)
        allowed = (key >= self.start) & (key <= self.position)
        e_t = jnp.where(allowed, jnp.exp2(s_t * (sizes.scale * LOG2E)), 0.0)
        return k_at, v_at, k_tile, v_tile, e_t

    def put(self, ref, value_t):
        rows = value_t.T.astype(ref.dtype)
        for h, s in enumerate(self.head):
            ref[self.own, s] = rows[h * self.sizes.half : (h + 1) * self.sizes.half, :]


def transposed_product(tile, weights):
    dims = (((0,), (0,)), ((), ()))
    return lax.dot_general(tile, weights, dims, preferred_element_type=jnp.float32)


def forward_kernel(sizes, table, *refs):
    pieces, refs = refs[:-9], refs[-9:]
    out_ref, stats_ref, q_all, g_all, k_all, v_all, out_t, totals, sems = refs
    copies = loaded(sizes, pieces, q_all, g_all, k_all, v_all, sems)
    for copy in copies:
        copy.wait()

    def one_block(b, carry):
        block = Block(sizes, table, b, q_all, g_all)
        out_t[...] = jnp.zeros_like(out_t)
        totals[...] = jnp.zeros_like(totals)

        def step(i, inner):
            _, _, _, v_tile, e_t = block.tile(i, k_all, v_all)
            totals[...] += jnp.sum(e_t.reshape(sizes.tile // 8, 8, sizes.rows), axis=0)
            out_t[...] += transposed_product(v_tile, e_t.astype(jnp.bfloat16))
            return inner

        lax.fori_loop(0, block.steps, step, 0)
        o_t = out_t[...]
        total = jnp.sum(totals[...], axis=0, keepdims=True)
        row_dot = jnp.sum(block.g_t.astype(jnp.float32) * o_t, axis=0, keepdims=True)
        stats_ref[b] = jnp.concatenate([total, row_dot], axis=0)
        block.put(out_ref, o_t)
        return carry

    lax.fori_loop(0, sizes.queries, one_block, 0)


def backward_kernel(sizes, table, *refs):
    pieces, refs = refs[:-14], refs[-14:]
    stats_ref, dq_ref, dk_own, dk_other, dv_own, dv_other = refs[:6]
    q_all, g_all, k_all, v_all, dk_acc, dv_acc, dq_t, sems = refs[6:]
    half = sizes.half
    copies = loaded(sizes, pieces, q_all, g_all, k_all, v_all, sems)

    def clear(i, carry):
        at = pl.ds(pl.multiple_of(i * 256, 256), 256)
        dk_acc[at, :] = jnp.zeros((256, sizes.hdim), jnp.float32)
        dv_acc[at, :] = jnp.zeros((256, sizes.hdim), jnp.float32)
        return carry

    lax.fori_loop(0, sizes.keys // 256, clear, 0)
    for copy in copies:
        copy.wait()

    def one_block(b, carry):
        block = Block(sizes, table, b, q_all, g_all)
        dq_t[...] = jnp.zeros_like(dq_t)
        stats = stats_ref[b]
        inverse = 1.0 / stats[0:1, :]
        row_dot = stats[1:2, :] * inverse

        def step(i, inner):
            k_at, v_at, k_tile, v_tile, e_t = block.tile(i, k_all, v_all)
            dp_t = jnp.dot(v_tile, block.g_t, preferred_element_type=jnp.float32)
            p_t = e_t * inverse
            ds_t = (p_t * (dp_t - row_dot)).astype(jnp.bfloat16)
            p_b = p_t.astype(jnp.bfloat16)
            dq_t[...] += transposed_product(k_tile, ds_t)
            dk = jnp.dot(ds_t, block.q_rows, preferred_element_type=jnp.float32)
            dv = jnp.dot(p_b, block.g_rows, preferred_element_type=jnp.float32)
            for u in range(sizes.per_tile):
                dk_acc[k_at[u], :] += dk[u * half : (u + 1) * half, :]
                dv_acc[v_at[u], :] += dv[u * half : (u + 1) * half, :]
            return inner

        lax.fori_loop(0, block.steps, step, 0)
        block.put(dq_ref, dq_t[...] * sizes.scale)
        return carry

    lax.fori_loop(0, sizes.queries, one_block, 0)

    def finish(i, carry):
        at = pl.ds(pl.multiple_of(i * 256, 256), 256)
        far = pl.ds(pl.multiple_of(sizes.keys // 2 + i * 256, 256), 256)
        dk_own[at, :] = (dk_acc[at, :] * sizes.scale).astype(jnp.bfloat16)
        dk_other[at, :] = (dk_acc[far, :] * sizes.scale).astype(jnp.bfloat16)
        dv_own[at, :] = dv_acc[at, :].astype(jnp.bfloat16)
        dv_other[at, :] = dv_acc[far, :].astype(jnp.bfloat16)
        return carry

    lax.fori_loop(0, sizes.keys // 512, finish, 0)


VMEM_SPEC = pl.BlockSpec(memory_space=pltpu.VMEM)
SMEM_SPEC = pl.BlockSpec(memory_space=pltpu.SMEM)
HBM_SPEC = pl.BlockSpec(memory_space=pltpu.HBM)


def held_arrays(sizes):
    wide = pltpu.VMEM((GROUP * sizes.tokens, sizes.width), jnp.bfloat16)
    narrow = pltpu.VMEM((sizes.keys, sizes.hdim), jnp.bfloat16)
    return [wide, wide, narrow, narrow]


def cost(sizes, products):
    pairs = sizes.keys * sizes.queries * sizes.rows // 4
    return pl.CostEstimate(
        flops=2 * products * sizes.hdim * pairs, bytes_accessed=6 << 20, transcendentals=pairs
    )


def forward(sizes, table, pieces):
    wide = jax.ShapeDtypeStruct((GROUP * sizes.tokens, sizes.width), jnp.bfloat16)
    return pl.pallas_call(
        functools.partial(forward_kernel, sizes),
        out_shape=(wide, jax.ShapeDtypeStruct((sizes.queries, 2, sizes.rows), jnp.float32)),
        in_specs=[SMEM_SPEC] + [HBM_SPEC] * len(pieces),
        out_specs=(VMEM_SPEC, VMEM_SPEC),
        scratch_shapes=held_arrays(sizes)
        + [
            pltpu.VMEM((sizes.hdim, sizes.rows), jnp.float32),
            pltpu.VMEM((8, sizes.rows), jnp.float32),
            pltpu.SemaphoreType.DMA((len(pieces) + GROUP,)),
        ],
        compiler_params=pltpu.CompilerParams(vmem_limit_bytes=24 * 1024 * 1024),
        cost_estimate=cost(sizes, 2),
        name="forward",
    )(table, *pieces)


def backward(sizes, table, pieces, stats):
    wide = jax.ShapeDtypeStruct((GROUP * sizes.tokens, sizes.width), jnp.bfloat16)
    term = jax.ShapeDtypeStruct((sizes.keys // 2, sizes.hdim), jnp.bfloat16)
    return pl.pallas_call(
        functools.partial(backward_kernel, sizes),
        out_shape=(wide, term, term, term, term),
        in_specs=[SMEM_SPEC] + [HBM_SPEC] * len(pieces) + [VMEM_SPEC],
        out_specs=(VMEM_SPEC,) * 5,
        scratch_shapes=held_arrays(sizes)
        + [
            pltpu.VMEM((sizes.keys, sizes.hdim), jnp.float32),
            pltpu.VMEM((sizes.keys, sizes.hdim), jnp.float32),
            pltpu.VMEM((sizes.hdim, sizes.rows), jnp.float32),
            pltpu.SemaphoreType.DMA((len(pieces) + GROUP,)),
        ],
        compiler_params=pltpu.CompilerParams(vmem_limit_bytes=32 * 1024 * 1024),
        cost_estimate=cost(sizes, 6),
        name="backward",
    )(table, *pieces, stats)


def index_table(sizes, pair_order, doc_lengths, z, y, x, core):
    devices = pair_order.shape[0]
    device = jnp.arange(devices, dtype=jnp.int32)
    far_core, far_y = lax.rem(device % 2 + core, 2), lax.rem(device // 8 % 2 + y, 2)
    k_row = (far_core * 16 + far_y * 8 + device // 16) * sizes.tokens
    v_row = (far_core * 16 + device // 16 * 2 + far_y) * sizes.tokens
    mirrored = 2 * devices - 1 - pair_order
    block = jnp.concatenate([pair_order, mirrored])
    k_row = jnp.concatenate([k_row, k_row + sizes.half])
    v_row = jnp.concatenate([v_row, v_row + sizes.half])
    local = device // 2 % 4 == x
    local = jnp.concatenate([local, local])
    rank = jnp.sum((local[None, :] & (block[None, :] < block[:, None])).astype(jnp.int32), axis=1)
    place = jnp.arange(sizes.local, dtype=jnp.int32)
    chosen = local[None, :] & (rank[None, :] == place[:, None])
    k_at = jnp.sum(jnp.where(chosen, k_row[None, :], 0), axis=1)
    v_at = jnp.sum(jnp.where(chosen, v_row[None, :], 0), axis=1)
    held = jnp.sum(jnp.where(chosen, block[None, :], 0), axis=1)
    docs = jnp.arange(sizes.docs, dtype=jnp.int32)
    ends = jnp.sum(jnp.where(docs[None, :] <= docs[:, None], doc_lengths[None, :], 0), axis=1)
    query = jnp.arange(sizes.queries, dtype=jnp.int32)
    owner = z * 16 + y * 8 + lax.rem(x + query // 2, 4) * 2 + core
    own = jnp.sum(jnp.where(owner[:, None] == device[None, :], pair_order[None, :], 0), axis=1)
    own = jnp.where(query % 2 == 0, own, 2 * devices - 1 - own)
    first = own * sizes.half
    start = jnp.max(jnp.where(ends[None, :] <= first[:, None], ends[None, :], 0), axis=1)
    low = jnp.sum((held[None, :] < (start // sizes.half)[:, None]).astype(jnp.int32), axis=1)
    high = jnp.sum((held[None, :] <= own[:, None]).astype(jnp.int32), axis=1)
    return jnp.concatenate([k_at, v_at, held, ends, own, low, high]).astype(jnp.int32)


def from_x(a, step):
    return lax.ppermute(a, "x", [((i + step) % 4, i) for i in range(4)])


def swap(a, axis):
    return lax.ppermute(a, axis, [(0, 1), (1, 0)])


def added(*terms):
    return sum(t.astype(jnp.float32) for t in terms).astype(jnp.bfloat16)


def over_z(a):
    return lax.all_to_all(a, "z", 0, 0, tiled=True)


def gathered_x(queries, grad_out):
    both = jnp.concatenate([queries, grad_out], axis=0)
    pieces = [both]
    for step in (1, 2, 3):
        pieces.append(from_x(both, step))
    return pieces


def gathered_keys(keys, values):
    values = jnp.concatenate([values, swap(values, "y")], axis=0)
    k_near = over_z(jnp.tile(keys, (8, 1)))
    v = over_z(jnp.tile(values, (8, 1)))
    k_far = swap(k_near, "y")
    return [k_near, k_far, swap(k_near, "core"), swap(k_far, "core"), v, swap(v, "core")]


def scattered_keys(own, other, tokens):
    n = 8 * tokens
    other = swap(other, "core")
    far = swap(added(own[n:], other[n:]), "y")
    column = over_z(added(own[:n], other[:n], far))
    column = column.reshape(8, tokens, -1).astype(jnp.float32)
    return jnp.sum(column, axis=0).astype(jnp.bfloat16)


def scattered_values(own, other, tokens):
    other = swap(other, "core")
    column = over_z(added(own, other))
    column = column.reshape(8, 2 * tokens, -1).astype(jnp.float32)
    column = jnp.sum(column, axis=0)
    far = swap(column[tokens:].astype(jnp.bfloat16), "y")
    return added(column[:tokens], far)


def summed_x(parts, tokens):
    part = [parts[i * tokens : (i + 1) * tokens] for i in range(GROUP)]
    received = [part[0]]
    for step in (1, 2, 3):
        received.append(from_x(part[(4 - step) % 4], step))
    return received


def shared_stats(stats):
    total = stats
    for step in (1, 2, 3):
        arrived = from_x(stats, step)
        total = total + jnp.roll(arrived, 2 * step, axis=0)
    return total


def grads_of(queries, keys, values, grad_out, pair_order, doc_lengths):
    tokens, hdim = keys.shape
    width = queries.shape[1]
    sizes = Sizes(tokens, width, hdim, pair_order.shape[0], doc_lengths.shape[0])
    spot = [lax.axis_index(a) for a in AXES]
    table = index_table(sizes, pair_order, doc_lengths, *spot)
    pieces = gathered_x(queries, grad_out) + gathered_keys(keys, values)
    out_parts, stats = forward(sizes, table, pieces)
    stats = shared_stats(stats)
    out_parts = summed_x(out_parts, tokens)
    dq_parts, *terms = backward(sizes, table, pieces, stats)
    total = stats[:2, 0, :].reshape(2, sizes.heads, sizes.half)
    total = jnp.swapaxes(total, 1, 2).reshape(tokens, sizes.heads, 1)
    out = sum(p.astype(jnp.float32) for p in out_parts).reshape(tokens, sizes.heads, hdim)
    out = (out / total).astype(jnp.bfloat16).reshape(tokens, width)
    query_grad = added(*summed_x(dq_parts, tokens))
    key_grad = scattered_keys(*terms[:2], tokens)
    value_grad = scattered_values(*terms[2:], tokens)
    return out, query_grad, key_grad, value_grad


def solution(mesh):
    torus = Mesh(mesh.devices.reshape(*DIMS, mesh.shape["dp"]), AXES + ("dp",))
    rows = P(DP_CTX, None)
    return jax.shard_map(
        grads_of,
        mesh=torus,
        in_specs=(rows, rows, rows, rows, P("dp"), P("dp")),
        out_specs=(rows, rows, rows, rows),
        check_vma=False,
    )
```

profile of v0, /device:TPU:16, one launch (start us, length us, event | category | flops | bytes accessed | tf_op | source)
XLA Modules:
  0.0 143.5 jit_solution(12885699088526853553)
XLA Ops:
  0.6 1.0 constant_dynamic-update-slice_fusion.1
  1.7 2.8 %collective-permute-start = (bf16[256,1024]{1,0:T(8,128)(2,1)S(1)}, bf16[256,1024]{1,0:T(8,128)(2,1)S(1)}, u32[]{:S(2)}, u32[]{:S(2)}) collective-permute-start(bf16[256,1024]{1,0:T(8,128)(2,1)S(1)} %constant_dynamic-update-slice_fusion.refs_0_), channel_id=1, source_target_pairs={{4,0},{8,4},{12,8},{0,12},{5,1},{9,5},{13,9},{1,13},{6,2},{10,6},{... | collective-permute-start | bytes 1572872 | tf_op jit(solution)/shard_map/ppermute | solution.py:286
  7.0 8.6 %all-to-all-start = ((bf16[8,128,128]{2,1,0:T(8,128)(2,1)}), bf16[8,128,128]{2,1,0:T(8,128)(2,1)S(1)}, u32[]{:S(2)}, u32[]{:S(2)}) async-start(bf16[8,128,128]{2,1,0:T(8,128)(2,1)} %tile.4), calls=%async_computation | async-start | bytes 524288 | tf_op jit(solution)/shard_map/all_to_all | solution.py:298
  16.1 5.0 %collective-permute-done.6 = bf16[128,128]{1,0:T(8,128)(2,1)S(1)} collective-permute-done((bf16[128,128]{1,0:T(8,128)(2,1)S(1)}, bf16[128,128]{1,0:T(8,128)(2,1)S(1)}, u32[]{:S(2)}, u32[]{:S(2)}) %collective-permute-start.6) | collective-permute-done | bytes 32800 | tf_op jit(solution)/shard_map/ppermute | solution.py:290
  21.1 5.5 %all-to-all-done = bf16[8,128,128]{2,1,0:T(8,128)(2,1)S(1)} async-done(((bf16[8,128,128]{2,1,0:T(8,128)(2,1)}), bf16[8,128,128]{2,1,0:T(8,128)(2,1)S(1)}, u32[]{:S(2)}, u32[]{:S(2)}) %all-to-all-start) | async-done | bytes 262176 | tf_op jit(solution)/shard_map/all_to_all | solution.py:298
  27.5 3.5 %all-to-all-start.1 = ((bf16[8,256,128]{2,1,0:T(8,128)(2,1)}), bf16[8,256,128]{2,1,0:T(8,128)(2,1)S(1)}, u32[]{:S(2)}, u32[]{:S(2)}) async-start(bf16[8,256,128]{2,1,0:T(8,128)(2,1)} %tile.5), calls=%async_computation.1 | async-start | bytes 1048576 | tf_op jit(solution)/shard_map/all_to_all | solution.py:298
  32.8 13.4 %all-to-all-done.1 = bf16[8,256,128]{2,1,0:T(8,128)(2,1)S(1)} async-done(((bf16[8,256,128]{2,1,0:T(8,128)(2,1)}), bf16[8,256,128]{2,1,0:T(8,128)(2,1)S(1)}, u32[]{:S(2)}, u32[]{:S(2)}) %all-to-all-start.1) | async-done | bytes 524320 | tf_op jit(solution)/shard_map/all_to_all | solution.py:298
  49.8 1.0 copy-done.7
  50.8 1.0 copy-done.10
  51.9 8.7 %forward.1 = (bf16[512,1024]{1,0:T(8,128)(2,1)S(1)}, f32[8,2,512]{2,1,0:T(2,128)S(1)}) custom-call(s32[232]{0:T(256)S(1)} %concatenate.37.table, bf16[256,1024]{1,0:T(8,128)(2,1)S(1)} %constant_dynamic-update-slice_fusion.refs_0_, bf16[256,1024]{1,0:T(8,128)(2,1)S(1)} %collective-permute-done.refs_1_, bf16[256,1024]{1,0:T(8,128)(2,1)S(1)} %collective-permute-done.1.refs_2_, ...), custom_call_target="tpu_custom_call" | custom-call | flops 2147483648 | bytes 6291456 | tf_op jit(solution)/shard_map/forward/pallas_call | solution.py:216
  60.6 2.4 %collective-permute-start.11 = (f32[8,2,512]{2,1,0:T(2,128)S(1)}, f32[8,2,512]{2,1,0:T(2,128)S(1)}, u32[]{:S(2)}, u32[]{:S(2)}) collective-permute-start(f32[8,2,512]{2,1,0:T(2,128)S(1)} %get-tuple-element.12), channel_id=1, source_target_pairs={{4,0},{8,4},{12,8},{0,12},{5,1},{9,5},{13,9},{1,13},{6,2},{10,6},{... | collective-permute-start | bytes 98312 | tf_op jit(solution)/shard_map/ppermute | solution.py:286
  63.9 2.0 %collective-permute-start.12 = (f32[8,2,512]{2,1,0:T(2,128)S(1)}, f32[8,2,512]{2,1,0:T(2,128)S(1)}, u32[]{:S(2)}, u32[]{:S(2)}) collective-permute-start(f32[8,2,512]{2,1,0:T(2,128)S(1)} %get-tuple-element.12), channel_id=1, source_target_pairs={{8,0},{12,4},{0,8},{4,12},{9,1},{13,5},{1,9},{5,13},{10,2},{14,6},... | collective-permute-start | bytes 98312 | tf_op jit(solution)/shard_map/ppermute | solution.py:286
  66.5 1.8 %collective-permute-done.13 = f32[8,2,512]{2,1,0:T(2,128)S(1)} collective-permute-done((f32[8,2,512]{2,1,0:T(2,128)S(1)}, f32[8,2,512]{2,1,0:T(2,128)S(1)}, u32[]{:S(2)}, u32[]{:S(2)}) %collective-permute-start.13) | collective-permute-done | bytes 32800 | tf_op jit(solution)/shard_map/ppermute | solution.py:286
  70.1 1.0 copy-done.1
  71.2 1.0 copy-done.3
  72.2 1.0 copy-done.5
  73.3 1.0 copy-done.11
  74.3 11.6 %backward.1 = (bf16[512,1024]{1,0:T(8,128)(2,1)S(1)}, bf16[2048,128]{1,0:T(8,128)(2,1)S(1)}, bf16[2048,128]{1,0:T(8,128)(2,1)}, bf16[2048,128]{1,0:T(8,128)(2,1)S(1)}, bf16[2048,128]{1,0:T(8,128)(2,1)S(1)}) custom-call(s32[232]{0:T(256)S(1)} %concatenate.37.table, bf16[256,1024]{1,0:T(8,128)(2,1)S(1)} %copy-done.1, bf16[256,1024]{1,0:T(8,128)(2,1)S(1)} %copy-done.3, ...), custom_call_target="tpu_custom_call" | custom-call | flops 6442450944 | bytes 6291456 | tf_op jit(solution)/shard_map/backward/pallas_call | solution.py:236
  86.7 1.4 %collective-permute-done.19 = bf16[2048,128]{1,0:T(8,128)(2,1)S(1)} collective-permute-done((bf16[2048,128]{1,0:T(8,128)(2,1)S(1)}, bf16[2048,128]{1,0:T(8,128)(2,1)S(1)}, u32[]{:S(2)}, u32[]{:S(2)}) %collective-permute-start.19) | collective-permute-done | bytes 524320 | tf_op jit(solution)/shard_map/ppermute | solution.py:290
  88.2 0.9 add_convert_fusion
  89.1 13.1 %all-to-all-start.3 = ((bf16[8,256,128]{2,1,0:T(8,128)(2,1)}), bf16[8,256,128]{2,1,0:T(8,128)(2,1)S(1)}, u32[]{:S(2)}, u32[]{:S(2)}) async-start(bf16[8,256,128]{2,1,0:T(8,128)(2,1)} %bitcast.5), calls=%async_computation.3 | async-start | bytes 1048576 | tf_op jit(solution)/shard_map/all_to_all | solution.py:298
  103.1 4.3 %collective-permute-start.9 = (bf16[128,1024]{1,0:T(8,128)(2,1)}, bf16[128,1024]{1,0:T(8,128)(2,1)}, u32[]{:S(2)}, u32[]{:S(2)}) collective-permute-start(bf16[128,1024]{1,0:T(8,128)(2,1)} %get-tuple-element.34), channel_id=1, source_target_pairs={{8,0},{12,4},{0,8},{4,12},{9,1},{13,5},{1,9},{5,13},{10,2},{14,6},... | collective-permute-start | bytes 786440 | tf_op jit(solution)/shard_map/ppermute | solution.py:286
  107.4 1.7 %add_convert_fusion.2 = bf16[1024,128]{1,0:T(8,128)(2,1)} fusion(bf16[2048,128]{1,0:T(8,128)(2,1)} %collective-permute-done.17, bf16[2048,128]{1,0:T(8,128)(2,1)S(1)} %get-tuple-element.14), kind=kLoop, calls=%fused_computation.5 | loop fusion | flops 524288 | bytes 786432 | tf_op jit(solution)/shard_map/convert_element_type | solution.py:294
  110.3 2.1 %collective-permute-start.16 = (bf16[128,1024]{1,0:T(8,128)(2,1)}, bf16[128,1024]{1,0:T(8,128)(2,1)}, u32[]{:S(2)}, u32[]{:S(2)}) collective-permute-start(bf16[128,1024]{1,0:T(8,128)(2,1)} %get-tuple-element.30), channel_id=1, source_target_pairs={{12,0},{0,4},{4,8},{8,12},{13,1},{1,5},{5,9},{9,13},{14,2},{2,6},{... | collective-permute-start | bytes 786440 | tf_op jit(solution)/shard_map/ppermute | solution.py:286
  112.4 6.1 %collective-permute-done.18 = bf16[1024,128]{1,0:T(8,128)(2,1)} collective-permute-done((bf16[1024,128]{1,0:T(8,128)(2,1)}, bf16[1024,128]{1,0:T(8,128)(2,1)}, u32[]{:S(2)}, u32[]{:S(2)}) %collective-permute-start.18) | collective-permute-done | bytes 262176 | tf_op jit(solution)/shard_map/ppermute | solution.py:290
  118.5 1.5 %collective-permute-start.15 = (bf16[128,1024]{1,0:T(8,128)(2,1)}, bf16[128,1024]{1,0:T(8,128)(2,1)}, u32[]{:S(2)}, u32[]{:S(2)}) collective-permute-start(bf16[128,1024]{1,0:T(8,128)(2,1)} %get-tuple-element.31), channel_id=1, source_target_pairs={{8,0},{12,4},{0,8},{4,12},{9,1},{13,5},{1,9},{5,13},{10,2},{14,6},... | collective-permute-start | bytes 786440 | tf_op jit(solution)/shard_map/ppermute | solution.py:286
  120.0 1.9 %add_convert_fusion.1 = bf16[1024,128]{1,0:T(8,128)(2,1)} fusion(bf16[1024,128]{1,0:T(8,128)(2,1)} %collective-permute-done.18, bf16[2048,128]{1,0:T(8,128)(2,1)} %collective-permute-done.17, bf16[2048,128]{1,0:T(8,128)(2,1)S(1)} %get-tuple-element.14), kind=kLoop, calls=%fused_computation.4 | loop fusion | flops 786432 | bytes 1048576 | tf_op jit(solution)/shard_map/convert_element_type | solution.py:294
  121.9 2.9 %collective-permute-start.14 = (bf16[128,1024]{1,0:T(8,128)(2,1)}, bf16[128,1024]{1,0:T(8,128)(2,1)S(1)}, u32[]{:S(2)}, u32[]{:S(2)}) collective-permute-start(bf16[128,1024]{1,0:T(8,128)(2,1)} %get-tuple-element.29), channel_id=1, source_target_pairs={{4,0},{8,4},{12,8},{0,12},{5,1},{9,5},{13,9},{1,13},{6,2},{10,6},{... | collective-permute-start | bytes 786440 | tf_op jit(solution)/shard_map/ppermute | solution.py:286
  124.8 6.9 %all-to-all-start.2 = ((bf16[8,128,128]{2,1,0:T(8,128)(2,1)}), bf16[8,128,128]{2,1,0:T(8,128)(2,1)S(1)}, u32[]{:S(2)}, u32[]{:S(2)}) async-start(bf16[8,128,128]{2,1,0:T(8,128)(2,1)} %bitcast.4), calls=%async_computation.2 | async-start | bytes 524288 | tf_op jit(solution)/shard_map/all_to_all | solution.py:298
  131.9 2.0 %fusion = bf16[128,1024]{1,0:T(8,128)(2,1)} fusion(f32[16,8,8,128]{3,2,1,0:T(8,128)S(1)} %bitcast.20, bf16[128,1024]{1,0:T(8,128)(2,1)S(1)} %collective-permute-done.10, bf16[128,1024]{1,0:T(8,128)(2,1)} %collective-permute-done.9, bf16[128,1024]{1,0:T(8,128)(2,1)} %collective-permute-done.8, bf16[512,1024]{1,0:T(8,128)(2,1)S(1)} %get-tuple-element.11), kind=kLoop, calls=%fused_computation.3 | loop fusion | flops 1179648 | bytes 1835008 | tf_op jit(solution)/shard_map/convert_element_type | solution.py:365
  134.4 1.9 %add_convert_fusion.3 = bf16[128,1024]{1,0:T(8,128)(2,1)} fusion(bf16[128,1024]{1,0:T(8,128)(2,1)} %collective-permute-done.16, bf16[128,1024]{1,0:T(8,128)(2,1)} %collective-permute-done.15, bf16[128,1024]{1,0:T(8,128)(2,1)S(1)} %collective-permute-done.14, bf16[512,1024]{1,0:T(8,128)(2,1)S(1)} %get-tuple-element.13), kind=kLoop, calls=%fused_computation.6 | loop fusion | flops 1048576 | bytes 1310720 | tf_op jit(solution)/shard_map/convert_element_type | solution.py:294
  136.3 5.9 %all-to-all-done.2 = bf16[8,128,128]{2,1,0:T(8,128)(2,1)S(1)} async-done(((bf16[8,128,128]{2,1,0:T(8,128)(2,1)}), bf16[8,128,128]{2,1,0:T(8,128)(2,1)S(1)}, u32[]{:S(2)}, u32[]{:S(2)}) %all-to-all-start.2) | async-done | bytes 262176 | tf_op jit(solution)/shard_map/all_to_all | solution.py:298
  (105 shorter events, 17.2 us)
Async XLA Ops:
  1.7 4.6 %copy-start.15 = (bf16[128,128]{1,0:T(8,128)(2,1)S(1)}, bf16[128,128]{1,0:T(8,128)(2,1)}, u32[]{:S(2)}) copy-start(bf16[128,128]{1,0:T(8,128)(2,1)} %param.7) | copy-start | bytes 98308
  1.7 47.3 %copy-start = (bf16[256,1024]{1,0:T(8,128)(2,1)}, bf16[256,1024]{1,0:T(8,128)(2,1)S(1)}, u32[]{:S(2)}) copy-start(bf16[256,1024]{1,0:T(8,128)(2,1)S(1)} %constant_dynamic-update-slice_fusion.refs_0_) | copy-start | bytes 1572868
  1.7 44.5 %collective-permute-start = (bf16[256,1024]{1,0:T(8,128)(2,1)S(1)}, bf16[256,1024]{1,0:T(8,128)(2,1)S(1)}, u32[]{:S(2)}, u32[]{:S(2)}) collective-permute-start(bf16[256,1024]{1,0:T(8,128)(2,1)S(1)} %constant_dynamic-update-slice_fusion.refs_0_), channel_id=1, source_target_pairs={{4,0},{8,4},{12,8},{0,12},{5,1},{9,5},{13,9},{1,13},{6,2},{10,6},{... | collective-permute-start | bytes 1572872 | tf_op jit(solution)/shard_map/ppermute | solution.py:286
  4.5 42.8 %collective-permute-start.1 = (bf16[256,1024]{1,0:T(8,128)(2,1)S(1)}, bf16[256,1024]{1,0:T(8,128)(2,1)S(1)}, u32[]{:S(2)}, u32[]{:S(2)}) collective-permute-start(bf16[256,1024]{1,0:T(8,128)(2,1)S(1)} %constant_dynamic-update-slice_fusion.refs_0_), channel_id=1, source_target_pairs={{8,0},{12,4},{0,8},{4,12},{9,1},{13,5},{1,9},{5,13},{10,2},{14,6},... | collective-permute-start | bytes 1572872 | tf_op jit(solution)/shard_map/ppermute | solution.py:286
  5.3 42.0 %collective-permute-start.2 = (bf16[256,1024]{1,0:T(8,128)(2,1)S(1)}, bf16[256,1024]{1,0:T(8,128)(2,1)S(1)}, u32[]{:S(2)}, u32[]{:S(2)}) collective-permute-start(bf16[256,1024]{1,0:T(8,128)(2,1)S(1)} %constant_dynamic-update-slice_fusion.refs_0_), channel_id=1, source_target_pairs={{12,0},{0,4},{4,8},{8,12},{13,1},{1,5},{5,9},{9,13},{14,2},{2,6},{... | collective-permute-start | bytes 1572872 | tf_op jit(solution)/shard_map/ppermute | solution.py:286
  7.0 8.6 %copy-start.16 = (bf16[128,128]{1,0:T(8,128)(2,1)S(1)}, bf16[128,128]{1,0:T(8,128)(2,1)}, u32[]{:S(2)}) copy-start(bf16[128,128]{1,0:T(8,128)(2,1)} %param.8) | copy-start | bytes 98308
  7.0 9.0 %copy-start.17 = (s32[128]{0:T(128)S(1)}, s32[128]{0:T(128)}, u32[]{:S(2)}) copy-start(s32[128]{0:T(128)} %param.10) | copy-start | bytes 1540
  7.0 19.6 %all-to-all-start = ((bf16[8,128,128]{2,1,0:T(8,128)(2,1)}), bf16[8,128,128]{2,1,0:T(8,128)(2,1)S(1)}, u32[]{:S(2)}, u32[]{:S(2)}) async-start(bf16[8,128,128]{2,1,0:T(8,128)(2,1)} %tile.4), calls=%async_computation | async-start | bytes 524288 | tf_op jit(solution)/shard_map/all_to_all | solution.py:298
  15.6 5.5 %collective-permute-start.6 = (bf16[128,128]{1,0:T(8,128)(2,1)S(1)}, bf16[128,128]{1,0:T(8,128)(2,1)S(1)}, u32[]{:S(2)}, u32[]{:S(2)}) collective-permute-start(bf16[128,128]{1,0:T(8,128)(2,1)S(1)} %copy-done.16), channel_id=1, source_target_pairs={{0,16},{16,0},{1,17},{17,1},{2,18},{18,2},{3,19},{19,3},{4,20},{20... | collective-permute-start | bytes 98312 | tf_op jit(solution)/shard_map/ppermute | solution.py:290
  27.5 18.7 %all-to-all-start.1 = ((bf16[8,256,128]{2,1,0:T(8,128)(2,1)}), bf16[8,256,128]{2,1,0:T(8,128)(2,1)S(1)}, u32[]{:S(2)}, u32[]{:S(2)}) async-start(bf16[8,256,128]{2,1,0:T(8,128)(2,1)} %tile.5), calls=%async_computation.1 | async-start | bytes 1048576 | tf_op jit(solution)/shard_map/all_to_all | solution.py:298
  32.3 14.5 %collective-permute-start.3 = (bf16[1024,128]{1,0:T(8,128)(2,1)S(1)}, bf16[1024,128]{1,0:T(8,128)(2,1)}, u32[]{:S(2)}, u32[]{:S(2)}) collective-permute-start(bf16[1024,128]{1,0:T(8,128)(2,1)S(1)} %bitcast.16), channel_id=1, source_target_pairs={{0,16},{16,0},{1,17},{17,1},{2,18},{18,2},{3,19},{19,3},{4,20},{20... | collective-permute-start | bytes 786440 | tf_op jit(solution)/shard_map/ppermute | solution.py:290
  46.2 2.8 %collective-permute-start.7 = (bf16[2048,128]{1,0:T(8,128)(2,1)S(1)}, bf16[2048,128]{1,0:T(8,128)(2,1)S(1)}, u32[]{:S(2)}, u32[]{:S(2)}) collective-permute-start(bf16[2048,128]{1,0:T(8,128)(2,1)S(1)} %bitcast.13), channel_id=1, source_target_pairs={{0,2},{2,0},{1,3},{3,1},{4,6},{6,4},{5,7},{7,5},{8,10},{10,8},{9,1... | collective-permute-start | bytes 1572872 | tf_op jit(solution)/shard_map/ppermute | solution.py:290
  46.2 14.4 %copy-start.2 = (bf16[256,1024]{1,0:T(8,128)(2,1)}, bf16[256,1024]{1,0:T(8,128)(2,1)S(1)}, u32[]{:S(2)}) copy-start(bf16[256,1024]{1,0:T(8,128)(2,1)S(1)} %collective-permute-done.refs_1_) | copy-start | bytes 1572868
  46.2 2.4 %collective-permute-start.4 = (bf16[1024,128]{1,0:T(8,128)(2,1)S(1)}, bf16[1024,128]{1,0:T(8,128)(2,1)}, u32[]{:S(2)}, u32[]{:S(2)}) collective-permute-start(bf16[1024,128]{1,0:T(8,128)(2,1)S(1)} %bitcast.17), channel_id=1, source_target_pairs={{0,2},{2,0},{1,3},{3,1},{4,6},{6,4},{5,7},{7,5},{8,10},{10,8},{9,1... | collective-permute-start | bytes 786440 | tf_op jit(solution)/shard_map/ppermute | solution.py:290
  46.8 2.2 %collective-permute-start.5 = (bf16[1024,128]{1,0:T(8,128)(2,1)}, bf16[1024,128]{1,0:T(8,128)(2,1)}, u32[]{:S(2)}, u32[]{:S(2)}) collective-permute-start(bf16[1024,128]{1,0:T(8,128)(2,1)} %collective-permute-done.3.refs_5_), channel_id=1, source_target_pairs={{0,2},{2,0},{1,3},{3,1},{4,6},{6,4},{5,7},{7,5},{8,10},{10,8},{9,1... | collective-permute-start | bytes 786440 | tf_op jit(solution)/shard_map/ppermute | solution.py:290
  47.4 13.2 %copy-start.4 = (bf16[256,1024]{1,0:T(8,128)(2,1)}, bf16[256,1024]{1,0:T(8,128)(2,1)S(1)}, u32[]{:S(2)}) copy-start(bf16[256,1024]{1,0:T(8,128)(2,1)S(1)} %collective-permute-done.1.refs_2_) | copy-start | bytes 1572868
  51.9 18.3 %copy-start.8 = (bf16[256,1024]{1,0:T(8,128)(2,1)S(1)}, bf16[256,1024]{1,0:T(8,128)(2,1)}, u32[]{:S(2)}) copy-start(bf16[256,1024]{1,0:T(8,128)(2,1)} %copy-done.6) | copy-start | bytes 1572868
  60.6 5.3 %collective-permute-start.11 = (f32[8,2,512]{2,1,0:T(2,128)S(1)}, f32[8,2,512]{2,1,0:T(2,128)S(1)}, u32[]{:S(2)}, u32[]{:S(2)}) collective-permute-start(f32[8,2,512]{2,1,0:T(2,128)S(1)} %get-tuple-element.12), channel_id=1, source_target_pairs={{4,0},{8,4},{12,8},{0,12},{5,1},{9,5},{13,9},{1,13},{6,2},{10,6},{... | collective-permute-start | bytes 98312 | tf_op jit(solution)/shard_map/ppermute | solution.py:286
  63.0 5.3 %collective-permute-start.13 = (f32[8,2,512]{2,1,0:T(2,128)S(1)}, f32[8,2,512]{2,1,0:T(2,128)S(1)}, u32[]{:S(2)}, u32[]{:S(2)}) collective-permute-start(f32[8,2,512]{2,1,0:T(2,128)S(1)} %get-tuple-element.12), channel_id=1, source_target_pairs={{12,0},{0,4},{4,8},{8,12},{13,1},{1,5},{5,9},{9,13},{14,2},{2,6},{... | collective-permute-start | bytes 98312 | tf_op jit(solution)/shard_map/ppermute | solution.py:286
  63.9 5.4 %collective-permute-start.12 = (f32[8,2,512]{2,1,0:T(2,128)S(1)}, f32[8,2,512]{2,1,0:T(2,128)S(1)}, u32[]{:S(2)}, u32[]{:S(2)}) collective-permute-start(f32[8,2,512]{2,1,0:T(2,128)S(1)} %get-tuple-element.12), channel_id=1, source_target_pairs={{8,0},{12,4},{0,8},{4,12},{9,1},{13,5},{1,9},{5,13},{10,2},{14,6},... | collective-permute-start | bytes 98312 | tf_op jit(solution)/shard_map/ppermute | solution.py:286
  85.9 2.3 %collective-permute-start.19 = (bf16[2048,128]{1,0:T(8,128)(2,1)S(1)}, bf16[2048,128]{1,0:T(8,128)(2,1)S(1)}, u32[]{:S(2)}, u32[]{:S(2)}) collective-permute-start(bf16[2048,128]{1,0:T(8,128)(2,1)S(1)} %get-tuple-element.17), channel_id=1, source_target_pairs={{0,2},{2,0},{1,3},{3,1},{4,6},{6,4},{5,7},{7,5},{8,10},{10,8},{9,1... | collective-permute-start | bytes 1572872 | tf_op jit(solution)/shard_map/ppermute | solution.py:290
  86.6 20.8 %collective-permute-start.17 = (bf16[2048,128]{1,0:T(8,128)(2,1)}, bf16[2048,128]{1,0:T(8,128)(2,1)}, u32[]{:S(2)}, u32[]{:S(2)}) collective-permute-start(bf16[2048,128]{1,0:T(8,128)(2,1)} %get-tuple-element.15), channel_id=1, source_target_pairs={{0,2},{2,0},{1,3},{3,1},{4,6},{6,4},{5,7},{7,5},{8,10},{10,8},{9,1... | collective-permute-start | bytes 1572872 | tf_op jit(solution)/shard_map/ppermute | solution.py:290
  89.1 35.7 %all-to-all-start.3 = ((bf16[8,256,128]{2,1,0:T(8,128)(2,1)}), bf16[8,256,128]{2,1,0:T(8,128)(2,1)S(1)}, u32[]{:S(2)}, u32[]{:S(2)}) async-start(bf16[8,256,128]{2,1,0:T(8,128)(2,1)} %bitcast.5), calls=%async_computation.3 | async-start | bytes 1048576 | tf_op jit(solution)/shard_map/all_to_all | solution.py:298
  103.1 18.8 %collective-permute-start.10 = (bf16[128,1024]{1,0:T(8,128)(2,1)}, bf16[128,1024]{1,0:T(8,128)(2,1)S(1)}, u32[]{:S(2)}, u32[]{:S(2)}) collective-permute-start(bf16[128,1024]{1,0:T(8,128)(2,1)} %get-tuple-element.33), channel_id=1, source_target_pairs={{12,0},{0,4},{4,8},{8,12},{13,1},{1,5},{5,9},{9,13},{14,2},{2,6},{... | collective-permute-start | bytes 786440 | tf_op jit(solution)/shard_map/ppermute | solution.py:286
  103.1 28.6 %collective-permute-start.9 = (bf16[128,1024]{1,0:T(8,128)(2,1)}, bf16[128,1024]{1,0:T(8,128)(2,1)}, u32[]{:S(2)}, u32[]{:S(2)}) collective-permute-start(bf16[128,1024]{1,0:T(8,128)(2,1)} %get-tuple-element.34), channel_id=1, source_target_pairs={{8,0},{12,4},{0,8},{4,12},{9,1},{13,5},{1,9},{5,13},{10,2},{14,6},... | collective-permute-start | bytes 786440 | tf_op jit(solution)/shard_map/ppermute | solution.py:286
  107.4 24.3 %collective-permute-start.8 = (bf16[128,1024]{1,0:T(8,128)(2,1)}, bf16[128,1024]{1,0:T(8,128)(2,1)}, u32[]{:S(2)}, u32[]{:S(2)}) collective-permute-start(bf16[128,1024]{1,0:T(8,128)(2,1)} %get-tuple-element.32), channel_id=1, source_target_pairs={{4,0},{8,4},{12,8},{0,12},{5,1},{9,5},{13,9},{1,13},{6,2},{10,6},{... | collective-permute-start | bytes 786440 | tf_op jit(solution)/shard_map/ppermute | solution.py:286
  109.2 9.3 %collective-permute-start.18 = (bf16[1024,128]{1,0:T(8,128)(2,1)}, bf16[1024,128]{1,0:T(8,128)(2,1)}, u32[]{:S(2)}, u32[]{:S(2)}) collective-permute-start(bf16[1024,128]{1,0:T(8,128)(2,1)} %add_convert_fusion.2), channel_id=1, source_target_pairs={{0,16},{16,0},{1,17},{17,1},{2,18},{18,2},{3,19},{19,3},{4,20},{20... | collective-permute-start | bytes 786440 | tf_op jit(solution)/shard_map/ppermute | solution.py:290
  110.3 24.1 %collective-permute-start.16 = (bf16[128,1024]{1,0:T(8,128)(2,1)}, bf16[128,1024]{1,0:T(8,128)(2,1)}, u32[]{:S(2)}, u32[]{:S(2)}) collective-permute-start(bf16[128,1024]{1,0:T(8,128)(2,1)} %get-tuple-element.30), channel_id=1, source_target_pairs={{12,0},{0,4},{4,8},{8,12},{13,1},{1,5},{5,9},{9,13},{14,2},{2,6},{... | collective-permute-start | bytes 786440 | tf_op jit(solution)/shard_map/ppermute | solution.py:286
  118.5 15.9 %collective-permute-start.15 = (bf16[128,1024]{1,0:T(8,128)(2,1)}, bf16[128,1024]{1,0:T(8,128)(2,1)}, u32[]{:S(2)}, u32[]{:S(2)}) collective-permute-start(bf16[128,1024]{1,0:T(8,128)(2,1)} %get-tuple-element.31), channel_id=1, source_target_pairs={{8,0},{12,4},{0,8},{4,12},{9,1},{13,5},{1,9},{5,13},{10,2},{14,6},... | collective-permute-start | bytes 786440 | tf_op jit(solution)/shard_map/ppermute | solution.py:286
  121.9 12.5 %collective-permute-start.14 = (bf16[128,1024]{1,0:T(8,128)(2,1)}, bf16[128,1024]{1,0:T(8,128)(2,1)S(1)}, u32[]{:S(2)}, u32[]{:S(2)}) collective-permute-start(bf16[128,1024]{1,0:T(8,128)(2,1)} %get-tuple-element.29), channel_id=1, source_target_pairs={{4,0},{8,4},{12,8},{0,12},{5,1},{9,5},{13,9},{1,13},{6,2},{10,6},{... | collective-permute-start | bytes 786440 | tf_op jit(solution)/shard_map/ppermute | solution.py:286
  124.8 17.4 %all-to-all-start.2 = ((bf16[8,128,128]{2,1,0:T(8,128)(2,1)}), bf16[8,128,128]{2,1,0:T(8,128)(2,1)S(1)}, u32[]{:S(2)}, u32[]{:S(2)}) async-start(bf16[8,128,128]{2,1,0:T(8,128)(2,1)} %bitcast.4), calls=%async_computation.2 | async-start | bytes 524288 | tf_op jit(solution)/shard_map/all_to_all | solution.py:298
  134.0 8.8 %collective-permute-start.20 = (bf16[128,128]{1,0:T(8,128)(2,1)S(1)}, bf16[128,128]{1,0:T(8,128)(2,1)S(1)}, u32[]{:S(2)}, u32[]{:S(2)}) collective-permute-start(bf16[128,128]{1,0:T(8,128)(2,1)S(1)} %slice.113), channel_id=1, source_target_pairs={{0,16},{16,0},{1,17},{17,1},{2,18},{18,2},{3,19},{19,3},{4,20},{20... | collective-permute-start | bytes 98312 | tf_op jit(solution)/shard_map/ppermute | solution.py:290
  (15 other events, 13.0 us)
where the time goes:
time: 145 us; the launch traced here: 143 us
  starting transfers between devices  55.5 us (38%)
  waiting for transfers between devices  40.3 us (28%)
  Pallas kernels  20.3 us (14%)
  local copies, waits for them, and re-layouts  15.5 us (11%)
  other arithmetic  11 us (8%)
    all_to_all x4, starting transfers between devices, over_z(): return lax.all_to_all(a, 'z', 0, 0, tiled=True)  32.1 us
    all_to_all x4, waiting for transfers between devices, over_z(): return lax.all_to_all(a, 'z', 0, 0, tiled=True)  24.8 us
    ppermute x12, starting transfers between devices, from_x(): return lax.ppermute(a, 'x', [((i + step) % 4, i) for i in range(4)])  20.7 us
    ppermute x9, waiting for transfers between devices, swap(): return lax.ppermute(a, axis, [(0, 1), (1, 0)])  13.3 us
    pallas_call x1, Pallas kernels, backward(): pl.pallas_call(functools.partial(backward_kernel, sizes), out_shape=(wide...  11.6 us
    unnamed x39, local copies, waits for them, and re-layouts  10.8 us
    pallas_call x1, Pallas kernels, forward(): pl.pallas_call(functools.partial(forward_kernel, sizes), out_shape=(wide,...  8.7 us
    convert_element_type x5, other arithmetic, added(): return sum((t.astype(jnp.float32) for t in terms)).astype(jnp.bfloat16)  7.06 us
  transfers between devices with their start and end apart: 25, of which 10 were waited for; matrix products, arithmetic and copies ran while one was open for 10% of the time, Pallas kernels for 0%

commit v1 on v0

--- a/solution.py
+++ b/solution.py
@@ -138,9 +138,10 @@
 
 
 def backward_kernel(sizes, table, *refs):
-    pieces, refs = refs[:-14], refs[-14:]
-    stats_ref, dq_ref, dk_own, dk_other, dv_own, dv_other = refs[:6]
-    q_all, g_all, k_all, v_all, dk_acc, dv_acc, dq_t, sems = refs[6:]
+    pieces, refs = refs[: -13 - GROUP], refs[-13 - GROUP :]
+    stats_refs, refs = refs[:GROUP], refs[GROUP:]
+    dq_ref, dk_own, dk_other, dv_own, dv_other = refs[:5]
+    q_all, g_all, k_all, v_all, dk_acc, dv_acc, dq_t, sems = refs[5:]
     half = sizes.half
     copies = loaded(sizes, pieces, q_all, g_all, k_all, v_all, sems)
 
@@ -157,7 +158,9 @@
     def one_block(b, carry):
         block = Block(sizes, table, b, q_all, g_all)
         dq_t[...] = jnp.zeros_like(dq_t)
-        stats = stats_ref[b]
+        stats = stats_refs[0][b]
+        for i in range(1, GROUP):
+            stats = stats + stats_refs[i][lax.rem(b + sizes.queries - 2 * i, sizes.queries)]
         inverse = 1.0 / stats[0:1, :]
         row_dot = stats[1:2, :] * inverse
 
@@ -236,7 +239,7 @@
     return pl.pallas_call(
         functools.partial(backward_kernel, sizes),
         out_shape=(wide, term, term, term, term),
-        in_specs=[SMEM_SPEC] + [HBM_SPEC] * len(pieces) + [VMEM_SPEC],
+        in_specs=[SMEM_SPEC] + [HBM_SPEC] * len(pieces) + [VMEM_SPEC] * GROUP,
         out_specs=(VMEM_SPEC,) * 5,
         scratch_shapes=held_arrays(sizes)
         + [
@@ -248,7 +251,7 @@
         compiler_params=pltpu.CompilerParams(vmem_limit_bytes=32 * 1024 * 1024),
         cost_estimate=cost(sizes, 6),
         name="backward",
-    )(table, *pieces, stats)
+    )(table, *pieces, *stats)
 
 
 def index_table(sizes, pair_order, doc_lengths, z, y, x, core):
@@ -341,11 +344,10 @@
 
 
 def shared_stats(stats):
-    total = stats
+    arrived = [stats]
     for step in (1, 2, 3):
-        arrived = from_x(stats, step)
-        total = total + jnp.roll(arrived, 2 * step, axis=0)
-    return total
+        arrived.append(from_x(stats, step))
+    return arrived
 
 
 def grads_of(queries, keys, values, grad_out, pair_order, doc_lengths):
@@ -355,11 +357,13 @@
     spot = [lax.axis_index(a) for a in AXES]
     table = index_table(sizes, pair_order, doc_lengths, *spot)
     pieces = gathered_x(queries, grad_out) + gathered_keys(keys, values)
+    pieces = [pltpu.with_memory_space_constraint(p, pltpu.HBM) for p in pieces]
     out_parts, stats = forward(sizes, table, pieces)
     stats = shared_stats(stats)
     out_parts = summed_x(out_parts, tokens)
     dq_parts, *terms = backward(sizes, table, pieces, stats)
-    total = stats[:2, 0, :].reshape(2, sizes.heads, sizes.half)
+    total = sum(stats[i][(8 - 2 * i) % 8 : (8 - 2 * i) % 8 + 2, 0, :] for i in range(GROUP))
+    total = total.reshape(2, sizes.heads, sizes.half)
     total = jnp.swapaxes(total, 1, 2).reshape(tokens, sizes.heads, 1)
     out = sum(p.astype(jnp.float32) for p in out_parts).reshape(tokens, sizes.heads, hdim)
     out = (out / total).astype(jnp.bfloat16).reshape(tokens, width)

time: 145 us -> 134 us (0.924)
  local copies, waits for them, and re-layouts: 15.5 us -> 5.58 us
  starting transfers between devices: 55.5 us -> 53.9 us
  waiting for transfers between devices: 40.3 us -> 41.8 us
    unnamed x39 -> x25, local copies, waits for them, and re-layouts: 10.8 us -> 1.69 us
    convert_element_type x5, other arithmetic: 7.06 us -> 5.28 us  [added(): return sum((t.astype(jnp.float32) for t in terms)).astype(jnp.bfloat16)]
  transfers between devices with their start and end apart: 25 -> 25, of which waited for: 10 -> 9; matrix products, arithmetic and copies ran while one was open for 10% -> 10% of each run, Pallas kernels for 0% -> 0%
where the time goes in v1:
time: 134 us
  starting transfers between devices  53.9 us (40%)
  waiting for transfers between devices  41.8 us (31%)
  Pallas kernels  21.3 us (16%)
  other arithmetic  10.2 us (8%)
  local copies, waits for them, and re-layouts  5.58 us (4%)
    all_to_all x4, starting transfers between devices, over_z(): return lax.all_to_all(a, 'z', 0, 0, tiled=True)  32 us
    all_to_all x4, waiting for transfers between devices, over_z(): return lax.all_to_all(a, 'z', 0, 0, tiled=True)  24.8 us
    ppermute x12, starting transfers between devices, from_x(): return lax.ppermute(a, 'x', [((i + step) % 4, i) for i in range(4)])  19.3 us
    ppermute x9, waiting for transfers between devices, swap(): return lax.ppermute(a, axis, [(0, 1), (1, 0)])  14.4 us
    pallas_call x1, Pallas kernels, backward(): pl.pallas_call(functools.partial(backward_kernel, sizes), out_shape=(wide...  11.7 us
    pallas_call x1, Pallas kernels, forward(): pl.pallas_call(functools.partial(forward_kernel, sizes), out_shape=(wide,...  9.58 us
    convert_element_type x5, other arithmetic, added(): return sum((t.astype(jnp.float32) for t in terms)).astype(jnp.bfloat16)  5.28 us
  transfers between devices with their start and end apart: 25, of which 9 were waited for; matrix products, arithmetic and copies ran while one was open for 10% of the time, Pallas kernels for 0%

profile of v1, /device:TPU:16, one launch (start us, length us, event | category | flops | bytes accessed | tf_op | source)
XLA Modules:
  0.0 133.7 jit_solution(14841196968757297332)
XLA Ops:
  0.6 1.0 constant_dynamic-update-slice_fusion.1
  1.7 2.8 %collective-permute-start = (bf16[256,1024]{1,0:T(8,128)(2,1)S(1)}, bf16[256,1024]{1,0:T(8,128)(2,1)S(1)}, u32[]{:S(2)}, u32[]{:S(2)}) collective-permute-start(bf16[256,1024]{1,0:T(8,128)(2,1)S(1)} %constant_dynamic-update-slice_fusion.refs_0_), channel_id=1, source_target_pairs={{4,0},{8,4},{12,8},{0,12},{5,1},{9,5},{13,9},{1,13},{6,2},{10,6},{... | collective-permute-start | bytes 1572872 | tf_op jit(solution)/shard_map/ppermute | solution.py:289
  5.3 0.9 collective-permute-start.2
  7.0 8.6 %all-to-all-start = ((bf16[8,128,128]{2,1,0:T(8,128)(2,1)}), bf16[8,128,128]{2,1,0:T(8,128)(2,1)S(1)}, u32[]{:S(2)}, u32[]{:S(2)}) async-start(bf16[8,128,128]{2,1,0:T(8,128)(2,1)} %tile.4), calls=%async_computation | async-start | bytes 524288 | tf_op jit(solution)/shard_map/all_to_all | solution.py:301
  16.1 5.0 %collective-permute-done.6 = bf16[128,128]{1,0:T(8,128)(2,1)S(1)} collective-permute-done((bf16[128,128]{1,0:T(8,128)(2,1)S(1)}, bf16[128,128]{1,0:T(8,128)(2,1)S(1)}, u32[]{:S(2)}, u32[]{:S(2)}) %collective-permute-start.6) | collective-permute-done | bytes 32800 | tf_op jit(solution)/shard_map/ppermute | solution.py:293
  21.1 5.5 %all-to-all-done = bf16[8,128,128]{2,1,0:T(8,128)(2,1)S(1)} async-done(((bf16[8,128,128]{2,1,0:T(8,128)(2,1)}), bf16[8,128,128]{2,1,0:T(8,128)(2,1)S(1)}, u32[]{:S(2)}, u32[]{:S(2)}) %all-to-all-start) | async-done | bytes 262176 | tf_op jit(solution)/shard_map/all_to_all | solution.py:301
  26.6 0.9 tile.5
  27.5 3.5 %all-to-all-start.1 = ((bf16[8,256,128]{2,1,0:T(8,128)(2,1)}), bf16[8,256,128]{2,1,0:T(8,128)(2,1)S(1)}, u32[]{:S(2)}, u32[]{:S(2)}) async-start(bf16[8,256,128]{2,1,0:T(8,128)(2,1)} %tile.5), calls=%async_computation.1 | async-start | bytes 1048576 | tf_op jit(solution)/shard_map/all_to_all | solution.py:301
  32.8 13.4 %all-to-all-done.1 = bf16[8,256,128]{2,1,0:T(8,128)(2,1)S(1)} async-done(((bf16[8,256,128]{2,1,0:T(8,128)(2,1)}), bf16[8,256,128]{2,1,0:T(8,128)(2,1)S(1)}, u32[]{:S(2)}, u32[]{:S(2)}) %all-to-all-start.1) | async-done | bytes 524320 | tf_op jit(solution)/shard_map/all_to_all | solution.py:301
  47.4 1.2 collective-permute-done.4.refs_6_
  49.0 9.6 %forward.1 = (bf16[512,1024]{1,0:T(8,128)(2,1)S(1)}, f32[8,2,512]{2,1,0:T(2,128)S(1)}) custom-call(s32[232]{0:T(256)S(1)} %concatenate.25.table, bf16[256,1024]{1,0:T(8,128)(2,1)} %copy-done.3, bf16[256,1024]{1,0:T(8,128)(2,1)} %copy-done.7, bf16[256,1024]{1,0:T(8,128)(2,1)} %copy-done.8, bf16[256,1024]{1,0:T(8,128)(2,1)} %copy-done.9, ...), custom_call_target="tpu_custom_call" | custom-call | flops 2147483648 | bytes 6291456 | tf_op jit(solution)/shard_map/forward/pallas_call | solution.py:219
  58.6 3.2 %collective-permute-start.13 = (f32[8,2,512]{2,1,0:T(2,128)S(1)}, f32[8,2,512]{2,1,0:T(2,128)S(1)}, u32[]{:S(2)}, u32[]{:S(2)}) collective-permute-start(f32[8,2,512]{2,1,0:T(2,128)S(1)} %get-tuple-element.12.refs_10_), channel_id=1, source_target_pairs={{12,0},{0,4},{4,8},{8,12},{13,1},{1,5},{5,9},{9,13},{14,2},{2,6},{... | collective-permute-start | bytes 98312 | tf_op jit(solution)/shard_map/ppermute | solution.py:289
  62.5 2.1 %collective-permute-start.11 = (f32[8,2,512]{2,1,0:T(2,128)S(1)}, f32[8,2,512]{2,1,0:T(2,128)S(1)}, u32[]{:S(2)}, u32[]{:S(2)}) collective-permute-start(f32[8,2,512]{2,1,0:T(2,128)S(1)} %get-tuple-element.12.refs_10_), channel_id=1, source_target_pairs={{4,0},{8,4},{12,8},{0,12},{5,1},{9,5},{13,9},{1,13},{6,2},{10,6},{... | collective-permute-start | bytes 98312 | tf_op jit(solution)/shard_map/ppermute | solution.py:289
  64.6 2.6 %collective-permute-done.12.refs_12_ = f32[8,2,512]{2,1,0:T(2,128)S(1)} collective-permute-done((f32[8,2,512]{2,1,0:T(2,128)S(1)}, f32[8,2,512]{2,1,0:T(2,128)S(1)}, u32[]{:S(2)}, u32[]{:S(2)}) %collective-permute-start.12) | collective-permute-done | bytes 32800 | tf_op jit(solution)/shard_map/ppermute | solution.py:289
  67.2 11.7 %backward.1 = (bf16[512,1024]{1,0:T(8,128)(2,1)S(1)}, bf16[2048,128]{1,0:T(8,128)(2,1)S(1)}, bf16[2048,128]{1,0:T(8,128)(2,1)S(1)}, bf16[2048,128]{1,0:T(8,128)(2,1)S(1)}, bf16[2048,128]{1,0:T(8,128)(2,1)S(1)}) custom-call(s32[232]{0:T(256)S(1)} %concatenate.25.table, bf16[256,1024]{1,0:T(8,128)(2,1)} %copy-done.3, bf16[256,1024]{1,0:T(8,128)(2,1)} %copy-done.7, ...), custom_call_target="tpu_custom_call" | custom-call | flops 6442450944 | bytes 6291456 | tf_op jit(solution)/shard_map/backward/pallas_call | solution.py:239
  79.6 1.4 %collective-permute-done.19 = bf16[2048,128]{1,0:T(8,128)(2,1)S(1)} collective-permute-done((bf16[2048,128]{1,0:T(8,128)(2,1)S(1)}, bf16[2048,128]{1,0:T(8,128)(2,1)S(1)}, u32[]{:S(2)}, u32[]{:S(2)}) %collective-permute-start.19) | collective-permute-done | bytes 524320 | tf_op jit(solution)/shard_map/ppermute | solution.py:293
  81.0 0.9 add_convert_fusion
  81.9 13.0 %all-to-all-start.3 = ((bf16[8,256,128]{2,1,0:T(8,128)(2,1)}), bf16[8,256,128]{2,1,0:T(8,128)(2,1)}, u32[]{:S(2)}, u32[]{:S(2)}) async-start(bf16[8,256,128]{2,1,0:T(8,128)(2,1)} %bitcast.13), calls=%async_computation.3 | async-start | bytes 1048576 | tf_op jit(solution)/shard_map/all_to_all | solution.py:301
  94.9 0.9 fusion.19
  95.8 2.7 %collective-permute-start.9 = (bf16[128,1024]{1,0:T(8,128)(2,1)}, bf16[128,1024]{1,0:T(8,128)(2,1)}, u32[]{:S(2)}, u32[]{:S(2)}) collective-permute-start(bf16[128,1024]{1,0:T(8,128)(2,1)} %get-tuple-element.34), channel_id=1, source_target_pairs={{8,0},{12,4},{0,8},{4,12},{9,1},{13,5},{1,9},{5,13},{10,2},{14,6},... | collective-permute-start | bytes 786440 | tf_op jit(solution)/shard_map/ppermute | solution.py:289
  99.0 1.0 add_convert_fusion.2
  100.2 0.9 fusion.18
  101.3 1.6 %collective-permute-start.16 = (bf16[128,1024]{1,0:T(8,128)(2,1)}, bf16[128,1024]{1,0:T(8,128)(2,1)S(1)}, u32[]{:S(2)}, u32[]{:S(2)}) collective-permute-start(bf16[128,1024]{1,0:T(8,128)(2,1)} %get-tuple-element.30), channel_id=1, source_target_pairs={{12,0},{0,4},{4,8},{8,12},{13,1},{1,5},{5,9},{9,13},{14,2},{2,6},{... | collective-permute-start | bytes 786440 | tf_op jit(solution)/shard_map/ppermute | solution.py:289
  102.9 6.4 %collective-permute-done.18 = bf16[1024,128]{1,0:T(8,128)(2,1)} collective-permute-done((bf16[1024,128]{1,0:T(8,128)(2,1)S(1)}, bf16[1024,128]{1,0:T(8,128)(2,1)}, u32[]{:S(2)}, u32[]{:S(2)}) %collective-permute-start.18) | collective-permute-done | bytes 262176 | tf_op jit(solution)/shard_map/ppermute | solution.py:293
  109.3 2.6 %collective-permute-start.15 = (bf16[128,1024]{1,0:T(8,128)(2,1)}, bf16[128,1024]{1,0:T(8,128)(2,1)S(1)}, u32[]{:S(2)}, u32[]{:S(2)}) collective-permute-start(bf16[128,1024]{1,0:T(8,128)(2,1)} %get-tuple-element.31), channel_id=1, source_target_pairs={{8,0},{12,4},{0,8},{4,12},{9,1},{13,5},{1,9},{5,13},{10,2},{14,6},... | collective-permute-start | bytes 786440 | tf_op jit(solution)/shard_map/ppermute | solution.py:289
  111.9 1.8 %add_convert_fusion.1 = bf16[1024,128]{1,0:T(8,128)(2,1)} fusion(bf16[1024,128]{1,0:T(8,128)(2,1)} %collective-permute-done.18, bf16[2048,128]{1,0:T(8,128)(2,1)} %collective-permute-done.17, bf16[2048,128]{1,0:T(8,128)(2,1)S(1)} %get-tuple-element.14), kind=kLoop, calls=%fused_computation.4 | loop fusion | flops 786432 | bytes 1048576 | tf_op jit(solution)/shard_map/convert_element_type | solution.py:297
  113.8 1.3 collective-permute-start.14
  115.0 6.9 %all-to-all-start.2 = ((bf16[8,128,128]{2,1,0:T(8,128)(2,1)}), bf16[8,128,128]{2,1,0:T(8,128)(2,1)S(1)}, u32[]{:S(2)}, u32[]{:S(2)}) async-start(bf16[8,128,128]{2,1,0:T(8,128)(2,1)} %bitcast.4), calls=%async_computation.2 | async-start | bytes 524288 | tf_op jit(solution)/shard_map/all_to_all | solution.py:301
  122.2 2.0 %fusion = bf16[128,1024]{1,0:T(8,128)(2,1)} fusion(f32[16,8,8,128]{3,2,1,0:T(8,128)S(1)} %bitcast.14, bf16[128,1024]{1,0:T(8,128)(2,1)S(1)} %collective-permute-done.10, bf16[128,1024]{1,0:T(8,128)(2,1)} %collective-permute-done.9, bf16[128,1024]{1,0:T(8,128)(2,1)} %collective-permute-done.8, bf16[512,1024]{1,0:T(8,128)(2,1)S(1)} %get-tuple-element.11), kind=kLoop, calls=%fused_computation.3 | loop fusion | flops 1179648 | bytes 1835008 | tf_op jit(solution)/shard_map/convert_element_type | solution.py:369
  124.2 1.1 convert_reduce_fusion
  125.7 0.9 add_convert_fusion.3
  126.6 5.9 %all-to-all-done.2 = bf16[8,128,128]{2,1,0:T(8,128)(2,1)S(1)} async-done(((bf16[8,128,128]{2,1,0:T(8,128)(2,1)}), bf16[8,128,128]{2,1,0:T(8,128)(2,1)S(1)}, u32[]{:S(2)}, u32[]{:S(2)}) %all-to-all-start.2) | async-done | bytes 262176 | tf_op jit(solution)/shard_map/all_to_all | solution.py:301
  (82 shorter events, 9.4 us)
Async XLA Ops:
  1.7 4.6 %copy-start.4 = (bf16[128,128]{1,0:T(8,128)(2,1)S(1)}, bf16[128,128]{1,0:T(8,128)(2,1)}, u32[]{:S(2)}) copy-start(bf16[128,128]{1,0:T(8,128)(2,1)} %param.7) | copy-start | bytes 98308
  1.7 25.8 %copy-start.3 = (bf16[256,1024]{1,0:T(8,128)(2,1)}, bf16[256,1024]{1,0:T(8,128)(2,1)S(1)}, u32[]{:S(2)}) copy-start(bf16[256,1024]{1,0:T(8,128)(2,1)S(1)} %constant_dynamic-update-slice_fusion.refs_0_) | copy-start | bytes 1572868
  1.7 44.5 %collective-permute-start = (bf16[256,1024]{1,0:T(8,128)(2,1)S(1)}, bf16[256,1024]{1,0:T(8,128)(2,1)S(1)}, u32[]{:S(2)}, u32[]{:S(2)}) collective-permute-start(bf16[256,1024]{1,0:T(8,128)(2,1)S(1)} %constant_dynamic-update-slice_fusion.refs_0_), channel_id=1, source_target_pairs={{4,0},{8,4},{12,8},{0,12},{5,1},{9,5},{13,9},{1,13},{6,2},{10,6},{... | collective-permute-start | bytes 1572872 | tf_op jit(solution)/shard_map/ppermute | solution.py:289
  4.5 42.9 %collective-permute-start.1 = (bf16[256,1024]{1,0:T(8,128)(2,1)S(1)}, bf16[256,1024]{1,0:T(8,128)(2,1)S(1)}, u32[]{:S(2)}, u32[]{:S(2)}) collective-permute-start(bf16[256,1024]{1,0:T(8,128)(2,1)S(1)} %constant_dynamic-update-slice_fusion.refs_0_), channel_id=1, source_target_pairs={{8,0},{12,4},{0,8},{4,12},{9,1},{13,5},{1,9},{5,13},{10,2},{14,6},... | collective-permute-start | bytes 1572872 | tf_op jit(solution)/shard_map/ppermute | solution.py:289
  5.3 42.1 %collective-permute-start.2 = (bf16[256,1024]{1,0:T(8,128)(2,1)S(1)}, bf16[256,1024]{1,0:T(8,128)(2,1)S(1)}, u32[]{:S(2)}, u32[]{:S(2)}) collective-permute-start(bf16[256,1024]{1,0:T(8,128)(2,1)S(1)} %constant_dynamic-update-slice_fusion.refs_0_), channel_id=1, source_target_pairs={{12,0},{0,4},{4,8},{8,12},{13,1},{1,5},{5,9},{9,13},{14,2},{2,6},{... | collective-permute-start | bytes 1572872 | tf_op jit(solution)/shard_map/ppermute | solution.py:289
  7.0 8.6 %copy-start.5 = (bf16[128,128]{1,0:T(8,128)(2,1)S(1)}, bf16[128,128]{1,0:T(8,128)(2,1)}, u32[]{:S(2)}) copy-start(bf16[128,128]{1,0:T(8,128)(2,1)} %param.8) | copy-start | bytes 98308
  7.0 9.0 %copy-start.6 = (s32[128]{0:T(128)S(1)}, s32[128]{0:T(128)}, u32[]{:S(2)}) copy-start(s32[128]{0:T(128)} %param.10) | copy-start | bytes 1540
  7.0 19.6 %all-to-all-start = ((bf16[8,128,128]{2,1,0:T(8,128)(2,1)}), bf16[8,128,128]{2,1,0:T(8,128)(2,1)S(1)}, u32[]{:S(2)}, u32[]{:S(2)}) async-start(bf16[8,128,128]{2,1,0:T(8,128)(2,1)} %tile.4), calls=%async_computation | async-start | bytes 524288 | tf_op jit(solution)/shard_map/all_to_all | solution.py:301
  15.6 5.5 %collective-permute-start.6 = (bf16[128,128]{1,0:T(8,128)(2,1)S(1)}, bf16[128,128]{1,0:T(8,128)(2,1)S(1)}, u32[]{:S(2)}, u32[]{:S(2)}) collective-permute-start(bf16[128,128]{1,0:T(8,128)(2,1)S(1)} %copy-done.5), channel_id=1, source_target_pairs={{0,16},{16,0},{1,17},{17,1},{2,18},{18,2},{3,19},{19,3},{4,20},{20... | collective-permute-start | bytes 98312 | tf_op jit(solution)/shard_map/ppermute | solution.py:293
  26.6 19.6 %copy-start.2 = (bf16[8,128,128]{2,1,0:T(8,128)(2,1)}, bf16[8,128,128]{2,1,0:T(8,128)(2,1)S(1)}, u32[]{:S(2)}) copy-start(bf16[8,128,128]{2,1,0:T(8,128)(2,1)S(1)} %all-to-all-done) | copy-start | bytes 786436
  27.5 18.7 %all-to-all-start.1 = ((bf16[8,256,128]{2,1,0:T(8,128)(2,1)}), bf16[8,256,128]{2,1,0:T(8,128)(2,1)S(1)}, u32[]{:S(2)}, u32[]{:S(2)}) async-start(bf16[8,256,128]{2,1,0:T(8,128)(2,1)} %tile.5), calls=%async_computation.1 | async-start | bytes 1048576 | tf_op jit(solution)/shard_map/all_to_all | solution.py:301
  32.3 14.5 %collective-permute-start.3 = (bf16[1024,128]{1,0:T(8,128)(2,1)S(1)}, bf16[1024,128]{1,0:T(8,128)(2,1)S(1)}, u32[]{:S(2)}, u32[]{:S(2)}) collective-permute-start(bf16[1024,128]{1,0:T(8,128)(2,1)S(1)} %bitcast.19), channel_id=1, source_target_pairs={{0,16},{16,0},{1,17},{17,1},{2,18},{18,2},{3,19},{19,3},{4,20},{20... | collective-permute-start | bytes 786440 | tf_op jit(solution)/shard_map/ppermute | solution.py:293
  46.2 2.8 %copy-start = (bf16[8,256,128]{2,1,0:T(8,128)(2,1)}, bf16[8,256,128]{2,1,0:T(8,128)(2,1)S(1)}, u32[]{:S(2)}) copy-start(bf16[8,256,128]{2,1,0:T(8,128)(2,1)S(1)} %all-to-all-done.1) | copy-start | bytes 1572868
  46.2 2.8 %collective-permute-start.7 = (bf16[2048,128]{1,0:T(8,128)(2,1)S(1)}, bf16[2048,128]{1,0:T(8,128)(2,1)}, u32[]{:S(2)}, u32[]{:S(2)}) collective-permute-start(bf16[2048,128]{1,0:T(8,128)(2,1)S(1)} %bitcast.15), channel_id=1, source_target_pairs={{0,2},{2,0},{1,3},{3,1},{4,6},{6,4},{5,7},{7,5},{8,10},{10,8},{9,1... | collective-permute-start | bytes 1572872 | tf_op jit(solution)/shard_map/ppermute | solution.py:293
  46.2 2.8 %copy-start.7 = (bf16[256,1024]{1,0:T(8,128)(2,1)}, bf16[256,1024]{1,0:T(8,128)(2,1)S(1)}, u32[]{:S(2)}) copy-start(bf16[256,1024]{1,0:T(8,128)(2,1)S(1)} %collective-permute-done.refs_1_) | copy-start | bytes 1572868
  46.2 2.4 %collective-permute-start.4 = (bf16[1024,128]{1,0:T(8,128)(2,1)S(1)}, bf16[1024,128]{1,0:T(8,128)(2,1)}, u32[]{:S(2)}, u32[]{:S(2)}) collective-permute-start(bf16[1024,128]{1,0:T(8,128)(2,1)S(1)} %bitcast.20), channel_id=1, source_target_pairs={{0,2},{2,0},{1,3},{3,1},{4,6},{6,4},{5,7},{7,5},{8,10},{10,8},{9,1... | collective-permute-start | bytes 786440 | tf_op jit(solution)/shard_map/ppermute | solution.py:293
  46.8 2.2 %collective-permute-start.5 = (bf16[1024,128]{1,0:T(8,128)(2,1)S(1)}, bf16[1024,128]{1,0:T(8,128)(2,1)}, u32[]{:S(2)}, u32[]{:S(2)}) collective-permute-start(bf16[1024,128]{1,0:T(8,128)(2,1)S(1)} %collective-permute-done.3.refs_5_), channel_id=1, source_target_pairs={{0,2},{2,0},{1,3},{3,1},{4,6},{6,4},{5,7},{7,5},{8,10},{10,8},{9,1... | collective-permute-start | bytes 786440 | tf_op jit(solution)/shard_map/ppermute | solution.py:293
  58.6 6.0 %collective-permute-start.13 = (f32[8,2,512]{2,1,0:T(2,128)S(1)}, f32[8,2,512]{2,1,0:T(2,128)S(1)}, u32[]{:S(2)}, u32[]{:S(2)}) collective-permute-start(f32[8,2,512]{2,1,0:T(2,128)S(1)} %get-tuple-element.12.refs_10_), channel_id=1, source_target_pairs={{12,0},{0,4},{4,8},{8,12},{13,1},{1,5},{5,9},{9,13},{14,2},{2,6},{... | collective-permute-start | bytes 98312 | tf_op jit(solution)/shard_map/ppermute | solution.py:289
  61.8 5.4 %collective-permute-start.12 = (f32[8,2,512]{2,1,0:T(2,128)S(1)}, f32[8,2,512]{2,1,0:T(2,128)S(1)}, u32[]{:S(2)}, u32[]{:S(2)}) collective-permute-start(f32[8,2,512]{2,1,0:T(2,128)S(1)} %get-tuple-element.12.refs_10_), channel_id=1, source_target_pairs={{8,0},{12,4},{0,8},{4,12},{9,1},{13,5},{1,9},{5,13},{10,2},{14,6},... | collective-permute-start | bytes 98312 | tf_op jit(solution)/shard_map/ppermute | solution.py:289
  62.5 4.7 %collective-permute-start.11 = (f32[8,2,512]{2,1,0:T(2,128)S(1)}, f32[8,2,512]{2,1,0:T(2,128)S(1)}, u32[]{:S(2)}, u32[]{:S(2)}) collective-permute-start(f32[8,2,512]{2,1,0:T(2,128)S(1)} %get-tuple-element.12.refs_10_), channel_id=1, source_target_pairs={{4,0},{8,4},{12,8},{0,12},{5,1},{9,5},{13,9},{1,13},{6,2},{10,6},{... | collective-permute-start | bytes 98312 | tf_op jit(solution)/shard_map/ppermute | solution.py:289
  79.0 2.0 %collective-permute-start.19 = (bf16[2048,128]{1,0:T(8,128)(2,1)S(1)}, bf16[2048,128]{1,0:T(8,128)(2,1)S(1)}, u32[]{:S(2)}, u32[]{:S(2)}) collective-permute-start(bf16[2048,128]{1,0:T(8,128)(2,1)S(1)} %get-tuple-element.17), channel_id=1, source_target_pairs={{0,2},{2,0},{1,3},{3,1},{4,6},{6,4},{5,7},{7,5},{8,10},{10,8},{9,1... | collective-permute-start | bytes 1572872 | tf_op jit(solution)/shard_map/ppermute | solution.py:293
  79.2 19.8 %collective-permute-start.17 = (bf16[2048,128]{1,0:T(8,128)(2,1)S(1)}, bf16[2048,128]{1,0:T(8,128)(2,1)}, u32[]{:S(2)}, u32[]{:S(2)}) collective-permute-start(bf16[2048,128]{1,0:T(8,128)(2,1)S(1)} %get-tuple-element.15), channel_id=1, source_target_pairs={{0,2},{2,0},{1,3},{3,1},{4,6},{6,4},{5,7},{7,5},{8,10},{10,8},{9,1... | collective-permute-start | bytes 1572872 | tf_op jit(solution)/shard_map/ppermute | solution.py:293
  81.9 33.1 %all-to-all-start.3 = ((bf16[8,256,128]{2,1,0:T(8,128)(2,1)}), bf16[8,256,128]{2,1,0:T(8,128)(2,1)}, u32[]{:S(2)}, u32[]{:S(2)}) async-start(bf16[8,256,128]{2,1,0:T(8,128)(2,1)} %bitcast.13), calls=%async_computation.3 | async-start | bytes 1048576 | tf_op jit(solution)/shard_map/all_to_all | solution.py:301
  95.8 18.0 %collective-permute-start.10 = (bf16[128,1024]{1,0:T(8,128)(2,1)}, bf16[128,1024]{1,0:T(8,128)(2,1)S(1)}, u32[]{:S(2)}, u32[]{:S(2)}) collective-permute-start(bf16[128,1024]{1,0:T(8,128)(2,1)} %get-tuple-element.33), channel_id=1, source_target_pairs={{12,0},{0,4},{4,8},{8,12},{13,1},{1,5},{5,9},{9,13},{14,2},{2,6},{... | collective-permute-start | bytes 786440 | tf_op jit(solution)/shard_map/ppermute | solution.py:289
  95.8 26.2 %collective-permute-start.9 = (bf16[128,1024]{1,0:T(8,128)(2,1)}, bf16[128,1024]{1,0:T(8,128)(2,1)}, u32[]{:S(2)}, u32[]{:S(2)}) collective-permute-start(bf16[128,1024]{1,0:T(8,128)(2,1)} %get-tuple-element.34), channel_id=1, source_target_pairs={{8,0},{12,4},{0,8},{4,12},{9,1},{13,5},{1,9},{5,13},{10,2},{14,6},... | collective-permute-start | bytes 786440 | tf_op jit(solution)/shard_map/ppermute | solution.py:289
  98.5 23.4 %collective-permute-start.8 = (bf16[128,1024]{1,0:T(8,128)(2,1)}, bf16[128,1024]{1,0:T(8,128)(2,1)}, u32[]{:S(2)}, u32[]{:S(2)}) collective-permute-start(bf16[128,1024]{1,0:T(8,128)(2,1)} %get-tuple-element.32), channel_id=1, source_target_pairs={{4,0},{8,4},{12,8},{0,12},{5,1},{9,5},{13,9},{1,13},{6,2},{10,6},{... | collective-permute-start | bytes 786440 | tf_op jit(solution)/shard_map/ppermute | solution.py:289
  100.1 9.2 %collective-permute-start.18 = (bf16[1024,128]{1,0:T(8,128)(2,1)S(1)}, bf16[1024,128]{1,0:T(8,128)(2,1)}, u32[]{:S(2)}, u32[]{:S(2)}) collective-permute-start(bf16[1024,128]{1,0:T(8,128)(2,1)S(1)} %add_convert_fusion.2), channel_id=1, source_target_pairs={{0,16},{16,0},{1,17},{17,1},{2,18},{18,2},{3,19},{19,3},{4,20},{20... | collective-permute-start | bytes 786440 | tf_op jit(solution)/shard_map/ppermute | solution.py:293
  101.3 24.4 %collective-permute-start.16 = (bf16[128,1024]{1,0:T(8,128)(2,1)}, bf16[128,1024]{1,0:T(8,128)(2,1)S(1)}, u32[]{:S(2)}, u32[]{:S(2)}) collective-permute-start(bf16[128,1024]{1,0:T(8,128)(2,1)} %get-tuple-element.30), channel_id=1, source_target_pairs={{12,0},{0,4},{4,8},{8,12},{13,1},{1,5},{5,9},{9,13},{14,2},{2,6},{... | collective-permute-start | bytes 786440 | tf_op jit(solution)/shard_map/ppermute | solution.py:289
  109.3 16.4 %collective-permute-start.15 = (bf16[128,1024]{1,0:T(8,128)(2,1)}, bf16[128,1024]{1,0:T(8,128)(2,1)S(1)}, u32[]{:S(2)}, u32[]{:S(2)}) collective-permute-start(bf16[128,1024]{1,0:T(8,128)(2,1)} %get-tuple-element.31), channel_id=1, source_target_pairs={{8,0},{12,4},{0,8},{4,12},{9,1},{13,5},{1,9},{5,13},{10,2},{14,6},... | collective-permute-start | bytes 786440 | tf_op jit(solution)/shard_map/ppermute | solution.py:289
  113.8 12.0 %collective-permute-start.14 = (bf16[128,1024]{1,0:T(8,128)(2,1)}, bf16[128,1024]{1,0:T(8,128)(2,1)S(1)}, u32[]{:S(2)}, u32[]{:S(2)}) collective-permute-start(bf16[128,1024]{1,0:T(8,128)(2,1)} %get-tuple-element.29), channel_id=1, source_target_pairs={{4,0},{8,4},{12,8},{0,12},{5,1},{9,5},{13,9},{1,13},{6,2},{10,6},{... | collective-permute-start | bytes 786440 | tf_op jit(solution)/shard_map/ppermute | solution.py:289
  115.0 17.4 %all-to-all-start.2 = ((bf16[8,128,128]{2,1,0:T(8,128)(2,1)}), bf16[8,128,128]{2,1,0:T(8,128)(2,1)S(1)}, u32[]{:S(2)}, u32[]{:S(2)}) async-start(bf16[8,128,128]{2,1,0:T(8,128)(2,1)} %bitcast.4), calls=%async_computation.2 | async-start | bytes 524288 | tf_op jit(solution)/shard_map/all_to_all | solution.py:301
  125.3 7.8 %collective-permute-start.20 = (bf16[128,128]{1,0:T(8,128)(2,1)S(1)}, bf16[128,128]{1,0:T(8,128)(2,1)S(1)}, u32[]{:S(2)}, u32[]{:S(2)}) collective-permute-start(bf16[128,128]{1,0:T(8,128)(2,1)S(1)} %slice.100), channel_id=1, source_target_pairs={{0,16},{16,0},{1,17},{17,1},{2,18},{18,2},{3,19},{19,3},{4,20},{20... | collective-permute-start | bytes 98312 | tf_op jit(solution)/shard_map/ppermute | solution.py:293
  (5 other events, 7.0 us)

commit v2 on v1

--- a/solution.py
+++ b/solution.py
@@ -74,11 +74,34 @@
             end = table[sizes.at_ends + d]
             start = jnp.where(end <= self.position, jnp.maximum(start, end), start)
         self.start = start
+        self.block = table[sizes.at_own + b]
+        last = self.block * half + half - 1
+        self.last_start = jnp.int32(0)
+        for d in range(sizes.docs):
+            end = table[sizes.at_ends + d]
+            self.last_start = jnp.where(end <= last, jnp.maximum(self.last_start, end), self.last_start)
         self.low = table[sizes.at_low + b]
         self.high = table[sizes.at_high + b]
         self.steps = lax.div(self.high - self.low + sizes.per_tile - 1, sizes.per_tile)
 
-    def tile(self, i, k_all, v_all):
+    def whole(self, i):
+        sizes, table = self.sizes, self.table
+        first = self.low + i * sizes.per_tile
+        last = jnp.minimum(first + sizes.per_tile, self.high) - 1
+        inside = table[sizes.at_block + first] * sizes.half >= self.last_start
+        past = table[sizes.at_block + last] < self.block
+        return inside & past & (first + sizes.per_tile <= self.high)
+
+    def each(self, step):
+        def one(i, carry):
+            whole = self.whole(i)
+            pl.when(whole)(lambda: step(i, False))
+            pl.when(jnp.logical_not(whole))(lambda: step(i, True))
+            return carry
+
+        lax.fori_loop(0, self.steps, one, 0)
+
+    def tile(self, i, k_all, v_all, masked):
         sizes, half = self.sizes, self.sizes.half
         k_at, v_at, keys = [], [], []
         inside = lax.broadcasted_iota(jnp.int32, (half, 1), 0)
@@ -93,8 +116,9 @@
         k_tile = jnp.concatenate([k_all[p, :] for p in k_at], axis=0)
         v_tile = jnp.concatenate([v_all[p, :] for p in v_at], axis=0)
         s_t = jnp.dot(k_tile, self.q_t, preferred_element_type=jnp.float32)
-        allowed = (key >= self.start) & (key <= self.position)
-        e_t = jnp.where(allowed, jnp.exp2(s_t * (sizes.scale * LOG2E)), 0.0)
+        e_t = jnp.exp2(s_t * (sizes.scale * LOG2E))
+        if masked:
+            e_t = jnp.where((key >= self.start) & (key <= self.position), e_t, 0.0)
         return k_at, v_at, k_tile, v_tile, e_t
 
     def put(self, ref, value_t):
@@ -120,13 +144,12 @@
         out_t[...] = jnp.zeros_like(out_t)
         totals[...] = jnp.zeros_like(totals)
 
-        def step(i, inner):
-            _, _, _, v_tile, e_t = block.tile(i, k_all, v_all)
+        def step(i, masked):
+            _, _, _, v_tile, e_t = block.tile(i, k_all, v_all, masked)
             totals[...] += jnp.sum(e_t.reshape(sizes.tile // 8, 8, sizes.rows), axis=0)
             out_t[...] += transposed_product(v_tile, e_t.astype(jnp.bfloat16))
-            return inner
-
-        lax.fori_loop(0, block.steps, step, 0)
+
+        block.each(step)
         o_t = out_t[...]
         total = jnp.sum(totals[...], axis=0, keepdims=True)
         row_dot = jnp.sum(block.g_t.astype(jnp.float32) * o_t, axis=0, keepdims=True)
@@ -164,8 +187,8 @@
         inverse = 1.0 / stats[0:1, :]
         row_dot = stats[1:2, :] * inverse
 
-        def step(i, inner):
-            k_at, v_at, k_tile, v_tile, e_t = block.tile(i, k_all, v_all)
+        def step(i, masked):
+            k_at, v_at, k_tile, v_tile, e_t = block.tile(i, k_all, v_all, masked)
             dp_t = jnp.dot(v_tile, block.g_t, preferred_element_type=jnp.float32)
             p_t = e_t * inverse
             ds_t = (p_t * (dp_t - row_dot)).astype(jnp.bfloat16)
@@ -176,9 +199,8 @@
             for u in range(sizes.per_tile):
                 dk_acc[k_at[u], :] += dk[u * half : (u + 1) * half, :]
                 dv_acc[v_at[u], :] += dv[u * half : (u + 1) * half, :]
-            return inner
-
-        lax.fori_loop(0, block.steps, step, 0)
+
+        block.each(step)
         block.put(dq_ref, dq_t[...] * sizes.scale)
         return carry
 
@@ -259,7 +281,7 @@
     device = jnp.arange(devices, dtype=jnp.int32)
     far_core, far_y = lax.rem(device % 2 + core, 2), lax.rem(device // 8 % 2 + y, 2)
     k_row = (far_core * 16 + far_y * 8 + device // 16) * sizes.tokens
-    v_row = (far_core * 16 + device // 16 * 2 + far_y) * sizes.tokens
+    v_row = (far_core * 16 + lax.rem(device // 16 - z + 8, 8) * 2 + far_y) * sizes.tokens
     mirrored = 2 * devices - 1 - pair_order
     block = jnp.concatenate([pair_order, mirrored])
     k_row = jnp.concatenate([k_row, k_row + sizes.half])
@@ -301,6 +323,10 @@
     return lax.all_to_all(a, "z", 0, 0, tiled=True)
 
 
+def from_z(a, step):
+    return lax.ppermute(a, "z", [((i + step) % 8, i) for i in range(8)])
+
+
 def gathered_x(queries, grad_out):
     both = jnp.concatenate([queries, grad_out], axis=0)
     pieces = [both]
@@ -312,7 +338,10 @@
 def gathered_keys(keys, values):
     values = jnp.concatenate([values, swap(values, "y")], axis=0)
     k_near = over_z(jnp.tile(keys, (8, 1)))
-    v = over_z(jnp.tile(values, (8, 1)))
+    v = [values]
+    for step in range(1, 8):
+        v.append(from_z(values, step))
+    v = jnp.concatenate(v, axis=0)
     k_far = swap(k_near, "y")
     return [k_near, k_far, swap(k_near, "core"), swap(k_far, "core"), v, swap(v, "core")]
 
@@ -328,9 +357,12 @@
 
 def scattered_values(own, other, tokens):
     other = swap(other, "core")
-    column = over_z(added(own, other))
-    column = column.reshape(8, 2 * tokens, -1).astype(jnp.float32)
-    column = jnp.sum(column, axis=0)
+    n = 2 * tokens
+    parts = [added(own[i * n : (i + 1) * n], other[i * n : (i + 1) * n]) for i in range(8)]
+    column = parts[0].astype(jnp.float32)
+    for step in range(1, 8):
+        arrived = from_z(parts[8 - step], step)
+        column = column + arrived.astype(jnp.float32)
     far = swap(column[tokens:].astype(jnp.bfloat16), "y")
     return added(column[:tokens], far)
 

time: 134 us -> 152 us (1.13)
  the two profiles are of different devices: /device:TPU:16 before, /device:TPU:8 now
where the time goes in v2:
time: 152 us; the launch traced here: 151 us
  starting transfers between devices  87.1 us (57%)
  waiting for transfers between devices  26.2 us (17%)
  Pallas kernels  20.3 us (13%)
  other arithmetic  10.2 us (7%)
  local copies, waits for them, and re-layouts  6.55 us (4%)
    ppermute x14, starting transfers between devices, from_z(): return lax.ppermute(a, 'z', [((i + step) % 8, i) for i in range(8)])  43.7 us
    ppermute x9, starting transfers between devices, swap(): return lax.ppermute(a, axis, [(0, 1), (1, 0)])  15.6 us
    ppermute x12, starting transfers between devices, from_x(): return lax.ppermute(a, 'x', [((i + step) % 4, i) for i in range(4)])  15.2 us
    all_to_all x2, starting transfers between devices, over_z(): return lax.all_to_all(a, 'z', 0, 0, tiled=True)  12.5 us
    pallas_call x1, Pallas kernels, backward(): pl.pallas_call(functools.partial(backward_kernel, sizes), out_shape=(wide...  11.5 us
    all_to_all x2, waiting for transfers between devices, over_z(): return lax.all_to_all(a, 'z', 0, 0, tiled=True)  9.47 us
    pallas_call x1, Pallas kernels, forward(): pl.pallas_call(functools.partial(forward_kernel, sizes), out_shape=(wide,...  8.74 us
    ppermute x14, waiting for transfers between devices, from_z(): return lax.ppermute(a, 'z', [((i + step) % 8, i) for i in range(8)])  8.46 us
  transfers between devices with their start and end apart: 37, of which 15 were waited for; matrix products, arithmetic and copies ran while one was open for 8% of the time, Pallas kernels for 0%

profile of v2, /device:TPU:8, one launch (start us, length us, event | category | flops | bytes accessed | tf_op | source)
XLA Modules:
  0.0 151.2 jit_solution(13536833179151472404)
XLA Ops:
  1.7 2.8 %collective-permute-start = (bf16[256,1024]{1,0:T(8,128)(2,1)S(1)}, bf16[256,1024]{1,0:T(8,128)(2,1)S(1)}, u32[]{:S(2)}, u32[]{:S(2)}) collective-permute-start(bf16[256,1024]{1,0:T(8,128)(2,1)S(1)} %constant_dynamic-update-slice_fusion.refs_0_), channel_id=1, source_target_pairs={{4,0},{8,4},{12,8},{0,12},{5,1},{9,5},{13,9},{1,13},{6,2},{10,6},{... | collective-permute-start | bytes 1572872 | tf_op jit(solution)/shard_map/ppermute | solution.py:311
  7.0 8.6 %all-to-all-start = ((bf16[8,128,128]{2,1,0:T(8,128)(2,1)}), bf16[8,128,128]{2,1,0:T(8,128)(2,1)S(1)}, u32[]{:S(2)}, u32[]{:S(2)}) async-start(bf16[8,128,128]{2,1,0:T(8,128)(2,1)} %tile.2), calls=%async_computation | async-start | bytes 524288 | tf_op jit(solution)/shard_map/all_to_all | solution.py:323
  15.6 2.4 %collective-permute-start.6 = (bf16[128,128]{1,0:T(8,128)(2,1)S(1)}, bf16[128,128]{1,0:T(8,128)(2,1)S(1)}, u32[]{:S(2)}, u32[]{:S(2)}) collective-permute-start(bf16[128,128]{1,0:T(8,128)(2,1)S(1)} %copy-done.4), channel_id=1, source_target_pairs={{0,16},{16,0},{1,17},{17,1},{2,18},{18,2},{3,19},{19,3},{4,20},{20... | collective-permute-start | bytes 98312 | tf_op jit(solution)/shard_map/ppermute | solution.py:315
  21.1 3.2 %collective-permute-start.7 = (bf16[256,128]{1,0:T(8,128)(2,1)S(1)}, bf16[256,128]{1,0:T(8,128)(2,1)S(1)}, u32[]{:S(2)}, u32[]{:S(2)}) collective-permute-start(bf16[256,128]{1,0:T(8,128)(2,1)S(1)} %get-tuple-element.42), channel_id=1, source_target_pairs={{32,0},{64,32},{96,64},{128,96},{160,128},{192,160},{224,192},{0,2... | collective-permute-start | bytes 196616 | tf_op jit(solution)/shard_map/ppermute | solution.py:327
  24.3 2.4 %collective-permute-start.8 = (bf16[256,128]{1,0:T(8,128)(2,1)S(1)}, bf16[256,128]{1,0:T(8,128)(2,1)S(1)}, u32[]{:S(2)}, u32[]{:S(2)}) collective-permute-start(bf16[256,128]{1,0:T(8,128)(2,1)S(1)} %get-tuple-element.42), channel_id=1, source_target_pairs={{64,0},{96,32},{128,64},{160,96},{192,128},{224,160},{0,192},{32,2... | collective-permute-start | bytes 196616 | tf_op jit(solution)/shard_map/ppermute | solution.py:327
  26.7 3.7 %collective-permute-start.9 = (bf16[256,128]{1,0:T(8,128)(2,1)S(1)}, bf16[256,128]{1,0:T(8,128)(2,1)S(1)}, u32[]{:S(2)}, u32[]{:S(2)}) collective-permute-start(bf16[256,128]{1,0:T(8,128)(2,1)S(1)} %get-tuple-element.42), channel_id=1, source_target_pairs={{96,0},{128,32},{160,64},{192,96},{224,128},{0,160},{32,192},{64,2... | collective-permute-start | bytes 196616 | tf_op jit(solution)/shard_map/ppermute | solution.py:327
  31.4 3.0 %collective-permute-start.10 = (bf16[256,128]{1,0:T(8,128)(2,1)S(1)}, bf16[256,128]{1,0:T(8,128)(2,1)S(1)}, u32[]{:S(2)}, u32[]{:S(2)}) collective-permute-start(bf16[256,128]{1,0:T(8,128)(2,1)S(1)} %get-tuple-element.42), channel_id=1, source_target_pairs={{128,0},{160,32},{192,64},{224,96},{0,128},{32,160},{64,192},{96,2... | collective-permute-start | bytes 196616 | tf_op jit(solution)/shard_map/ppermute | solution.py:327
  35.1 4.1 %collective-permute-start.11 = (bf16[256,128]{1,0:T(8,128)(2,1)S(1)}, bf16[256,128]{1,0:T(8,128)(2,1)S(1)}, u32[]{:S(2)}, u32[]{:S(2)}) collective-permute-start(bf16[256,128]{1,0:T(8,128)(2,1)S(1)} %get-tuple-element.42), channel_id=1, source_target_pairs={{160,0},{192,32},{224,64},{0,96},{32,128},{64,160},{96,192},{128,2... | collective-permute-start | bytes 196616 | tf_op jit(solution)/shard_map/ppermute | solution.py:327
  39.6 3.0 %collective-permute-start.12 = (bf16[256,128]{1,0:T(8,128)(2,1)S(1)}, bf16[256,128]{1,0:T(8,128)(2,1)S(1)}, u32[]{:S(2)}, u32[]{:S(2)}) collective-permute-start(bf16[256,128]{1,0:T(8,128)(2,1)S(1)} %get-tuple-element.42), channel_id=1, source_target_pairs={{192,0},{224,32},{0,64},{32,96},{64,128},{96,160},{128,192},{160,2... | collective-permute-start | bytes 196616 | tf_op jit(solution)/shard_map/ppermute | solution.py:327
  42.6 2.4 %collective-permute-done.11 = bf16[256,128]{1,0:T(8,128)(2,1)S(1)} collective-permute-done((bf16[256,128]{1,0:T(8,128)(2,1)S(1)}, bf16[256,128]{1,0:T(8,128)(2,1)S(1)}, u32[]{:S(2)}, u32[]{:S(2)}) %collective-permute-start.11) | collective-permute-done | bytes 65568 | tf_op jit(solution)/shard_map/ppermute | solution.py:327
  45.0 1.7 %collective-permute-start.13 = (bf16[256,128]{1,0:T(8,128)(2,1)S(1)}, bf16[256,128]{1,0:T(8,128)(2,1)S(1)}, u32[]{:S(2)}, u32[]{:S(2)}) collective-permute-start(bf16[256,128]{1,0:T(8,128)(2,1)S(1)} %get-tuple-element.42), channel_id=1, source_target_pairs={{224,0},{0,32},{32,64},{64,96},{96,128},{128,160},{160,192},{192,2... | collective-permute-start | bytes 196616 | tf_op jit(solution)/shard_map/ppermute | solution.py:327
  46.8 2.6 %collective-permute-start.3 = (bf16[1024,128]{1,0:T(8,128)(2,1)S(1)}, bf16[1024,128]{1,0:T(8,128)(2,1)S(1)}, u32[]{:S(2)}, u32[]{:S(2)}) collective-permute-start(bf16[1024,128]{1,0:T(8,128)(2,1)S(1)} %bitcast.13), channel_id=1, source_target_pairs={{0,16},{16,0},{1,17},{17,1},{2,18},{18,2},{3,19},{19,3},{4,20},{20... | collective-permute-start | bytes 786440 | tf_op jit(solution)/shard_map/ppermute | solution.py:315
  51.2 3.5 %collective-permute-done.3.refs_5_ = bf16[1024,128]{1,0:T(8,128)(2,1)S(1)} collective-permute-done((bf16[1024,128]{1,0:T(8,128)(2,1)S(1)}, bf16[1024,128]{1,0:T(8,128)(2,1)S(1)}, u32[]{:S(2)}, u32[]{:S(2)}) %collective-permute-start.3) | collective-permute-done | bytes 262176 | tf_op jit(solution)/shard_map/ppermute | solution.py:315
  56.7 8.7 %forward.1 = (bf16[512,1024]{1,0:T(8,128)(2,1)S(1)}, f32[8,2,512]{2,1,0:T(2,128)S(1)}) custom-call(s32[232]{0:T(256)S(1)} %concatenate.29.table, bf16[256,1024]{1,0:T(8,128)(2,1)} %copy-done.2, bf16[256,1024]{1,0:T(8,128)(2,1)} %copy-done.7, bf16[256,1024]{1,0:T(8,128)(2,1)} %copy-done.8, bf16[256,1024]{1,0:T(8,128)(2,1)} %collective-permute-done.2.refs_3_, ...), custom_call_target="tpu_custom_call" | custom-call | flops 2147483648 | bytes 6291456 | tf_op jit(solution)/shard_map/forward/pallas_call | solution.py:241
  65.5 2.7 %collective-permute-start.20 = (f32[8,2,512]{2,1,0:T(2,128)S(1)}, f32[8,2,512]{2,1,0:T(2,128)S(1)}, u32[]{:S(2)}, u32[]{:S(2)}) collective-permute-start(f32[8,2,512]{2,1,0:T(2,128)S(1)} %get-tuple-element.12.refs_10_), channel_id=1, source_target_pairs={{12,0},{0,4},{4,8},{8,12},{13,1},{1,5},{5,9},{9,13},{14,2},{2,6},{... | collective-permute-start | bytes 98312 | tf_op jit(solution)/shard_map/ppermute | solution.py:311
  69.2 1.7 %collective-permute-start.18 = (f32[8,2,512]{2,1,0:T(2,128)S(1)}, f32[8,2,512]{2,1,0:T(2,128)S(1)}, u32[]{:S(2)}, u32[]{:S(2)}) collective-permute-start(f32[8,2,512]{2,1,0:T(2,128)S(1)} %get-tuple-element.12.refs_10_), channel_id=1, source_target_pairs={{4,0},{8,4},{12,8},{0,12},{5,1},{9,5},{13,9},{1,13},{6,2},{10,6},{... | collective-permute-start | bytes 98312 | tf_op jit(solution)/shard_map/ppermute | solution.py:311
  71.2 2.4 %collective-permute-done.19.refs_12_ = f32[8,2,512]{2,1,0:T(2,128)S(1)} collective-permute-done((f32[8,2,512]{2,1,0:T(2,128)S(1)}, f32[8,2,512]{2,1,0:T(2,128)S(1)}, u32[]{:S(2)}, u32[]{:S(2)}) %collective-permute-start.19) | collective-permute-done | bytes 32800 | tf_op jit(solution)/shard_map/ppermute | solution.py:311
  73.6 11.5 %backward.1 = (bf16[512,1024]{1,0:T(8,128)(2,1)S(1)}, bf16[2048,128]{1,0:T(8,128)(2,1)S(1)}, bf16[2048,128]{1,0:T(8,128)(2,1)}, bf16[2048,128]{1,0:T(8,128)(2,1)S(1)}, bf16[2048,128]{1,0:T(8,128)(2,1)}) custom-call(s32[232]{0:T(256)S(1)} %concatenate.29.table, bf16[256,1024]{1,0:T(8,128)(2,1)} %copy-done.2, bf16[256,1024]{1,0:T(8,128)(2,1)} %copy-done.7, ...), custom_call_target="tpu_custom_call" | custom-call | flops 6442450944 | bytes 6291456 | tf_op jit(solution)/shard_map/backward/pallas_call | solution.py:261
  86.2 1.2 collective-permute-start.17
  87.4 3.0 %collective-permute-start.16 = (bf16[128,1024]{1,0:T(8,128)(2,1)}, bf16[128,1024]{1,0:T(8,128)(2,1)}, u32[]{:S(2)}, u32[]{:S(2)}) collective-permute-start(bf16[128,1024]{1,0:T(8,128)(2,1)} %get-tuple-element.41), channel_id=1, source_target_pairs={{8,0},{12,4},{0,8},{4,12},{9,1},{13,5},{1,9},{5,13},{10,2},{14,6},... | collective-permute-start | bytes 786440 | tf_op jit(solution)/shard_map/ppermute | solution.py:311
  93.1 3.6 %collective-permute-start.33 = (bf16[256,128]{1,0:T(8,128)(2,1)S(1)}, bf16[256,128]{1,0:T(8,128)(2,1)S(1)}, u32[]{:S(2)}, u32[]{:S(2)}) collective-permute-start(bf16[256,128]{1,0:T(8,128)(2,1)S(1)} %get-tuple-element.30), channel_id=1, source_target_pairs={{224,0},{0,32},{32,64},{64,96},{96,128},{128,160},{160,192},{192,2... | collective-permute-start | bytes 196616 | tf_op jit(solution)/shard_map/ppermute | solution.py:327
  96.8 4.7 %collective-permute-start.32 = (bf16[256,128]{1,0:T(8,128)(2,1)S(1)}, bf16[256,128]{1,0:T(8,128)(2,1)S(1)}, u32[]{:S(2)}, u32[]{:S(2)}) collective-permute-start(bf16[256,128]{1,0:T(8,128)(2,1)S(1)} %get-tuple-element.31), channel_id=1, source_target_pairs={{192,0},{224,32},{0,64},{32,96},{64,128},{96,160},{128,192},{160,2... | collective-permute-start | bytes 196616 | tf_op jit(solution)/shard_map/ppermute | solution.py:327
  101.5 7.5 %collective-permute-start.31 = (bf16[256,128]{1,0:T(8,128)(2,1)S(1)}, bf16[256,128]{1,0:T(8,128)(2,1)S(1)}, u32[]{:S(2)}, u32[]{:S(2)}) collective-permute-start(bf16[256,128]{1,0:T(8,128)(2,1)S(1)} %get-tuple-element.32), channel_id=1, source_target_pairs={{160,0},{192,32},{224,64},{0,96},{32,128},{64,160},{96,192},{128,2... | collective-permute-start | bytes 196616 | tf_op jit(solution)/shard_map/ppermute | solution.py:327
  110.1 7.9 %collective-permute-start.25 = (bf16[1024,128]{1,0:T(8,128)(2,1)S(1)}, bf16[1024,128]{1,0:T(8,128)(2,1)S(1)}, u32[]{:S(2)}, u32[]{:S(2)}) collective-permute-start(bf16[1024,128]{1,0:T(8,128)(2,1)S(1)} %add_convert_fusion.1), channel_id=1, source_target_pairs={{0,16},{16,0},{1,17},{17,1},{2,18},{18,2},{3,19},{19,3},{4,20},{20... | collective-permute-start | bytes 786440 | tf_op jit(solution)/shard_map/ppermute | solution.py:315
  119.1 4.1 %collective-permute-start.28 = (bf16[256,128]{1,0:T(8,128)(2,1)S(1)}, bf16[256,128]{1,0:T(8,128)(2,1)S(1)}, u32[]{:S(2)}, u32[]{:S(2)}) collective-permute-start(bf16[256,128]{1,0:T(8,128)(2,1)S(1)} %get-tuple-element.35), channel_id=1, source_target_pairs={{64,0},{96,32},{128,64},{160,96},{192,128},{224,160},{0,192},{32,2... | collective-permute-start | bytes 196616 | tf_op jit(solution)/shard_map/ppermute | solution.py:327
  123.2 1.6 %collective-permute-start.27 = (bf16[256,128]{1,0:T(8,128)(2,1)S(1)}, bf16[256,128]{1,0:T(8,128)(2,1)S(1)}, u32[]{:S(2)}, u32[]{:S(2)}) collective-permute-start(bf16[256,128]{1,0:T(8,128)(2,1)S(1)} %get-tuple-element.29), channel_id=1, source_target_pairs={{32,0},{64,32},{96,64},{128,96},{160,128},{192,160},{224,192},{0,2... | collective-permute-start | bytes 196616 | tf_op jit(solution)/shard_map/ppermute | solution.py:327
  125.0 2.0 %fusion = bf16[128,1024]{1,0:T(8,128)(2,1)} fusion(f32[16,8,8,128]{3,2,1,0:T(8,128)S(1)} %bitcast.11, bf16[128,1024]{1,0:T(8,128)(2,1)S(1)} %collective-permute-done.17, bf16[128,1024]{1,0:T(8,128)(2,1)} %collective-permute-done.16, bf16[128,1024]{1,0:T(8,128)(2,1)} %collective-permute-done.15, bf16[512,1024]{1,0:T(8,128)(2,1)S(1)} %get-tuple-element.11), kind=kLoop, calls=%fused_computation.1 | loop fusion | flops 1179648 | bytes 1835008 | tf_op jit(solution)/shard_map/convert_element_type | solution.py:401
  128.1 1.7 %collective-permute-done.28 = bf16[256,128]{1,0:T(8,128)(2,1)S(1)} collective-permute-done((bf16[256,128]{1,0:T(8,128)(2,1)S(1)}, bf16[256,128]{1,0:T(8,128)(2,1)S(1)}, u32[]{:S(2)}, u32[]{:S(2)}) %collective-permute-start.28) | collective-permute-done | bytes 65568 | tf_op jit(solution)/shard_map/ppermute | solution.py:327
  131.3 2.0 %collective-permute-start.34 = (bf16[128,128]{1,0:T(8,128)(2,1)S(1)}, bf16[128,128]{1,0:T(8,128)(2,1)S(1)}, u32[]{:S(2)}, u32[]{:S(2)}) collective-permute-start(bf16[128,128]{1,0:T(8,128)(2,1)S(1)} %slice.188), channel_id=1, source_target_pairs={{0,16},{16,0},{1,17},{17,1},{2,18},{18,2},{3,19},{19,3},{4,20},{20... | collective-permute-start | bytes 98312 | tf_op jit(solution)/shard_map/ppermute | solution.py:315
  133.3 1.8 %add_convert_fusion = bf16[1024,128]{1,0:T(8,128)(2,1)} fusion(bf16[1024,128]{1,0:T(8,128)(2,1)S(1)} %collective-permute-done.25, bf16[2048,128]{1,0:T(8,128)(2,1)} %collective-permute-done.24, bf16[2048,128]{1,0:T(8,128)(2,1)S(1)} %get-tuple-element.14), kind=kLoop, calls=%fused_computation.2 | loop fusion | flops 786432 | bytes 1048576 | tf_op jit(solution)/shard_map/convert_element_type | solution.py:319
  135.1 3.9 %all-to-all-start.1 = ((bf16[8,128,128]{2,1,0:T(8,128)(2,1)}), bf16[8,128,128]{2,1,0:T(8,128)(2,1)S(1)}, u32[]{:S(2)}, u32[]{:S(2)}) async-start(bf16[8,128,128]{2,1,0:T(8,128)(2,1)} %bitcast.3), calls=%async_computation.1 | async-start | bytes 524288 | tf_op jit(solution)/shard_map/all_to_all | solution.py:323
  141.1 9.5 %all-to-all-done.1 = bf16[8,128,128]{2,1,0:T(8,128)(2,1)S(1)} async-done(((bf16[8,128,128]{2,1,0:T(8,128)(2,1)}), bf16[8,128,128]{2,1,0:T(8,128)(2,1)S(1)}, u32[]{:S(2)}, u32[]{:S(2)}) %all-to-all-start.1) | async-done | bytes 262176 | tf_op jit(solution)/shard_map/all_to_all | solution.py:323
  (113 shorter events, 25.1 us)
Async XLA Ops:
  1.7 48.9 %collective-permute-start = (bf16[256,1024]{1,0:T(8,128)(2,1)S(1)}, bf16[256,1024]{1,0:T(8,128)(2,1)S(1)}, u32[]{:S(2)}, u32[]{:S(2)}) collective-permute-start(bf16[256,1024]{1,0:T(8,128)(2,1)S(1)} %constant_dynamic-update-slice_fusion.refs_0_), channel_id=1, source_target_pairs={{4,0},{8,4},{12,8},{0,12},{5,1},{9,5},{13,9},{1,13},{6,2},{10,6},{... | collective-permute-start | bytes 1572872 | tf_op jit(solution)/shard_map/ppermute | solution.py:311
  4.5 50.7 %collective-permute-start.1 = (bf16[256,1024]{1,0:T(8,128)(2,1)S(1)}, bf16[256,1024]{1,0:T(8,128)(2,1)S(1)}, u32[]{:S(2)}, u32[]{:S(2)}) collective-permute-start(bf16[256,1024]{1,0:T(8,128)(2,1)S(1)} %constant_dynamic-update-slice_fusion.refs_0_), channel_id=1, source_target_pairs={{8,0},{12,4},{0,8},{4,12},{9,1},{13,5},{1,9},{5,13},{10,2},{14,6},... | collective-permute-start | bytes 1572872 | tf_op jit(solution)/shard_map/ppermute | solution.py:311
  5.3 49.9 %collective-permute-start.2 = (bf16[256,1024]{1,0:T(8,128)(2,1)S(1)}, bf16[256,1024]{1,0:T(8,128)(2,1)}, u32[]{:S(2)}, u32[]{:S(2)}) collective-permute-start(bf16[256,1024]{1,0:T(8,128)(2,1)S(1)} %constant_dynamic-update-slice_fusion.refs_0_), channel_id=1, source_target_pairs={{12,0},{0,4},{4,8},{8,12},{13,1},{1,5},{5,9},{9,13},{14,2},{2,6},{... | collective-permute-start | bytes 1572872 | tf_op jit(solution)/shard_map/ppermute | solution.py:311
  7.0 39.8 %all-to-all-start = ((bf16[8,128,128]{2,1,0:T(8,128)(2,1)}), bf16[8,128,128]{2,1,0:T(8,128)(2,1)S(1)}, u32[]{:S(2)}, u32[]{:S(2)}) async-start(bf16[8,128,128]{2,1,0:T(8,128)(2,1)} %tile.2), calls=%async_computation | async-start | bytes 524288 | tf_op jit(solution)/shard_map/all_to_all | solution.py:323
  15.6 5.5 %collective-permute-start.6 = (bf16[128,128]{1,0:T(8,128)(2,1)S(1)}, bf16[128,128]{1,0:T(8,128)(2,1)S(1)}, u32[]{:S(2)}, u32[]{:S(2)}) collective-permute-start(bf16[128,128]{1,0:T(8,128)(2,1)S(1)} %copy-done.4), channel_id=1, source_target_pairs={{0,16},{16,0},{1,17},{17,1},{2,18},{18,2},{3,19},{19,3},{4,20},{20... | collective-permute-start | bytes 98312 | tf_op jit(solution)/shard_map/ppermute | solution.py:315
  21.1 5.6 %collective-permute-start.7 = (bf16[256,128]{1,0:T(8,128)(2,1)S(1)}, bf16[256,128]{1,0:T(8,128)(2,1)S(1)}, u32[]{:S(2)}, u32[]{:S(2)}) collective-permute-start(bf16[256,128]{1,0:T(8,128)(2,1)S(1)} %get-tuple-element.42), channel_id=1, source_target_pairs={{32,0},{64,32},{96,64},{128,96},{160,128},{192,160},{224,192},{0,2... | collective-permute-start | bytes 196616 | tf_op jit(solution)/shard_map/ppermute | solution.py:327
  24.3 7.1 %collective-permute-start.8 = (bf16[256,128]{1,0:T(8,128)(2,1)S(1)}, bf16[256,128]{1,0:T(8,128)(2,1)S(1)}, u32[]{:S(2)}, u32[]{:S(2)}) collective-permute-start(bf16[256,128]{1,0:T(8,128)(2,1)S(1)} %get-tuple-element.42), channel_id=1, source_target_pairs={{64,0},{96,32},{128,64},{160,96},{192,128},{224,160},{0,192},{32,2... | collective-permute-start | bytes 196616 | tf_op jit(solution)/shard_map/ppermute | solution.py:327
  26.7 8.4 %collective-permute-start.9 = (bf16[256,128]{1,0:T(8,128)(2,1)S(1)}, bf16[256,128]{1,0:T(8,128)(2,1)S(1)}, u32[]{:S(2)}, u32[]{:S(2)}) collective-permute-start(bf16[256,128]{1,0:T(8,128)(2,1)S(1)} %get-tuple-element.42), channel_id=1, source_target_pairs={{96,0},{128,32},{160,64},{192,96},{224,128},{0,160},{32,192},{64,2... | collective-permute-start | bytes 196616 | tf_op jit(solution)/shard_map/ppermute | solution.py:327
  31.4 8.2 %collective-permute-start.10 = (bf16[256,128]{1,0:T(8,128)(2,1)S(1)}, bf16[256,128]{1,0:T(8,128)(2,1)S(1)}, u32[]{:S(2)}, u32[]{:S(2)}) collective-permute-start(bf16[256,128]{1,0:T(8,128)(2,1)S(1)} %get-tuple-element.42), channel_id=1, source_target_pairs={{128,0},{160,32},{192,64},{224,96},{0,128},{32,160},{64,192},{96,2... | collective-permute-start | bytes 196616 | tf_op jit(solution)/shard_map/ppermute | solution.py:327
  35.1 9.9 %collective-permute-start.11 = (bf16[256,128]{1,0:T(8,128)(2,1)S(1)}, bf16[256,128]{1,0:T(8,128)(2,1)S(1)}, u32[]{:S(2)}, u32[]{:S(2)}) collective-permute-start(bf16[256,128]{1,0:T(8,128)(2,1)S(1)} %get-tuple-element.42), channel_id=1, source_target_pairs={{160,0},{192,32},{224,64},{0,96},{32,128},{64,160},{96,192},{128,2... | collective-permute-start | bytes 196616 | tf_op jit(solution)/shard_map/ppermute | solution.py:327
  39.6 7.1 %collective-permute-start.12 = (bf16[256,128]{1,0:T(8,128)(2,1)S(1)}, bf16[256,128]{1,0:T(8,128)(2,1)S(1)}, u32[]{:S(2)}, u32[]{:S(2)}) collective-permute-start(bf16[256,128]{1,0:T(8,128)(2,1)S(1)} %get-tuple-element.42), channel_id=1, source_target_pairs={{192,0},{224,32},{0,64},{32,96},{64,128},{96,160},{128,192},{160,2... | collective-permute-start | bytes 196616 | tf_op jit(solution)/shard_map/ppermute | solution.py:327
  45.0 5.5 %collective-permute-start.13 = (bf16[256,128]{1,0:T(8,128)(2,1)S(1)}, bf16[256,128]{1,0:T(8,128)(2,1)S(1)}, u32[]{:S(2)}, u32[]{:S(2)}) collective-permute-start(bf16[256,128]{1,0:T(8,128)(2,1)S(1)} %get-tuple-element.42), channel_id=1, source_target_pairs={{224,0},{0,32},{32,64},{64,96},{96,128},{128,160},{160,192},{192,2... | collective-permute-start | bytes 196616 | tf_op jit(solution)/shard_map/ppermute | solution.py:327
  46.8 8.0 %collective-permute-start.3 = (bf16[1024,128]{1,0:T(8,128)(2,1)S(1)}, bf16[1024,128]{1,0:T(8,128)(2,1)S(1)}, u32[]{:S(2)}, u32[]{:S(2)}) collective-permute-start(bf16[1024,128]{1,0:T(8,128)(2,1)S(1)} %bitcast.13), channel_id=1, source_target_pairs={{0,16},{16,0},{1,17},{17,1},{2,18},{18,2},{3,19},{19,3},{4,20},{20... | collective-permute-start | bytes 786440 | tf_op jit(solution)/shard_map/ppermute | solution.py:315
  65.5 5.7 %collective-permute-start.20 = (f32[8,2,512]{2,1,0:T(2,128)S(1)}, f32[8,2,512]{2,1,0:T(2,128)S(1)}, u32[]{:S(2)}, u32[]{:S(2)}) collective-permute-start(f32[8,2,512]{2,1,0:T(2,128)S(1)} %get-tuple-element.12.refs_10_), channel_id=1, source_target_pairs={{12,0},{0,4},{4,8},{8,12},{13,1},{1,5},{5,9},{9,13},{14,2},{2,6},{... | collective-permute-start | bytes 98312 | tf_op jit(solution)/shard_map/ppermute | solution.py:311
  85.2 6.8 %collective-permute-start.26 = (bf16[2048,128]{1,0:T(8,128)(2,1)}, bf16[2048,128]{1,0:T(8,128)(2,1)}, u32[]{:S(2)}, u32[]{:S(2)}) collective-permute-start(bf16[2048,128]{1,0:T(8,128)(2,1)} %get-tuple-element.17), channel_id=1, source_target_pairs={{0,2},{2,0},{1,3},{3,1},{4,6},{6,4},{5,7},{7,5},{8,10},{10,8},{9,1... | collective-permute-start | bytes 1572872 | tf_op jit(solution)/shard_map/ppermute | solution.py:315
  86.2 10.6 %collective-permute-start.17 = (bf16[128,1024]{1,0:T(8,128)(2,1)}, bf16[128,1024]{1,0:T(8,128)(2,1)S(1)}, u32[]{:S(2)}, u32[]{:S(2)}) collective-permute-start(bf16[128,1024]{1,0:T(8,128)(2,1)} %get-tuple-element.40), channel_id=1, source_target_pairs={{12,0},{0,4},{4,8},{8,12},{13,1},{1,5},{5,9},{9,13},{14,2},{2,6},{... | collective-permute-start | bytes 786440 | tf_op jit(solution)/shard_map/ppermute | solution.py:311
  87.4 22.7 %collective-permute-start.16 = (bf16[128,1024]{1,0:T(8,128)(2,1)}, bf16[128,1024]{1,0:T(8,128)(2,1)}, u32[]{:S(2)}, u32[]{:S(2)}) collective-permute-start(bf16[128,1024]{1,0:T(8,128)(2,1)} %get-tuple-element.41), channel_id=1, source_target_pairs={{8,0},{12,4},{0,8},{4,12},{9,1},{13,5},{1,9},{5,13},{10,2},{14,6},... | collective-permute-start | bytes 786440 | tf_op jit(solution)/shard_map/ppermute | solution.py:311
  90.4 27.6 %collective-permute-start.15 = (bf16[128,1024]{1,0:T(8,128)(2,1)}, bf16[128,1024]{1,0:T(8,128)(2,1)}, u32[]{:S(2)}, u32[]{:S(2)}) collective-permute-start(bf16[128,1024]{1,0:T(8,128)(2,1)} %get-tuple-element.39), channel_id=1, source_target_pairs={{4,0},{8,4},{12,8},{0,12},{5,1},{9,5},{13,9},{1,13},{6,2},{10,6},{... | collective-permute-start | bytes 786440 | tf_op jit(solution)/shard_map/ppermute | solution.py:311
  90.9 10.7 %collective-permute-start.24 = (bf16[2048,128]{1,0:T(8,128)(2,1)}, bf16[2048,128]{1,0:T(8,128)(2,1)}, u32[]{:S(2)}, u32[]{:S(2)}) collective-permute-start(bf16[2048,128]{1,0:T(8,128)(2,1)} %get-tuple-element.15), channel_id=1, source_target_pairs={{0,2},{2,0},{1,3},{3,1},{4,6},{6,4},{5,7},{7,5},{8,10},{10,8},{9,1... | collective-permute-start | bytes 1572872 | tf_op jit(solution)/shard_map/ppermute | solution.py:315
  93.1 24.8 %collective-permute-start.33 = (bf16[256,128]{1,0:T(8,128)(2,1)S(1)}, bf16[256,128]{1,0:T(8,128)(2,1)S(1)}, u32[]{:S(2)}, u32[]{:S(2)}) collective-permute-start(bf16[256,128]{1,0:T(8,128)(2,1)S(1)} %get-tuple-element.30), channel_id=1, source_target_pairs={{224,0},{0,32},{32,64},{64,96},{96,128},{128,160},{160,192},{192,2... | collective-permute-start | bytes 196616 | tf_op jit(solution)/shard_map/ppermute | solution.py:327
  96.8 22.3 %collective-permute-start.32 = (bf16[256,128]{1,0:T(8,128)(2,1)S(1)}, bf16[256,128]{1,0:T(8,128)(2,1)S(1)}, u32[]{:S(2)}, u32[]{:S(2)}) collective-permute-start(bf16[256,128]{1,0:T(8,128)(2,1)S(1)} %get-tuple-element.31), channel_id=1, source_target_pairs={{192,0},{224,32},{0,64},{32,96},{64,128},{96,160},{128,192},{160,2... | collective-permute-start | bytes 196616 | tf_op jit(solution)/shard_map/ppermute | solution.py:327
  101.5 21.7 %collective-permute-start.31 = (bf16[256,128]{1,0:T(8,128)(2,1)S(1)}, bf16[256,128]{1,0:T(8,128)(2,1)S(1)}, u32[]{:S(2)}, u32[]{:S(2)}) collective-permute-start(bf16[256,128]{1,0:T(8,128)(2,1)S(1)} %get-tuple-element.32), channel_id=1, source_target_pairs={{160,0},{192,32},{224,64},{0,96},{32,128},{64,160},{96,192},{128,2... | collective-permute-start | bytes 196616 | tf_op jit(solution)/shard_map/ppermute | solution.py:327
  110.1 23.2 %collective-permute-start.25 = (bf16[1024,128]{1,0:T(8,128)(2,1)S(1)}, bf16[1024,128]{1,0:T(8,128)(2,1)S(1)}, u32[]{:S(2)}, u32[]{:S(2)}) collective-permute-start(bf16[1024,128]{1,0:T(8,128)(2,1)S(1)} %add_convert_fusion.1), channel_id=1, source_target_pairs={{0,16},{16,0},{1,17},{17,1},{2,18},{18,2},{3,19},{19,3},{4,20},{20... | collective-permute-start | bytes 786440 | tf_op jit(solution)/shard_map/ppermute | solution.py:315
  118.0 9.0 %collective-permute-start.30 = (bf16[256,128]{1,0:T(8,128)(2,1)S(1)}, bf16[256,128]{1,0:T(8,128)(2,1)S(1)}, u32[]{:S(2)}, u32[]{:S(2)}) collective-permute-start(bf16[256,128]{1,0:T(8,128)(2,1)S(1)} %get-tuple-element.33), channel_id=1, source_target_pairs={{128,0},{160,32},{192,64},{224,96},{0,128},{32,160},{64,192},{96,2... | collective-permute-start | bytes 196616 | tf_op jit(solution)/shard_map/ppermute | solution.py:327
  118.0 10.1 %collective-permute-start.29 = (bf16[256,128]{1,0:T(8,128)(2,1)S(1)}, bf16[256,128]{1,0:T(8,128)(2,1)S(1)}, u32[]{:S(2)}, u32[]{:S(2)}) collective-permute-start(bf16[256,128]{1,0:T(8,128)(2,1)S(1)} %get-tuple-element.34), channel_id=1, source_target_pairs={{96,0},{128,32},{160,64},{192,96},{224,128},{0,160},{32,192},{64,2... | collective-permute-start | bytes 196616 | tf_op jit(solution)/shard_map/ppermute | solution.py:327
  119.1 10.8 %collective-permute-start.28 = (bf16[256,128]{1,0:T(8,128)(2,1)S(1)}, bf16[256,128]{1,0:T(8,128)(2,1)S(1)}, u32[]{:S(2)}, u32[]{:S(2)}) collective-permute-start(bf16[256,128]{1,0:T(8,128)(2,1)S(1)} %get-tuple-element.35), channel_id=1, source_target_pairs={{64,0},{96,32},{128,64},{160,96},{192,128},{224,160},{0,192},{32,2... | collective-permute-start | bytes 196616 | tf_op jit(solution)/shard_map/ppermute | solution.py:327
  123.2 7.2 %collective-permute-start.27 = (bf16[256,128]{1,0:T(8,128)(2,1)S(1)}, bf16[256,128]{1,0:T(8,128)(2,1)S(1)}, u32[]{:S(2)}, u32[]{:S(2)}) collective-permute-start(bf16[256,128]{1,0:T(8,128)(2,1)S(1)} %get-tuple-element.29), channel_id=1, source_target_pairs={{32,0},{64,32},{96,64},{128,96},{160,128},{192,160},{224,192},{0,2... | collective-permute-start | bytes 196616 | tf_op jit(solution)/shard_map/ppermute | solution.py:327
  127.0 12.4 %collective-permute-start.23 = (bf16[128,1024]{1,0:T(8,128)(2,1)}, bf16[128,1024]{1,0:T(8,128)(2,1)S(1)}, u32[]{:S(2)}, u32[]{:S(2)}) collective-permute-start(bf16[128,1024]{1,0:T(8,128)(2,1)} %get-tuple-element.37), channel_id=1, source_target_pairs={{12,0},{0,4},{4,8},{8,12},{13,1},{1,5},{5,9},{9,13},{14,2},{2,6},{... | collective-permute-start | bytes 786440 | tf_op jit(solution)/shard_map/ppermute | solution.py:311
  128.1 11.3 %collective-permute-start.22 = (bf16[128,1024]{1,0:T(8,128)(2,1)}, bf16[128,1024]{1,0:T(8,128)(2,1)S(1)}, u32[]{:S(2)}, u32[]{:S(2)}) collective-permute-start(bf16[128,1024]{1,0:T(8,128)(2,1)} %get-tuple-element.38), channel_id=1, source_target_pairs={{8,0},{12,4},{0,8},{4,12},{9,1},{13,5},{1,9},{5,13},{10,2},{14,6},... | collective-permute-start | bytes 786440 | tf_op jit(solution)/shard_map/ppermute | solution.py:311
  129.8 9.7 %collective-permute-start.21 = (bf16[128,1024]{1,0:T(8,128)(2,1)}, bf16[128,1024]{1,0:T(8,128)(2,1)S(1)}, u32[]{:S(2)}, u32[]{:S(2)}) collective-permute-start(bf16[128,1024]{1,0:T(8,128)(2,1)} %get-tuple-element.36), channel_id=1, source_target_pairs={{4,0},{8,4},{12,8},{0,12},{5,1},{9,5},{13,9},{1,13},{6,2},{10,6},{... | collective-permute-start | bytes 786440 | tf_op jit(solution)/shard_map/ppermute | solution.py:311
  131.3 9.2 %collective-permute-start.34 = (bf16[128,128]{1,0:T(8,128)(2,1)S(1)}, bf16[128,128]{1,0:T(8,128)(2,1)S(1)}, u32[]{:S(2)}, u32[]{:S(2)}) collective-permute-start(bf16[128,128]{1,0:T(8,128)(2,1)S(1)} %slice.188), channel_id=1, source_target_pairs={{0,16},{16,0},{1,17},{17,1},{2,18},{18,2},{3,19},{19,3},{4,20},{20... | collective-permute-start | bytes 98312 | tf_op jit(solution)/shard_map/ppermute | solution.py:315
  135.1 15.5 %all-to-all-start.1 = ((bf16[8,128,128]{2,1,0:T(8,128)(2,1)}), bf16[8,128,128]{2,1,0:T(8,128)(2,1)S(1)}, u32[]{:S(2)}, u32[]{:S(2)}) async-start(bf16[8,128,128]{2,1,0:T(8,128)(2,1)} %bitcast.3), calls=%async_computation.1 | async-start | bytes 524288 | tf_op jit(solution)/shard_map/all_to_all | solution.py:323
  (17 other events, 79.2 us)

commit v3 on v2

--- a/solution.py
+++ b/solution.py
@@ -32,25 +32,23 @@
         self.tile = self.per_tile * self.half
         self.scale = hdim ** (-0.5)
         self.at_key = 0
-        self.at_value = self.local
-        self.at_block = 2 * self.local
-        self.at_ends = 3 * self.local
+        self.at_block = self.local
+        self.at_ends = 2 * self.local
         self.at_own = self.at_ends + docs
         self.at_low = self.at_own + self.queries
         self.at_high = self.at_low + self.queries
 
 
-def loaded(sizes, pieces, q_all, g_all, k_all, v_all, sems):
+def loaded(sizes, pieces, q_all, g_all, kv_all, sems):
     moves = []
     tokens = sizes.tokens
     for i, piece in enumerate(pieces[:GROUP]):
         at = pl.ds(i * tokens, tokens)
         moves.append((piece.at[pl.ds(0, tokens), :], q_all.at[at, :]))
         moves.append((piece.at[pl.ds(tokens, tokens), :], g_all.at[at, :]))
-    for part, whole in ((pieces[GROUP:-2], k_all), (pieces[-2:], v_all)):
-        for i, piece in enumerate(part):
-            count = piece.shape[0]
-            moves.append((piece, whole.at[pl.ds(i * count, count), :]))
+    for i, piece in enumerate(pieces[GROUP:]):
+        count = piece.shape[0]
+        moves.append((piece, kv_all.at[pl.ds(i * count, count), :]))
     copies = [pltpu.make_async_copy(*move, sems.at[i]) for i, move in enumerate(moves)]
     for copy in copies:
         copy.start()
@@ -101,25 +99,24 @@
 
         lax.fori_loop(0, self.steps, one, 0)
 
-    def tile(self, i, k_all, v_all, masked):
-        sizes, half = self.sizes, self.sizes.half
-        k_at, v_at, keys = [], [], []
+    def tile(self, i, kv_all, masked):
+        sizes, half, hdim = self.sizes, self.sizes.half, self.sizes.hdim
+        places, keys = [], []
         inside = lax.broadcasted_iota(jnp.int32, (half, 1), 0)
         for u in range(sizes.per_tile):
             rank = self.low + i * sizes.per_tile + u
             held = jnp.minimum(rank, self.high - 1)
-            k_at.append(pl.ds(pl.multiple_of(self.table[sizes.at_key + held], half), half))
-            v_at.append(pl.ds(pl.multiple_of(self.table[sizes.at_value + held], half), half))
+            places.append(pl.ds(pl.multiple_of(self.table[sizes.at_key + held], half), half))
             first = jnp.where(rank < self.high, self.table[sizes.at_block + held] * half, FAR)
             keys.append(first + inside)
         key = jnp.concatenate(keys, axis=0)
-        k_tile = jnp.concatenate([k_all[p, :] for p in k_at], axis=0)
-        v_tile = jnp.concatenate([v_all[p, :] for p in v_at], axis=0)
+        k_tile = jnp.concatenate([kv_all[p, 0:hdim] for p in places], axis=0)
+        v_tile = jnp.concatenate([kv_all[p, hdim : 2 * hdim] for p in places], axis=0)
         s_t = jnp.dot(k_tile, self.q_t, preferred_element_type=jnp.float32)
         e_t = jnp.exp2(s_t * (sizes.scale * LOG2E))
         if masked:
             e_t = jnp.where((key >= self.start) & (key <= self.position), e_t, 0.0)
-        return k_at, v_at, k_tile, v_tile, e_t
+        return places, k_tile, v_tile, e_t
 
     def put(self, ref, value_t):
         rows = value_t.T.astype(ref.dtype)
@@ -133,9 +130,9 @@
 
 
 def forward_kernel(sizes, table, *refs):
-    pieces, refs = refs[:-9], refs[-9:]
-    out_ref, stats_ref, q_all, g_all, k_all, v_all, out_t, totals, sems = refs
-    copies = loaded(sizes, pieces, q_all, g_all, k_all, v_all, sems)
+    pieces, refs = refs[:-8], refs[-8:]
+    out_ref, stats_ref, q_all, g_all, kv_all, out_t, totals, sems = refs
+    copies = loaded(sizes, pieces, q_all, g_all, kv_all, sems)
     for copy in copies:
         copy.wait()
 
@@ -145,7 +142,7 @@
         totals[...] = jnp.zeros_like(totals)
 
         def step(i, masked):
-            _, _, _, v_tile, e_t = block.tile(i, k_all, v_all, masked)
+            _, _, v_tile, e_t = block.tile(i, kv_all, masked)
             totals[...] += jnp.sum(e_t.reshape(sizes.tile // 8, 8, sizes.rows), axis=0)
             out_t[...] += transposed_product(v_tile, e_t.astype(jnp.bfloat16))
 
@@ -161,12 +158,11 @@
 
 
 def backward_kernel(sizes, table, *refs):
-    pieces, refs = refs[: -13 - GROUP], refs[-13 - GROUP :]
+    pieces, refs = refs[: -10 - GROUP], refs[-10 - GROUP :]
     stats_refs, refs = refs[:GROUP], refs[GROUP:]
-    dq_ref, dk_own, dk_other, dv_own, dv_other = refs[:5]
-    q_all, g_all, k_all, v_all, dk_acc, dv_acc, dq_t, sems = refs[5:]
-    half = sizes.half
-    copies = loaded(sizes, pieces, q_all, g_all, k_all, v_all, sems)
+    dq_ref, own_ref, other_ref, q_all, g_all, kv_all, dk_acc, dv_acc, dq_t, sems = refs
+    half, hdim = sizes.half, sizes.hdim
+    copies = loaded(sizes, pieces, q_all, g_all, kv_all, sems)
 
     def clear(i, carry):
         at = pl.ds(pl.multiple_of(i * 256, 256), 256)
@@ -188,7 +184,7 @@
         row_dot = stats[1:2, :] * inverse
 
         def step(i, masked):
-            k_at, v_at, k_tile, v_tile, e_t = block.tile(i, k_all, v_all, masked)
+            places, k_tile, v_tile, e_t = block.tile(i, kv_all, masked)
             dp_t = jnp.dot(v_tile, block.g_t, preferred_element_type=jnp.float32)
             p_t = e_t * inverse
             ds_t = (p_t * (dp_t - row_dot)).astype(jnp.bfloat16)
@@ -196,9 +192,9 @@
             dq_t[...] += transposed_product(k_tile, ds_t)
             dk = jnp.dot(ds_t, block.q_rows, preferred_element_type=jnp.float32)
             dv = jnp.dot(p_b, block.g_rows, preferred_element_type=jnp.float32)
-            for u in range(sizes.per_tile):
-                dk_acc[k_at[u], :] += dk[u * half : (u + 1) * half, :]
-                dv_acc[v_at[u], :] += dv[u * half : (u + 1) * half, :]
+            for u, p in enumerate(places):
+                dk_acc[p, :] += dk[u * half : (u + 1) * half, :]
+                dv_acc[p, :] += dv[u * half : (u + 1) * half, :]
 
         block.each(step)
         block.put(dq_ref, dq_t[...] * sizes.scale)
@@ -209,10 +205,9 @@
     def finish(i, carry):
         at = pl.ds(pl.multiple_of(i * 256, 256), 256)
         far = pl.ds(pl.multiple_of(sizes.keys // 2 + i * 256, 256), 256)
-        dk_own[at, :] = (dk_acc[at, :] * sizes.scale).astype(jnp.bfloat16)
-        dk_other[at, :] = (dk_acc[far, :] * sizes.scale).astype(jnp.bfloat16)
-        dv_own[at, :] = dv_acc[at, :].astype(jnp.bfloat16)
-        dv_other[at, :] = dv_acc[far, :].astype(jnp.bfloat16)
+        for ref, rows in ((own_ref, at), (other_ref, far)):
+            ref[at, 0:hdim] = (dk_acc[rows, :] * sizes.scale).astype(jnp.bfloat16)
+            ref[at, hdim : 2 * hdim] = dv_acc[rows, :].astype(jnp.bfloat16)
         return carry
 
     lax.fori_loop(0, sizes.keys // 512, finish, 0)
@@ -225,8 +220,7 @@
 
 def held_arrays(sizes):
     wide = pltpu.VMEM((GROUP * sizes.tokens, sizes.width), jnp.bfloat16)
-    narrow = pltpu.VMEM((sizes.keys, sizes.hdim), jnp.bfloat16)
-    return [wide, wide, narrow, narrow]
+    return [wide, wide, pltpu.VMEM((sizes.keys, 2 * sizes.hdim), jnp.bfloat16)]
 
 
 def cost(sizes, products):
@@ -257,12 +251,12 @@
 
 def backward(sizes, table, pieces, stats):
     wide = jax.ShapeDtypeStruct((GROUP * sizes.tokens, sizes.width), jnp.bfloat16)
-    term = jax.ShapeDtypeStruct((sizes.keys // 2, sizes.hdim), jnp.bfloat16)
+    term = jax.ShapeDtypeStruct((sizes.keys // 2, 2 * sizes.hdim), jnp.bfloat16)
     return pl.pallas_call(
         functools.partial(backward_kernel, sizes),
-        out_shape=(wide, term, term, term, term),
+        out_shape=(wide, term, term),
         in_specs=[SMEM_SPEC] + [HBM_SPEC] * len(pieces) + [VMEM_SPEC] * GROUP,
-        out_specs=(VMEM_SPEC,) * 5,
+        out_specs=(VMEM_SPEC,) * 3,
         scratch_shapes=held_arrays(sizes)
         + [
             pltpu.VMEM((sizes.keys, sizes.hdim), jnp.float32),
@@ -280,19 +274,16 @@
     devices = pair_order.shape[0]
     device = jnp.arange(devices, dtype=jnp.int32)
     far_core, far_y = lax.rem(device % 2 + core, 2), lax.rem(device // 8 % 2 + y, 2)
-    k_row = (far_core * 16 + far_y * 8 + device // 16) * sizes.tokens
-    v_row = (far_core * 16 + lax.rem(device // 16 - z + 8, 8) * 2 + far_y) * sizes.tokens
+    row = (far_core * 16 + device // 16 * 2 + far_y) * sizes.tokens
     mirrored = 2 * devices - 1 - pair_order
     block = jnp.concatenate([pair_order, mirrored])
-    k_row = jnp.concatenate([k_row, k_row + sizes.half])
-    v_row = jnp.concatenate([v_row, v_row + sizes.half])
+    row = jnp.concatenate([row, row + sizes.half])
     local = device // 2 % 4 == x
     local = jnp.concatenate([local, local])
     rank = jnp.sum((local[None, :] & (block[None, :] < block[:, None])).astype(jnp.int32), axis=1)
     place = jnp.arange(sizes.local, dtype=jnp.int32)
     chosen = local[None, :] & (rank[None, :] == place[:, None])
-    k_at = jnp.sum(jnp.where(chosen, k_row[None, :], 0), axis=1)
-    v_at = jnp.sum(jnp.where(chosen, v_row[None, :], 0), axis=1)
+    address = jnp.sum(jnp.where(chosen, row[None, :], 0), axis=1)
     held = jnp.sum(jnp.where(chosen, block[None, :], 0), axis=1)
     docs = jnp.arange(sizes.docs, dtype=jnp.int32)
     ends = jnp.sum(jnp.where(docs[None, :] <= docs[:, None], doc_lengths[None, :], 0), axis=1)
@@ -304,7 +295,7 @@
     start = jnp.max(jnp.where(ends[None, :] <= first[:, None], ends[None, :], 0), axis=1)
     low = jnp.sum((held[None, :] < (start // sizes.half)[:, None]).astype(jnp.int32), axis=1)
     high = jnp.sum((held[None, :] <= own[:, None]).astype(jnp.int32), axis=1)
-    return jnp.concatenate([k_at, v_at, held, ends, own, low, high]).astype(jnp.int32)
+    return jnp.concatenate([address, held, ends, own, low, high]).astype(jnp.int32)
 
 
 def from_x(a, step):
@@ -321,10 +312,6 @@
 
 def over_z(a):
     return lax.all_to_all(a, "z", 0, 0, tiled=True)
-
-
-def from_z(a, step):
-    return lax.ppermute(a, "z", [((i + step) % 8, i) for i in range(8)])
 
 
 def gathered_x(queries, grad_out):
@@ -336,43 +323,28 @@
 
 
 def gathered_keys(keys, values):
-    values = jnp.concatenate([values, swap(values, "y")], axis=0)
-    k_near = over_z(jnp.tile(keys, (8, 1)))
-    v = [values]
-    for step in range(1, 8):
-        v.append(from_z(values, step))
-    v = jnp.concatenate(v, axis=0)
-    k_far = swap(k_near, "y")
-    return [k_near, k_far, swap(k_near, "core"), swap(k_far, "core"), v, swap(v, "core")]
+    kv = jnp.concatenate([keys, values], axis=1)
+    pair = jnp.concatenate([kv, swap(kv, "y")], axis=0)
+    near = over_z(jnp.tile(pair, (8, 1)))
+    return [near, swap(near, "core")]
 
 
 def scattered_keys(own, other, tokens):
-    n = 8 * tokens
     other = swap(other, "core")
-    far = swap(added(own[n:], other[n:]), "y")
-    column = over_z(added(own[:n], other[:n], far))
-    column = column.reshape(8, tokens, -1).astype(jnp.float32)
-    return jnp.sum(column, axis=0).astype(jnp.bfloat16)
-
-
-def scattered_values(own, other, tokens):
-    other = swap(other, "core")
-    n = 2 * tokens
-    parts = [added(own[i * n : (i + 1) * n], other[i * n : (i + 1) * n]) for i in range(8)]
-    column = parts[0].astype(jnp.float32)
-    for step in range(1, 8):
-        arrived = from_z(parts[8 - step], step)
-        column = column + arrived.astype(jnp.float32)
-    far = swap(column[tokens:].astype(jnp.bfloat16), "y")
-    return added(column[:tokens], far)
-
-
-def summed_x(parts, tokens):
-    part = [parts[i * tokens : (i + 1) * tokens] for i in range(GROUP)]
-    received = [part[0]]
+    own, other = (a.reshape(8, 2, tokens, -1) for a in (own, other))
+    far = swap(added(own[:, 1], other[:, 1]), "y")
+    column = over_z(added(own[:, 0], other[:, 0], far))
+    return jnp.sum(column.astype(jnp.float32), axis=0).astype(jnp.bfloat16)
+
+
+def summed_x(first, second, tokens):
+    totals = [a[:tokens].astype(jnp.float32) for a in (first, second)]
     for step in (1, 2, 3):
-        received.append(from_x(part[(4 - step) % 4], step))
-    return received
+        at = slice((4 - step) * tokens, (5 - step) * tokens)
+        arrived = from_x(jnp.concatenate([first[at], second[at]], axis=0), step)
+        totals[0] = totals[0] + arrived[:tokens].astype(jnp.float32)
+        totals[1] = totals[1] + arrived[tokens:].astype(jnp.float32)
+    return totals
 
 
 def shared_stats(stats):
@@ -392,17 +364,15 @@
     pieces = [pltpu.with_memory_space_constraint(p, pltpu.HBM) for p in pieces]
     out_parts, stats = forward(sizes, table, pieces)
     stats = shared_stats(stats)
-    out_parts = summed_x(out_parts, tokens)
     dq_parts, *terms = backward(sizes, table, pieces, stats)
     total = sum(stats[i][(8 - 2 * i) % 8 : (8 - 2 * i) % 8 + 2, 0, :] for i in range(GROUP))
     total = total.reshape(2, sizes.heads, sizes.half)
     total = jnp.swapaxes(total, 1, 2).reshape(tokens, sizes.heads, 1)
-    out = sum(p.astype(jnp.float32) for p in out_parts).reshape(tokens, sizes.heads, hdim)
-    out = (out / total).astype(jnp.bfloat16).reshape(tokens, width)
-    query_grad = added(*summed_x(dq_parts, tokens))
-    key_grad = scattered_keys(*terms[:2], tokens)
-    value_grad = scattered_values(*terms[2:], tokens)
-    return out, query_grad, key_grad, value_grad
+    out, query_grad = summed_x(out_parts, dq_parts, tokens)
+    out = out.reshape(tokens, sizes.heads, hdim) / total
+    out = out.astype(jnp.bfloat16).reshape(tokens, width)
+    grads = scattered_keys(*terms, tokens)
+    return out, query_grad.astype(jnp.bfloat16), grads[:, :hdim], grads[:, hdim:]
 
 
 def solution(mesh):

time: 152 us -> 129 us (0.85)
  the two profiles are of different devices: /device:TPU:8 before, /device:TPU:1 now
where the time goes in v3:
time: 129 us; the launch traced here: 128 us
  waiting for transfers between devices  49 us (38%)
  starting transfers between devices  44.8 us (35%)
  Pallas kernels  20.3 us (16%)
  other arithmetic  7.3 us (6%)
  local copies, waits for them, and re-layouts  6.2 us (5%)
    all_to_all x2, waiting for transfers between devices, over_z(): return lax.all_to_all(a, 'z', 0, 0, tiled=True)  23.7 us
    all_to_all x2, starting transfers between devices, over_z(): return lax.all_to_all(a, 'z', 0, 0, tiled=True)  20.2 us
    ppermute x9, starting transfers between devices, from_x(): return lax.ppermute(a, 'x', [((i + step) % 4, i) for i in range(4)])  14 us
    ppermute x9, waiting for transfers between devices, from_x(): return lax.ppermute(a, 'x', [((i + step) % 4, i) for i in range(4)])  12.9 us
    ppermute x4, waiting for transfers between devices, swap(): return lax.ppermute(a, axis, [(0, 1), (1, 0)])  12.4 us
    pallas_call x1, Pallas kernels, backward(): pl.pallas_call(functools.partial(backward_kernel, sizes), out_shape=(wide...  11.2 us
    ppermute x4, starting transfers between devices, swap(): return lax.ppermute(a, axis, [(0, 1), (1, 0)])  10.6 us
    pallas_call x1, Pallas kernels, forward(): pl.pallas_call(functools.partial(forward_kernel, sizes), out_shape=(wide,...  9.05 us
  transfers between devices with their start and end apart: 15, of which 9 were waited for; matrix products, arithmetic and copies ran while one was open for 6% of the time, Pallas kernels for 0%

profile of v3, /device:TPU:1, one launch (start us, length us, event | category | flops | bytes accessed | tf_op | source)
XLA Modules:
  0.0 128.4 jit_solution(3767066578376298767)
XLA Ops:
  0.6 0.8 constant_dynamic-update-slice_fusion.3
  1.4 3.8 %collective-permute-start.3 = (bf16[128,256]{1,0:T(8,128)(2,1)S(1)}, bf16[128,256]{1,0:T(8,128)(2,1)S(1)}, u32[]{:S(2)}, u32[]{:S(2)}) collective-permute-start(bf16[128,256]{1,0:T(8,128)(2,1)S(1)} %constant_dynamic-update-slice_fusion.2), channel_id=1, source_target_pairs={{0,16},{16,0},{1,17},{17,1},{2,18},{18,2},{3,19},{19,3},{4,20},{20... | collective-permute-start | bytes 196616 | tf_op jit(solution)/shard_map/ppermute | solution.py:306
  5.3 1.7 %collective-permute-done.3 = bf16[128,256]{1,0:T(8,128)(2,1)S(1)} collective-permute-done((bf16[128,256]{1,0:T(8,128)(2,1)S(1)}, bf16[128,256]{1,0:T(8,128)(2,1)S(1)}, u32[]{:S(2)}, u32[]{:S(2)}) %collective-permute-start.3) | collective-permute-done | bytes 65568 | tf_op jit(solution)/shard_map/ppermute | solution.py:306
  6.9 1.0 tile.2
  8.0 8.4 %all-to-all-start = ((bf16[8,256,256]{2,1,0:T(8,128)(2,1)}), bf16[8,256,256]{2,1,0:T(8,128)(2,1)S(1)}, u32[]{:S(2)}, u32[]{:S(2)}) async-start(bf16[8,256,256]{2,1,0:T(8,128)(2,1)} %tile.2), calls=%async_computation | async-start | bytes 2097152 | tf_op jit(solution)/shard_map/all_to_all | solution.py:314
  16.4 0.9 copy-done.2
  17.3 1.3 %collective-permute-start.2 = (bf16[256,1024]{1,0:T(8,128)(2,1)S(1)}, bf16[256,1024]{1,0:T(8,128)(2,1)S(1)}, u32[]{:S(2)}, u32[]{:S(2)}) collective-permute-start(bf16[256,1024]{1,0:T(8,128)(2,1)S(1)} %constant_dynamic-update-slice_fusion.refs_0_), channel_id=1, source_target_pairs={{12,0},{0,4},{4,8},{8,12},{13,1},{1,5},{5,9},{9,13},{14,2},{2,6},{... | collective-permute-start | bytes 1572872 | tf_op jit(solution)/shard_map/ppermute | solution.py:302
  18.6 2.5 %collective-permute-start.1 = (bf16[256,1024]{1,0:T(8,128)(2,1)S(1)}, bf16[256,1024]{1,0:T(8,128)(2,1)S(1)}, u32[]{:S(2)}, u32[]{:S(2)}) collective-permute-start(bf16[256,1024]{1,0:T(8,128)(2,1)S(1)} %constant_dynamic-update-slice_fusion.refs_0_), channel_id=1, source_target_pairs={{8,0},{12,4},{0,8},{4,12},{9,1},{13,5},{1,9},{5,13},{10,2},{14,6},... | collective-permute-start | bytes 1572872 | tf_op jit(solution)/shard_map/ppermute | solution.py:302
  21.1 1.2 collective-permute-start
  23.7 21.9 %all-to-all-done = bf16[8,256,256]{2,1,0:T(8,128)(2,1)S(1)} async-done(((bf16[8,256,256]{2,1,0:T(8,128)(2,1)}), bf16[8,256,256]{2,1,0:T(8,128)(2,1)S(1)}, u32[]{:S(2)}, u32[]{:S(2)}) %all-to-all-start) | async-done | bytes 1048608 | tf_op jit(solution)/shard_map/all_to_all | solution.py:314
  48.4 9.1 %forward.1 = (bf16[512,1024]{1,0:T(8,128)(2,1)S(1)}, f32[8,2,512]{2,1,0:T(2,128)S(1)}) custom-call(s32[168]{0:T(256)S(1)} %concatenate.33.table, bf16[256,1024]{1,0:T(8,128)(2,1)} %copy-done.3, bf16[256,1024]{1,0:T(8,128)(2,1)} %collective-permute-done.refs_1_, bf16[256,1024]{1,0:T(8,128)(2,1)} %copy-done.7, bf16[256,1024]{1,0:T(8,128)(2,1)} %copy-done.6, ...), custom_call_target="tpu_custom_call" | custom-call | flops 2147483648 | bytes 6291456 | tf_op jit(solution)/shard_map/forward/pallas_call | solution.py:235
  57.5 2.5 %collective-permute-start.7 = (f32[8,2,512]{2,1,0:T(2,128)S(1)}, f32[8,2,512]{2,1,0:T(2,128)S(1)}, u32[]{:S(2)}, u32[]{:S(2)}) collective-permute-start(f32[8,2,512]{2,1,0:T(2,128)S(1)} %get-tuple-element.10.refs_6_), channel_id=1, source_target_pairs={{12,0},{0,4},{4,8},{8,12},{13,1},{1,5},{5,9},{9,13},{14,2},{2,6},{... | collective-permute-start | bytes 98312 | tf_op jit(solution)/shard_map/ppermute | solution.py:302
  60.0 1.6 %collective-permute-start.6 = (f32[8,2,512]{2,1,0:T(2,128)S(1)}, f32[8,2,512]{2,1,0:T(2,128)S(1)}, u32[]{:S(2)}, u32[]{:S(2)}) collective-permute-start(f32[8,2,512]{2,1,0:T(2,128)S(1)} %get-tuple-element.10.refs_6_), channel_id=1, source_target_pairs={{8,0},{12,4},{0,8},{4,12},{9,1},{13,5},{1,9},{5,13},{10,2},{14,6},... | collective-permute-start | bytes 98312 | tf_op jit(solution)/shard_map/ppermute | solution.py:302
  61.6 1.7 %collective-permute-start.5 = (f32[8,2,512]{2,1,0:T(2,128)S(1)}, f32[8,2,512]{2,1,0:T(2,128)S(1)}, u32[]{:S(2)}, u32[]{:S(2)}) collective-permute-start(f32[8,2,512]{2,1,0:T(2,128)S(1)} %get-tuple-element.10.refs_6_), channel_id=1, source_target_pairs={{4,0},{8,4},{12,8},{0,12},{5,1},{9,5},{13,9},{1,13},{6,2},{10,6},{... | collective-permute-start | bytes 98312 | tf_op jit(solution)/shard_map/ppermute | solution.py:302
  63.4 1.3 %collective-permute-done.6.refs_8_ = f32[8,2,512]{2,1,0:T(2,128)S(1)} collective-permute-done((f32[8,2,512]{2,1,0:T(2,128)S(1)}, f32[8,2,512]{2,1,0:T(2,128)S(1)}, u32[]{:S(2)}, u32[]{:S(2)}) %collective-permute-start.6) | collective-permute-done | bytes 32800 | tf_op jit(solution)/shard_map/ppermute | solution.py:302
  64.7 11.2 %backward.1 = (bf16[512,1024]{1,0:T(8,128)(2,1)S(1)}, bf16[2048,256]{1,0:T(8,128)(2,1)S(1)}, bf16[2048,256]{1,0:T(8,128)(2,1)S(1)}) custom-call(s32[168]{0:T(256)S(1)} %concatenate.33.table, bf16[256,1024]{1,0:T(8,128)(2,1)} %copy-done.3, bf16[256,1024]{1,0:T(8,128)(2,1)} %collective-permute-done.refs_1_, bf16[256,1024]{1,0:T(8,128)(2,1)} %copy-done.7, ...), custom_call_target="tpu_custom_call" | custom-call | flops 6442450944 | bytes 6291456 | tf_op jit(solution)/shard_map/backward/pallas_call | solution.py:255
  75.9 1.8 %collective-permute-start.11 = (bf16[2048,256]{1,0:T(8,128)(2,1)S(1)}, bf16[2048,256]{1,0:T(8,128)(2,1)S(1)}, u32[]{:S(2)}, u32[]{:S(2)}) collective-permute-start(bf16[2048,256]{1,0:T(8,128)(2,1)S(1)} %get-tuple-element.13), channel_id=1, source_target_pairs={{0,2},{2,0},{1,3},{3,1},{4,6},{6,4},{5,7},{7,5},{8,10},{10,8},{9,1... | collective-permute-start | bytes 3145736 | tf_op jit(solution)/shard_map/ppermute | solution.py:306
  77.8 2.3 %collective-permute-done.11 = bf16[2048,256]{1,0:T(8,128)(2,1)S(1)} collective-permute-done((bf16[2048,256]{1,0:T(8,128)(2,1)S(1)}, bf16[2048,256]{1,0:T(8,128)(2,1)S(1)}, u32[]{:S(2)}, u32[]{:S(2)}) %collective-permute-start.11) | collective-permute-done | bytes 1048608 | tf_op jit(solution)/shard_map/ppermute | solution.py:306
  80.2 4.5 %collective-permute-start.12 = (bf16[8,128,256]{2,1,0:T(8,128)(2,1)S(1)}, bf16[8,128,256]{2,1,0:T(8,128)(2,1)S(1)}, u32[]{:S(2)}, u32[]{:S(2)}) collective-permute-start(bf16[8,128,256]{2,1,0:T(8,128)(2,1)S(1)} %fusion.1), channel_id=1, source_target_pairs={{0,16},{16,0},{1,17},{17,1},{2,18},{18,2},{3,19},{19,3},{4,20},{20... | collective-permute-start | bytes 1572872 | tf_op jit(solution)/shard_map/ppermute | solution.py:306
  84.8 0.8 pad_maximum_fusion.1
  85.6 1.1 collective-permute-start.9
  86.7 0.8 pad_maximum_fusion.2
  87.5 1.4 %collective-permute-start.10 = (bf16[256,1024]{1,0:T(8,128)(2,1)}, bf16[256,1024]{1,0:T(8,128)(2,1)}, u32[]{:S(2)}, u32[]{:S(2)}) collective-permute-start(bf16[256,1024]{1,0:T(8,128)(2,1)} %pad_maximum_fusion.2), channel_id=1, source_target_pairs={{12,0},{0,4},{4,8},{8,12},{13,1},{1,5},{5,9},{9,13},{14,2},{2,6},{... | collective-permute-start | bytes 1572872 | tf_op jit(solution)/shard_map/ppermute | solution.py:302
  88.9 8.0 %collective-permute-done.12 = bf16[8,128,256]{2,1,0:T(8,128)(2,1)S(1)} collective-permute-done((bf16[8,128,256]{2,1,0:T(8,128)(2,1)S(1)}, bf16[8,128,256]{2,1,0:T(8,128)(2,1)S(1)}, u32[]{:S(2)}, u32[]{:S(2)}) %collective-permute-start.12) | collective-permute-done | bytes 524320 | tf_op jit(solution)/shard_map/ppermute | solution.py:306
  96.9 1.0 fusion
  97.9 11.9 %all-to-all-start.1 = ((bf16[8,128,256]{2,1,0:T(8,128)(2,1)}), bf16[8,128,256]{2,1,0:T(8,128)(2,1)S(1)}, u32[]{:S(2)}, u32[]{:S(2)}) async-start(bf16[8,128,256]{2,1,0:T(8,128)(2,1)} %fusion), calls=%async_computation.1 | async-start | bytes 1048576 | tf_op jit(solution)/shard_map/all_to_all | solution.py:314
  109.8 0.8 pad_maximum_fusion
  110.6 0.8 collective-permute-start.8
  111.6 0.8 collective-permute-done.10
  112.5 10.7 %collective-permute-done.8 = bf16[256,1024]{1,0:T(8,128)(2,1)S(1)} collective-permute-done((bf16[256,1024]{1,0:T(8,128)(2,1)}, bf16[256,1024]{1,0:T(8,128)(2,1)S(1)}, u32[]{:S(2)}, u32[]{:S(2)}) %collective-permute-start.8) | collective-permute-done | bytes 524320 | tf_op jit(solution)/shard_map/ppermute | solution.py:302
  123.4 2.5 %add_convert_fusion.1 = (bf16[128,1024]{1,0:T(8,128)(2,1)}, bf16[128,1024]{1,0:T(8,128)(2,1)}) fusion(bf16[256,1024]{1,0:T(8,128)(2,1)} %collective-permute-done.10, bf16[256,1024]{1,0:T(8,128)(2,1)} %collective-permute-done.9, bf16[256,1024]{1,0:T(8,128)(2,1)S(1)} %collective-permute-done.8, bf16[512,1024]{1,0:T(8,128)(2,1)S(1)} %get-tuple-element.11, ...), kind=kLoop, calls=%fused_computation.11 | loop fusion | flops 2228224 | bytes 3145728 | tf_op jit(solution)/shard_map/convert_element_type | solution.py:375
  125.9 1.8 %all-to-all-done.1 = bf16[8,128,256]{2,1,0:T(8,128)(2,1)S(1)} async-done(((bf16[8,128,256]{2,1,0:T(8,128)(2,1)}), bf16[8,128,256]{2,1,0:T(8,128)(2,1)S(1)}, u32[]{:S(2)}, u32[]{:S(2)}) %all-to-all-start.1) | async-done | bytes 524320 | tf_op jit(solution)/shard_map/all_to_all | solution.py:314
  (54 shorter events, 5.7 us)
Async XLA Ops:
  0.6 0.8 copy-start.4
  1.4 5.5 %collective-permute-start.3 = (bf16[128,256]{1,0:T(8,128)(2,1)S(1)}, bf16[128,256]{1,0:T(8,128)(2,1)S(1)}, u32[]{:S(2)}, u32[]{:S(2)}) collective-permute-start(bf16[128,256]{1,0:T(8,128)(2,1)S(1)} %constant_dynamic-update-slice_fusion.2), channel_id=1, source_target_pairs={{0,16},{16,0},{1,17},{17,1},{2,18},{18,2},{3,19},{19,3},{4,20},{20... | collective-permute-start | bytes 196616 | tf_op jit(solution)/shard_map/ppermute | solution.py:306
  8.0 8.4 %copy-start.1 = (bf16[128,1024]{1,0:T(8,128)(2,1)S(1)}, bf16[128,1024]{1,0:T(8,128)(2,1)}, u32[]{:S(2)}) copy-start(bf16[128,1024]{1,0:T(8,128)(2,1)} %param.6) | copy-start | bytes 786436
  8.0 37.6 %all-to-all-start = ((bf16[8,256,256]{2,1,0:T(8,128)(2,1)}), bf16[8,256,256]{2,1,0:T(8,128)(2,1)S(1)}, u32[]{:S(2)}, u32[]{:S(2)}) async-start(bf16[8,256,256]{2,1,0:T(8,128)(2,1)} %tile.2), calls=%async_computation | async-start | bytes 2097152 | tf_op jit(solution)/shard_map/all_to_all | solution.py:314
  16.3 1.0 copy-start.2
  17.3 31.1 %copy-start.3 = (bf16[256,1024]{1,0:T(8,128)(2,1)}, bf16[256,1024]{1,0:T(8,128)(2,1)S(1)}, u32[]{:S(2)}) copy-start(bf16[256,1024]{1,0:T(8,128)(2,1)S(1)} %constant_dynamic-update-slice_fusion.refs_0_) | copy-start | bytes 1572868
  17.3 29.7 %collective-permute-start.2 = (bf16[256,1024]{1,0:T(8,128)(2,1)S(1)}, bf16[256,1024]{1,0:T(8,128)(2,1)S(1)}, u32[]{:S(2)}, u32[]{:S(2)}) collective-permute-start(bf16[256,1024]{1,0:T(8,128)(2,1)S(1)} %constant_dynamic-update-slice_fusion.refs_0_), channel_id=1, source_target_pairs={{12,0},{0,4},{4,8},{8,12},{13,1},{1,5},{5,9},{9,13},{14,2},{2,6},{... | collective-permute-start | bytes 1572872 | tf_op jit(solution)/shard_map/ppermute | solution.py:302
  18.6 28.4 %collective-permute-start.1 = (bf16[256,1024]{1,0:T(8,128)(2,1)S(1)}, bf16[256,1024]{1,0:T(8,128)(2,1)S(1)}, u32[]{:S(2)}, u32[]{:S(2)}) collective-permute-start(bf16[256,1024]{1,0:T(8,128)(2,1)S(1)} %constant_dynamic-update-slice_fusion.refs_0_), channel_id=1, source_target_pairs={{8,0},{12,4},{0,8},{4,12},{9,1},{13,5},{1,9},{5,13},{10,2},{14,6},... | collective-permute-start | bytes 1572872 | tf_op jit(solution)/shard_map/ppermute | solution.py:302
  21.1 26.0 %collective-permute-start = (bf16[256,1024]{1,0:T(8,128)(2,1)S(1)}, bf16[256,1024]{1,0:T(8,128)(2,1)}, u32[]{:S(2)}, u32[]{:S(2)}) collective-permute-start(bf16[256,1024]{1,0:T(8,128)(2,1)S(1)} %constant_dynamic-update-slice_fusion.refs_0_), channel_id=1, source_target_pairs={{4,0},{8,4},{12,8},{0,12},{5,1},{9,5},{13,9},{1,13},{6,2},{10,6},{... | collective-permute-start | bytes 1572872 | tf_op jit(solution)/shard_map/ppermute | solution.py:302
  22.2 0.7 copy-start.5
  22.9 0.7 copy-start.8
  45.5 2.9 %copy-start = (bf16[8,256,256]{2,1,0:T(8,128)(2,1)}, bf16[8,256,256]{2,1,0:T(8,128)(2,1)S(1)}, u32[]{:S(2)}) copy-start(bf16[8,256,256]{2,1,0:T(8,128)(2,1)S(1)} %all-to-all-done) | copy-start | bytes 3145732
  45.5 2.9 %collective-permute-start.4 = (bf16[2048,256]{1,0:T(8,128)(2,1)S(1)}, bf16[2048,256]{1,0:T(8,128)(2,1)}, u32[]{:S(2)}, u32[]{:S(2)}) collective-permute-start(bf16[2048,256]{1,0:T(8,128)(2,1)S(1)} %bitcast.29), channel_id=1, source_target_pairs={{0,2},{2,0},{1,3},{3,1},{4,6},{6,4},{5,7},{7,5},{8,10},{10,8},{9,1... | collective-permute-start | bytes 3145736 | tf_op jit(solution)/shard_map/ppermute | solution.py:306
  47.0 0.8 copy-start.6
  47.0 1.0 copy-start.7
  57.5 5.9 %collective-permute-start.7 = (f32[8,2,512]{2,1,0:T(2,128)S(1)}, f32[8,2,512]{2,1,0:T(2,128)S(1)}, u32[]{:S(2)}, u32[]{:S(2)}) collective-permute-start(f32[8,2,512]{2,1,0:T(2,128)S(1)} %get-tuple-element.10.refs_6_), channel_id=1, source_target_pairs={{12,0},{0,4},{4,8},{8,12},{13,1},{1,5},{5,9},{9,13},{14,2},{2,6},{... | collective-permute-start | bytes 98312 | tf_op jit(solution)/shard_map/ppermute | solution.py:302
  60.0 4.7 %collective-permute-start.6 = (f32[8,2,512]{2,1,0:T(2,128)S(1)}, f32[8,2,512]{2,1,0:T(2,128)S(1)}, u32[]{:S(2)}, u32[]{:S(2)}) collective-permute-start(f32[8,2,512]{2,1,0:T(2,128)S(1)} %get-tuple-element.10.refs_6_), channel_id=1, source_target_pairs={{8,0},{12,4},{0,8},{4,12},{9,1},{13,5},{1,9},{5,13},{10,2},{14,6},... | collective-permute-start | bytes 98312 | tf_op jit(solution)/shard_map/ppermute | solution.py:302
  61.6 3.1 %collective-permute-start.5 = (f32[8,2,512]{2,1,0:T(2,128)S(1)}, f32[8,2,512]{2,1,0:T(2,128)S(1)}, u32[]{:S(2)}, u32[]{:S(2)}) collective-permute-start(f32[8,2,512]{2,1,0:T(2,128)S(1)} %get-tuple-element.10.refs_6_), channel_id=1, source_target_pairs={{4,0},{8,4},{12,8},{0,12},{5,1},{9,5},{13,9},{1,13},{6,2},{10,6},{... | collective-permute-start | bytes 98312 | tf_op jit(solution)/shard_map/ppermute | solution.py:302
  75.9 4.1 %collective-permute-start.11 = (bf16[2048,256]{1,0:T(8,128)(2,1)S(1)}, bf16[2048,256]{1,0:T(8,128)(2,1)S(1)}, u32[]{:S(2)}, u32[]{:S(2)}) collective-permute-start(bf16[2048,256]{1,0:T(8,128)(2,1)S(1)} %get-tuple-element.13), channel_id=1, source_target_pairs={{0,2},{2,0},{1,3},{3,1},{4,6},{6,4},{5,7},{7,5},{8,10},{10,8},{9,1... | collective-permute-start | bytes 3145736 | tf_op jit(solution)/shard_map/ppermute | solution.py:306
  80.2 16.7 %collective-permute-start.12 = (bf16[8,128,256]{2,1,0:T(8,128)(2,1)S(1)}, bf16[8,128,256]{2,1,0:T(8,128)(2,1)S(1)}, u32[]{:S(2)}, u32[]{:S(2)}) collective-permute-start(bf16[8,128,256]{2,1,0:T(8,128)(2,1)S(1)} %fusion.1), channel_id=1, source_target_pairs={{0,16},{16,0},{1,17},{17,1},{2,18},{18,2},{3,19},{19,3},{4,20},{20... | collective-permute-start | bytes 1572872 | tf_op jit(solution)/shard_map/ppermute | solution.py:306
  85.6 26.0 %collective-permute-start.9 = (bf16[256,1024]{1,0:T(8,128)(2,1)}, bf16[256,1024]{1,0:T(8,128)(2,1)}, u32[]{:S(2)}, u32[]{:S(2)}) collective-permute-start(bf16[256,1024]{1,0:T(8,128)(2,1)} %pad_maximum_fusion.1), channel_id=1, source_target_pairs={{8,0},{12,4},{0,8},{4,12},{9,1},{13,5},{1,9},{5,13},{10,2},{14,6},... | collective-permute-start | bytes 1572872 | tf_op jit(solution)/shard_map/ppermute | solution.py:302
  87.5 25.0 %collective-permute-start.10 = (bf16[256,1024]{1,0:T(8,128)(2,1)}, bf16[256,1024]{1,0:T(8,128)(2,1)}, u32[]{:S(2)}, u32[]{:S(2)}) collective-permute-start(bf16[256,1024]{1,0:T(8,128)(2,1)} %pad_maximum_fusion.2), channel_id=1, source_target_pairs={{12,0},{0,4},{4,8},{8,12},{13,1},{1,5},{5,9},{9,13},{14,2},{2,6},{... | collective-permute-start | bytes 1572872 | tf_op jit(solution)/shard_map/ppermute | solution.py:302
  97.9 29.7 %all-to-all-start.1 = ((bf16[8,128,256]{2,1,0:T(8,128)(2,1)}), bf16[8,128,256]{2,1,0:T(8,128)(2,1)S(1)}, u32[]{:S(2)}, u32[]{:S(2)}) async-start(bf16[8,128,256]{2,1,0:T(8,128)(2,1)} %fusion), calls=%async_computation.1 | async-start | bytes 1048576 | tf_op jit(solution)/shard_map/all_to_all | solution.py:314
  110.6 12.6 %collective-permute-start.8 = (bf16[256,1024]{1,0:T(8,128)(2,1)}, bf16[256,1024]{1,0:T(8,128)(2,1)S(1)}, u32[]{:S(2)}, u32[]{:S(2)}) collective-permute-start(bf16[256,1024]{1,0:T(8,128)(2,1)} %pad_maximum_fusion), channel_id=1, source_target_pairs={{4,0},{8,4},{12,8},{0,12},{5,1},{9,5},{13,9},{1,13},{6,2},{10,6},{... | collective-permute-start | bytes 1572872 | tf_op jit(solution)/shard_map/ppermute | solution.py:302

commit v4 on v3

--- a/solution.py
+++ b/solution.py
@@ -28,7 +28,7 @@
         self.local = 2 * devices // GROUP
         self.keys = self.local * self.half
         self.queries = 2 * GROUP
-        self.per_tile = 4
+        self.per_tile = 6
         self.tile = self.per_tile * self.half
         self.scale = hdim ** (-0.5)
         self.at_key = 0
@@ -274,7 +274,7 @@
     devices = pair_order.shape[0]
     device = jnp.arange(devices, dtype=jnp.int32)
     far_core, far_y = lax.rem(device % 2 + core, 2), lax.rem(device // 8 % 2 + y, 2)
-    row = (far_core * 16 + device // 16 * 2 + far_y) * sizes.tokens
+    row = (far_core * 16 + far_y * 8 + device // 16) * sizes.tokens
     mirrored = 2 * devices - 1 - pair_order
     block = jnp.concatenate([pair_order, mirrored])
     row = jnp.concatenate([row, row + sizes.half])
@@ -324,17 +324,20 @@
 
 def gathered_keys(keys, values):
     kv = jnp.concatenate([keys, values], axis=1)
-    pair = jnp.concatenate([kv, swap(kv, "y")], axis=0)
-    near = over_z(jnp.tile(pair, (8, 1)))
-    return [near, swap(near, "core")]
+    near = over_z(jnp.tile(kv, (8, 1)))
+    far = swap(near, "y")
+    near_other = swap(near, "core")
+    far_other = swap(far, "core")
+    return [near, far, near_other, far_other]
 
 
 def scattered_keys(own, other, tokens):
+    n = 8 * tokens
     other = swap(other, "core")
-    own, other = (a.reshape(8, 2, tokens, -1) for a in (own, other))
-    far = swap(added(own[:, 1], other[:, 1]), "y")
-    column = over_z(added(own[:, 0], other[:, 0], far))
-    return jnp.sum(column.astype(jnp.float32), axis=0).astype(jnp.bfloat16)
+    far = swap(added(own[n:], other[n:]), "y")
+    column = over_z(added(own[:n], other[:n], far))
+    column = column.reshape(8, tokens, -1).astype(jnp.float32)
+    return jnp.sum(column, axis=0).astype(jnp.bfloat16)
 
 
 def summed_x(first, second, tokens):

time: 129 us -> 123 us (0.953)
  the two profiles are of different devices: /device:TPU:1 before, /device:TPU:8 now
where the time goes in v4:
time: 123 us; the launch traced here: 121 us
  waiting for transfers between devices  46.1 us (37%)
  starting transfers between devices  39.4 us (32%)
  Pallas kernels  21.7 us (18%)
  other arithmetic  8.1 us (7%)
  local copies, waits for them, and re-layouts  5.11 us (4%)
    ppermute x5, waiting for transfers between devices, swap(): return lax.ppermute(a, axis, [(0, 1), (1, 0)])  22.8 us
    ppermute x9, starting transfers between devices, from_x(): return lax.ppermute(a, 'x', [((i + step) % 4, i) for i in range(4)])  17 us
    ppermute x9, waiting for transfers between devices, from_x(): return lax.ppermute(a, 'x', [((i + step) % 4, i) for i in range(4)])  14 us
    pallas_call x1, Pallas kernels, backward(): pl.pallas_call(functools.partial(backward_kernel, sizes), out_shape=(wide...  12.3 us
    all_to_all x2, starting transfers between devices, over_z(): return lax.all_to_all(a, 'z', 0, 0, tiled=True)  12.1 us
    ppermute x5, starting transfers between devices, swap(): return lax.ppermute(a, axis, [(0, 1), (1, 0)])  10.3 us
    pallas_call x1, Pallas kernels, forward(): pl.pallas_call(functools.partial(forward_kernel, sizes), out_shape=(wide,...  9.48 us
    all_to_all x2, waiting for transfers between devices, over_z(): return lax.all_to_all(a, 'z', 0, 0, tiled=True)  9.32 us
  transfers between devices with their start and end apart: 16, of which 10 were waited for; matrix products, arithmetic and copies ran while one was open for 6% of the time, Pallas kernels for 0%

profile of v4, /device:TPU:8, one launch (start us, length us, event | category | flops | bytes accessed | tf_op | source)
XLA Modules:
  0.0 121.3 jit_solution(8098011704825091454)
XLA Ops:
  0.6 0.8 pad_maximum_fusion.3
  1.4 0.8 tile.2
  2.3 8.6 %all-to-all-start = ((bf16[8,128,256]{2,1,0:T(8,128)(2,1)}), bf16[8,128,256]{2,1,0:T(8,128)(2,1)S(1)}, u32[]{:S(2)}, u32[]{:S(2)}) async-start(bf16[8,128,256]{2,1,0:T(8,128)(2,1)} %tile.2), calls=%async_computation | async-start | bytes 1048576 | tf_op jit(solution)/shard_map/all_to_all | solution.py:314
  10.9 0.9 copy-done.2
  11.8 1.6 %collective-permute-start.2 = (bf16[256,1024]{1,0:T(8,128)(2,1)S(1)}, bf16[256,1024]{1,0:T(8,128)(2,1)S(1)}, u32[]{:S(2)}, u32[]{:S(2)}) collective-permute-start(bf16[256,1024]{1,0:T(8,128)(2,1)S(1)} %constant_dynamic-update-slice_fusion.refs_0_), channel_id=1, source_target_pairs={{12,0},{0,4},{4,8},{8,12},{13,1},{1,5},{5,9},{9,13},{14,2},{2,6},{... | collective-permute-start | bytes 1572872 | tf_op jit(solution)/shard_map/ppermute | solution.py:302
  13.4 2.7 %collective-permute-start.1 = (bf16[256,1024]{1,0:T(8,128)(2,1)S(1)}, bf16[256,1024]{1,0:T(8,128)(2,1)S(1)}, u32[]{:S(2)}, u32[]{:S(2)}) collective-permute-start(bf16[256,1024]{1,0:T(8,128)(2,1)S(1)} %constant_dynamic-update-slice_fusion.refs_0_), channel_id=1, source_target_pairs={{8,0},{12,4},{0,8},{4,12},{9,1},{13,5},{1,9},{5,13},{10,2},{14,6},... | collective-permute-start | bytes 1572872 | tf_op jit(solution)/shard_map/ppermute | solution.py:302
  16.1 1.4 %collective-permute-start = (bf16[256,1024]{1,0:T(8,128)(2,1)S(1)}, bf16[256,1024]{1,0:T(8,128)(2,1)S(1)}, u32[]{:S(2)}, u32[]{:S(2)}) collective-permute-start(bf16[256,1024]{1,0:T(8,128)(2,1)S(1)} %constant_dynamic-update-slice_fusion.refs_0_), channel_id=1, source_target_pairs={{4,0},{8,4},{12,8},{0,12},{5,1},{9,5},{13,9},{1,13},{6,2},{10,6},{... | collective-permute-start | bytes 1572872 | tf_op jit(solution)/shard_map/ppermute | solution.py:302
  19.0 9.3 %all-to-all-done = bf16[8,128,256]{2,1,0:T(8,128)(2,1)S(1)} async-done(((bf16[8,128,256]{2,1,0:T(8,128)(2,1)}), bf16[8,128,256]{2,1,0:T(8,128)(2,1)S(1)}, u32[]{:S(2)}, u32[]{:S(2)}) %all-to-all-start) | async-done | bytes 524320 | tf_op jit(solution)/shard_map/all_to_all | solution.py:314
  28.3 2.3 %collective-permute-start.3 = (bf16[1024,256]{1,0:T(8,128)(2,1)S(1)}, bf16[1024,256]{1,0:T(8,128)(2,1)}, u32[]{:S(2)}, u32[]{:S(2)}) collective-permute-start(bf16[1024,256]{1,0:T(8,128)(2,1)S(1)} %bitcast.12), channel_id=1, source_target_pairs={{0,16},{16,0},{1,17},{17,1},{2,18},{18,2},{3,19},{19,3},{4,20},{20... | collective-permute-start | bytes 1572872 | tf_op jit(solution)/shard_map/ppermute | solution.py:306
  31.1 12.7 %collective-permute-done.3.refs_5_ = bf16[1024,256]{1,0:T(8,128)(2,1)} collective-permute-done((bf16[1024,256]{1,0:T(8,128)(2,1)S(1)}, bf16[1024,256]{1,0:T(8,128)(2,1)}, u32[]{:S(2)}, u32[]{:S(2)}) %collective-permute-start.3) | collective-permute-done | bytes 524320 | tf_op jit(solution)/shard_map/ppermute | solution.py:306
  44.5 0.8 copy-done.7
  45.3 0.7 collective-permute-done.5.refs_7_
  46.1 9.5 %forward.1 = (bf16[512,1024]{1,0:T(8,128)(2,1)S(1)}, f32[8,2,512]{2,1,0:T(2,128)S(1)}) custom-call(s32[168]{0:T(256)S(1)} %concatenate.30.table, bf16[256,1024]{1,0:T(8,128)(2,1)} %copy-done.3, bf16[256,1024]{1,0:T(8,128)(2,1)} %copy-done.7, bf16[256,1024]{1,0:T(8,128)(2,1)} %copy-done.6, bf16[256,1024]{1,0:T(8,128)(2,1)} %copy-done.5, ...), custom_call_target="tpu_custom_call" | custom-call | flops 2147483648 | bytes 6291456 | tf_op jit(solution)/shard_map/forward/pallas_call | solution.py:235
  56.0 3.2 %collective-permute-start.7 = (f32[8,2,512]{2,1,0:T(2,128)S(1)}, f32[8,2,512]{2,1,0:T(2,128)S(1)}, u32[]{:S(2)}, u32[]{:S(2)}) collective-permute-start(f32[8,2,512]{2,1,0:T(2,128)S(1)} %get-tuple-element.10.refs_8_), channel_id=1, source_target_pairs={{8,0},{12,4},{0,8},{4,12},{9,1},{13,5},{1,9},{5,13},{10,2},{14,6},... | collective-permute-start | bytes 98312 | tf_op jit(solution)/shard_map/ppermute | solution.py:302
  59.2 1.0 collective-permute-start.6
  60.1 0.8 collective-permute-done.8.refs_11_
  61.4 1.7 %collective-permute-done.6.refs_9_ = f32[8,2,512]{2,1,0:T(2,128)S(1)} collective-permute-done((f32[8,2,512]{2,1,0:T(2,128)S(1)}, f32[8,2,512]{2,1,0:T(2,128)S(1)}, u32[]{:S(2)}, u32[]{:S(2)}) %collective-permute-start.6) | collective-permute-done | bytes 32800 | tf_op jit(solution)/shard_map/ppermute | solution.py:302
  63.1 12.3 %backward.1 = (bf16[512,1024]{1,0:T(8,128)(2,1)S(1)}, bf16[2048,256]{1,0:T(8,128)(2,1)S(1)}, bf16[2048,256]{1,0:T(8,128)(2,1)S(1)}) custom-call(s32[168]{0:T(256)S(1)} %concatenate.30.table, bf16[256,1024]{1,0:T(8,128)(2,1)} %copy-done.3, bf16[256,1024]{1,0:T(8,128)(2,1)} %copy-done.7, bf16[256,1024]{1,0:T(8,128)(2,1)} %copy-done.6, ...), custom_call_target="tpu_custom_call" | custom-call | flops 6442450944 | bytes 6291456 | tf_op jit(solution)/shard_map/backward/pallas_call | solution.py:255
  75.5 2.6 %collective-permute-done.12 = bf16[2048,256]{1,0:T(8,128)(2,1)S(1)} collective-permute-done((bf16[2048,256]{1,0:T(8,128)(2,1)S(1)}, bf16[2048,256]{1,0:T(8,128)(2,1)S(1)}, u32[]{:S(2)}, u32[]{:S(2)}) %collective-permute-start.12) | collective-permute-done | bytes 1048608 | tf_op jit(solution)/shard_map/ppermute | solution.py:306
  78.3 7.8 %collective-permute-start.13 = (bf16[1024,256]{1,0:T(8,128)(2,1)S(1)}, bf16[1024,256]{1,0:T(8,128)(2,1)S(1)}, u32[]{:S(2)}, u32[]{:S(2)}) collective-permute-start(bf16[1024,256]{1,0:T(8,128)(2,1)S(1)} %add_convert_fusion.1), channel_id=1, source_target_pairs={{0,16},{16,0},{1,17},{17,1},{2,18},{18,2},{3,19},{19,3},{4,20},{20... | collective-permute-start | bytes 1572872 | tf_op jit(solution)/shard_map/ppermute | solution.py:306
  86.2 0.8 pad_maximum_fusion.1
  87.0 1.2 collective-permute-start.10
  88.2 0.8 pad_maximum_fusion.2
  89.1 2.6 %collective-permute-start.11 = (bf16[256,1024]{1,0:T(8,128)(2,1)}, bf16[256,1024]{1,0:T(8,128)(2,1)}, u32[]{:S(2)}, u32[]{:S(2)}) collective-permute-start(bf16[256,1024]{1,0:T(8,128)(2,1)} %pad_maximum_fusion.2), channel_id=1, source_target_pairs={{12,0},{0,4},{4,8},{8,12},{13,1},{1,5},{5,9},{9,13},{14,2},{2,6},{... | collective-permute-start | bytes 1572872 | tf_op jit(solution)/shard_map/ppermute | solution.py:302
  91.6 6.7 %collective-permute-done.13 = bf16[1024,256]{1,0:T(8,128)(2,1)S(1)} collective-permute-done((bf16[1024,256]{1,0:T(8,128)(2,1)S(1)}, bf16[1024,256]{1,0:T(8,128)(2,1)S(1)}, u32[]{:S(2)}, u32[]{:S(2)}) %collective-permute-start.13) | collective-permute-done | bytes 524320 | tf_op jit(solution)/shard_map/ppermute | solution.py:306
  98.3 1.0 add_convert_fusion
  99.4 3.5 %all-to-all-start.1 = ((bf16[8,128,256]{2,1,0:T(8,128)(2,1)}), bf16[8,128,256]{2,1,0:T(8,128)(2,1)S(1)}, u32[]{:S(2)}, u32[]{:S(2)}) async-start(bf16[8,128,256]{2,1,0:T(8,128)(2,1)} %bitcast.3), calls=%async_computation.1 | async-start | bytes 1048576 | tf_op jit(solution)/shard_map/all_to_all | solution.py:314
  102.9 0.8 pad_maximum_fusion
  103.7 2.9 %collective-permute-start.9 = (bf16[256,1024]{1,0:T(8,128)(2,1)}, bf16[256,1024]{1,0:T(8,128)(2,1)S(1)}, u32[]{:S(2)}, u32[]{:S(2)}) collective-permute-start(bf16[256,1024]{1,0:T(8,128)(2,1)} %pad_maximum_fusion), channel_id=1, source_target_pairs={{4,0},{8,4},{12,8},{0,12},{5,1},{9,5},{13,9},{1,13},{6,2},{10,6},{... | collective-permute-start | bytes 1572872 | tf_op jit(solution)/shard_map/ppermute | solution.py:302
  106.8 7.0 %collective-permute-done.11 = bf16[256,1024]{1,0:T(8,128)(2,1)} collective-permute-done((bf16[256,1024]{1,0:T(8,128)(2,1)}, bf16[256,1024]{1,0:T(8,128)(2,1)}, u32[]{:S(2)}, u32[]{:S(2)}) %collective-permute-start.11) | collective-permute-done | bytes 524320 | tf_op jit(solution)/shard_map/ppermute | solution.py:302
  113.8 4.1 %collective-permute-done.9 = bf16[256,1024]{1,0:T(8,128)(2,1)S(1)} collective-permute-done((bf16[256,1024]{1,0:T(8,128)(2,1)}, bf16[256,1024]{1,0:T(8,128)(2,1)S(1)}, u32[]{:S(2)}, u32[]{:S(2)}) %collective-permute-start.9) | collective-permute-done | bytes 524320 | tf_op jit(solution)/shard_map/ppermute | solution.py:302
  118.1 2.5 %add_convert_fusion.2 = (bf16[128,1024]{1,0:T(8,128)(2,1)}, bf16[128,1024]{1,0:T(8,128)(2,1)}) fusion(bf16[256,1024]{1,0:T(8,128)(2,1)} %collective-permute-done.11, bf16[256,1024]{1,0:T(8,128)(2,1)} %collective-permute-done.10, bf16[256,1024]{1,0:T(8,128)(2,1)S(1)} %collective-permute-done.9, bf16[512,1024]{1,0:T(8,128)(2,1)S(1)} %get-tuple-element.11, ...), kind=kLoop, calls=%fused_computation.7 | loop fusion | flops 2228224 | bytes 3145728 | tf_op jit(solution)/shard_map/convert_element_type | solution.py:378
  (54 shorter events, 4.9 us)
Async XLA Ops:
  2.2 8.6 %copy-start.1 = (bf16[128,1024]{1,0:T(8,128)(2,1)S(1)}, bf16[128,1024]{1,0:T(8,128)(2,1)}, u32[]{:S(2)}) copy-start(bf16[128,1024]{1,0:T(8,128)(2,1)} %param.6) | copy-start | bytes 786436
  2.3 26.1 %all-to-all-start = ((bf16[8,128,256]{2,1,0:T(8,128)(2,1)}), bf16[8,128,256]{2,1,0:T(8,128)(2,1)S(1)}, u32[]{:S(2)}, u32[]{:S(2)}) async-start(bf16[8,128,256]{2,1,0:T(8,128)(2,1)} %tile.2), calls=%async_computation | async-start | bytes 1048576 | tf_op jit(solution)/shard_map/all_to_all | solution.py:314
  10.9 1.0 copy-start.2
  11.8 34.2 %copy-start.3 = (bf16[256,1024]{1,0:T(8,128)(2,1)}, bf16[256,1024]{1,0:T(8,128)(2,1)S(1)}, u32[]{:S(2)}) copy-start(bf16[256,1024]{1,0:T(8,128)(2,1)S(1)} %constant_dynamic-update-slice_fusion.refs_0_) | copy-start | bytes 1572868
  11.8 32.6 %collective-permute-start.2 = (bf16[256,1024]{1,0:T(8,128)(2,1)S(1)}, bf16[256,1024]{1,0:T(8,128)(2,1)S(1)}, u32[]{:S(2)}, u32[]{:S(2)}) collective-permute-start(bf16[256,1024]{1,0:T(8,128)(2,1)S(1)} %constant_dynamic-update-slice_fusion.refs_0_), channel_id=1, source_target_pairs={{12,0},{0,4},{4,8},{8,12},{13,1},{1,5},{5,9},{9,13},{14,2},{2,6},{... | collective-permute-start | bytes 1572872 | tf_op jit(solution)/shard_map/ppermute | solution.py:302
  13.4 31.0 %collective-permute-start.1 = (bf16[256,1024]{1,0:T(8,128)(2,1)S(1)}, bf16[256,1024]{1,0:T(8,128)(2,1)S(1)}, u32[]{:S(2)}, u32[]{:S(2)}) collective-permute-start(bf16[256,1024]{1,0:T(8,128)(2,1)S(1)} %constant_dynamic-update-slice_fusion.refs_0_), channel_id=1, source_target_pairs={{8,0},{12,4},{0,8},{4,12},{9,1},{13,5},{1,9},{5,13},{10,2},{14,6},... | collective-permute-start | bytes 1572872 | tf_op jit(solution)/shard_map/ppermute | solution.py:302
  16.1 28.3 %collective-permute-start = (bf16[256,1024]{1,0:T(8,128)(2,1)S(1)}, bf16[256,1024]{1,0:T(8,128)(2,1)S(1)}, u32[]{:S(2)}, u32[]{:S(2)}) collective-permute-start(bf16[256,1024]{1,0:T(8,128)(2,1)S(1)} %constant_dynamic-update-slice_fusion.refs_0_), channel_id=1, source_target_pairs={{4,0},{8,4},{12,8},{0,12},{5,1},{9,5},{13,9},{1,13},{6,2},{10,6},{... | collective-permute-start | bytes 1572872 | tf_op jit(solution)/shard_map/ppermute | solution.py:302
  17.6 0.7 copy-start.4
  18.3 0.7 copy-start.8
  28.3 17.7 %copy-start = (bf16[8,128,256]{2,1,0:T(8,128)(2,1)}, bf16[8,128,256]{2,1,0:T(8,128)(2,1)S(1)}, u32[]{:S(2)}) copy-start(bf16[8,128,256]{2,1,0:T(8,128)(2,1)S(1)} %all-to-all-done) | copy-start | bytes 1572868
  28.3 15.5 %collective-permute-start.3 = (bf16[1024,256]{1,0:T(8,128)(2,1)S(1)}, bf16[1024,256]{1,0:T(8,128)(2,1)}, u32[]{:S(2)}, u32[]{:S(2)}) collective-permute-start(bf16[1024,256]{1,0:T(8,128)(2,1)S(1)} %bitcast.12), channel_id=1, source_target_pairs={{0,16},{16,0},{1,17},{17,1},{2,18},{18,2},{3,19},{19,3},{4,20},{20... | collective-permute-start | bytes 1572872 | tf_op jit(solution)/shard_map/ppermute | solution.py:306
  31.0 13.4 %collective-permute-start.4 = (bf16[1024,256]{1,0:T(8,128)(2,1)S(1)}, bf16[1024,256]{1,0:T(8,128)(2,1)}, u32[]{:S(2)}, u32[]{:S(2)}) collective-permute-start(bf16[1024,256]{1,0:T(8,128)(2,1)S(1)} %bitcast.13), channel_id=1, source_target_pairs={{0,2},{2,0},{1,3},{3,1},{4,6},{6,4},{5,7},{7,5},{8,10},{10,8},{9,1... | collective-permute-start | bytes 1572872 | tf_op jit(solution)/shard_map/ppermute | solution.py:306
  43.8 2.3 %collective-permute-start.5 = (bf16[1024,256]{1,0:T(8,128)(2,1)}, bf16[1024,256]{1,0:T(8,128)(2,1)}, u32[]{:S(2)}, u32[]{:S(2)}) collective-permute-start(bf16[1024,256]{1,0:T(8,128)(2,1)} %collective-permute-done.3.refs_5_), channel_id=1, source_target_pairs={{0,2},{2,0},{1,3},{3,1},{4,6},{6,4},{5,7},{7,5},{8,10},{10,8},{9,1... | collective-permute-start | bytes 1572872 | tf_op jit(solution)/shard_map/ppermute | solution.py:306
  44.4 1.6 %copy-start.5 = (bf16[256,1024]{1,0:T(8,128)(2,1)}, bf16[256,1024]{1,0:T(8,128)(2,1)S(1)}, u32[]{:S(2)}) copy-start(bf16[256,1024]{1,0:T(8,128)(2,1)S(1)} %collective-permute-done.2.refs_3_) | copy-start | bytes 1572868
  44.4 1.6 %copy-start.6 = (bf16[256,1024]{1,0:T(8,128)(2,1)}, bf16[256,1024]{1,0:T(8,128)(2,1)S(1)}, u32[]{:S(2)}) copy-start(bf16[256,1024]{1,0:T(8,128)(2,1)S(1)} %collective-permute-done.1.refs_2_) | copy-start | bytes 1572868
  44.4 0.9 copy-start.7
  55.6 5.4 %collective-permute-start.8 = (f32[8,2,512]{2,1,0:T(2,128)S(1)}, f32[8,2,512]{2,1,0:T(2,128)S(1)}, u32[]{:S(2)}, u32[]{:S(2)}) collective-permute-start(f32[8,2,512]{2,1,0:T(2,128)S(1)} %get-tuple-element.10.refs_8_), channel_id=1, source_target_pairs={{12,0},{0,4},{4,8},{8,12},{13,1},{1,5},{5,9},{9,13},{14,2},{2,6},{... | collective-permute-start | bytes 98312 | tf_op jit(solution)/shard_map/ppermute | solution.py:302
  56.0 5.4 %collective-permute-start.7 = (f32[8,2,512]{2,1,0:T(2,128)S(1)}, f32[8,2,512]{2,1,0:T(2,128)S(1)}, u32[]{:S(2)}, u32[]{:S(2)}) collective-permute-start(f32[8,2,512]{2,1,0:T(2,128)S(1)} %get-tuple-element.10.refs_8_), channel_id=1, source_target_pairs={{8,0},{12,4},{0,8},{4,12},{9,1},{13,5},{1,9},{5,13},{10,2},{14,6},... | collective-permute-start | bytes 98312 | tf_op jit(solution)/shard_map/ppermute | solution.py:302
  59.2 3.9 %collective-permute-start.6 = (f32[8,2,512]{2,1,0:T(2,128)S(1)}, f32[8,2,512]{2,1,0:T(2,128)S(1)}, u32[]{:S(2)}, u32[]{:S(2)}) collective-permute-start(f32[8,2,512]{2,1,0:T(2,128)S(1)} %get-tuple-element.10.refs_8_), channel_id=1, source_target_pairs={{4,0},{8,4},{12,8},{0,12},{5,1},{9,5},{13,9},{1,13},{6,2},{10,6},{... | collective-permute-start | bytes 98312 | tf_op jit(solution)/shard_map/ppermute | solution.py:302
  75.4 2.7 %collective-permute-start.12 = (bf16[2048,256]{1,0:T(8,128)(2,1)S(1)}, bf16[2048,256]{1,0:T(8,128)(2,1)S(1)}, u32[]{:S(2)}, u32[]{:S(2)}) collective-permute-start(bf16[2048,256]{1,0:T(8,128)(2,1)S(1)} %get-tuple-element.13), channel_id=1, source_target_pairs={{0,2},{2,0},{1,3},{3,1},{4,6},{6,4},{5,7},{7,5},{8,10},{10,8},{9,1... | collective-permute-start | bytes 3145736 | tf_op jit(solution)/shard_map/ppermute | solution.py:306
  78.3 20.1 %collective-permute-start.13 = (bf16[1024,256]{1,0:T(8,128)(2,1)S(1)}, bf16[1024,256]{1,0:T(8,128)(2,1)S(1)}, u32[]{:S(2)}, u32[]{:S(2)}) collective-permute-start(bf16[1024,256]{1,0:T(8,128)(2,1)S(1)} %add_convert_fusion.1), channel_id=1, source_target_pairs={{0,16},{16,0},{1,17},{17,1},{2,18},{18,2},{3,19},{19,3},{4,20},{20... | collective-permute-start | bytes 1572872 | tf_op jit(solution)/shard_map/ppermute | solution.py:306
  87.0 19.8 %collective-permute-start.10 = (bf16[256,1024]{1,0:T(8,128)(2,1)}, bf16[256,1024]{1,0:T(8,128)(2,1)}, u32[]{:S(2)}, u32[]{:S(2)}) collective-permute-start(bf16[256,1024]{1,0:T(8,128)(2,1)} %pad_maximum_fusion.1), channel_id=1, source_target_pairs={{8,0},{12,4},{0,8},{4,12},{9,1},{13,5},{1,9},{5,13},{10,2},{14,6},... | collective-permute-start | bytes 1572872 | tf_op jit(solution)/shard_map/ppermute | solution.py:302
  89.1 24.7 %collective-permute-start.11 = (bf16[256,1024]{1,0:T(8,128)(2,1)}, bf16[256,1024]{1,0:T(8,128)(2,1)}, u32[]{:S(2)}, u32[]{:S(2)}) collective-permute-start(bf16[256,1024]{1,0:T(8,128)(2,1)} %pad_maximum_fusion.2), channel_id=1, source_target_pairs={{12,0},{0,4},{4,8},{8,12},{13,1},{1,5},{5,9},{9,13},{14,2},{2,6},{... | collective-permute-start | bytes 1572872 | tf_op jit(solution)/shard_map/ppermute | solution.py:302
  99.4 21.2 %all-to-all-start.1 = ((bf16[8,128,256]{2,1,0:T(8,128)(2,1)}), bf16[8,128,256]{2,1,0:T(8,128)(2,1)S(1)}, u32[]{:S(2)}, u32[]{:S(2)}) async-start(bf16[8,128,256]{2,1,0:T(8,128)(2,1)} %bitcast.3), calls=%async_computation.1 | async-start | bytes 1048576 | tf_op jit(solution)/shard_map/all_to_all | solution.py:314
  103.7 14.2 %collective-permute-start.9 = (bf16[256,1024]{1,0:T(8,128)(2,1)}, bf16[256,1024]{1,0:T(8,128)(2,1)S(1)}, u32[]{:S(2)}, u32[]{:S(2)}) collective-permute-start(bf16[256,1024]{1,0:T(8,128)(2,1)} %pad_maximum_fusion), channel_id=1, source_target_pairs={{4,0},{8,4},{12,8},{0,12},{5,1},{9,5},{13,9},{1,13},{6,2},{10,6},{... | collective-permute-start | bytes 1572872 | tf_op jit(solution)/shard_map/ppermute | solution.py:302
